TPU v7x, 128 devices: a whole 4x4x4 slice. The times are simulated.
128 devices in a mesh: tp: 4 (over x), fsdp: 32 (over z, y, core).
Axes of the slice: x: 4, y: 4, z: 4, core: 2. Of those that a mesh axis runs over, the one named last changes fastest.
Arguments:
- x_in: bfloat16 [384, 256, 768], P('fsdp')
- dy_out: bfloat16 [384, 256, 768], P('fsdp')
- ln_gain: float32 [768], P('fsdp')
- w_q: bfloat16 [768, 768], P('fsdp', 'tp')
- w_k: bfloat16 [768, 64], P('fsdp')
- w_v: bfloat16 [768, 64], P('fsdp')
- w_o: bfloat16 [768, 768], P('tp', 'fsdp')
- w_gate: bfloat16 [768, 3072], P('fsdp', 'tp')
- w_up: bfloat16 [768, 3072], P('fsdp', 'tp')
- w_down: bfloat16 [3072, 768], P('tp', 'fsdp')
Outputs:
- output 1: bfloat16 [384, 256, 768], P('fsdp')
- output 2: bfloat16 [384, 256, 768], P('fsdp')
- output 3: float32 [768], P('fsdp')
- output 4: float32 [768, 768], P('fsdp', 'tp')
- output 5: float32 [768, 64], P('fsdp')
- output 6: float32 [768, 64], P('fsdp')
- output 7: float32 [768, 768], P('tp', 'fsdp')
- output 8: float32 [768, 3072], P('fsdp', 'tp')
- output 9: float32 [768, 3072], P('fsdp', 'tp')
- output 10: float32 [3072, 768], P('tp', 'fsdp')
All inputs are finite; a program needn't handle non-finite values.
Results may differ from a plain program's by a relative error of at most 0.0154874.
Values are sent between devices in bfloat16 or wider.
A program may use at most 1 GiB of HBM per device.

v0:
```python
import math
import jax
import jax.numpy as jnp
from jax import lax
from jax.sharding import PartitionSpec as P


def layer_norm(x_f32, gain):
    x_mean = jnp.mean(x_f32, axis=-1, keepdims=True)
    x_cent = x_f32 - x_mean
    x_var = jnp.mean(x_cent * x_cent, axis=-1, keepdims=True)
    return (x_cent * lax.rsqrt(x_var + 1e-5) * gain).astype(jnp.bfloat16)


def rotate(vals, cos_t, sin_t):
    half_dim = vals.shape[-1] // 2
    first = vals[..., :half_dim]
    second = vals[..., half_dim:]
    return jnp.concatenate([first * cos_t - second * sin_t, second * cos_t + first * sin_t], axis=-1)


def qk_post(q_raw, k_raw):
    seq_len = k_raw.shape[1]
    head_dim = k_raw.shape[2]
    half_dim = head_dim // 2
    inv_freq = jnp.power(10000.0, -2.0 * jnp.arange(half_dim, dtype=jnp.float32) / head_dim)
    angle = jnp.arange(seq_len, dtype=jnp.float32)[:, None] * inv_freq[None, :]
    cos_t = jnp.cos(angle)
    sin_t = jnp.sin(angle)
    q_rot = rotate(q_raw.astype(jnp.float32), cos_t[:, None, :], sin_t[:, None, :]) * (1.0 / math.sqrt(head_dim))
    k_rot = rotate(k_raw.astype(jnp.float32), cos_t, sin_t)
    return q_rot.astype(jnp.bfloat16), k_rot.astype(jnp.bfloat16)


def attend(q_rot, k_rot, v_val):
    seq_len = q_rot.shape[1]
    causal = lax.broadcasted_iota(jnp.int32, (seq_len, 1, seq_len), 0) >= lax.broadcasted_iota(jnp.int32, (seq_len, 1, seq_len), 2)
    scores = jnp.einsum('crie,cle->cril', q_rot, k_rot, preferred_element_type=jnp.float32)
    scores = jnp.where(causal, scores, -1e30)
    row_max = lax.stop_gradient(jnp.max(scores, axis=-1, keepdims=True))
    exp_val = jnp.exp(scores - row_max)
    att_prob = (exp_val / jnp.sum(exp_val, axis=-1, keepdims=True)).astype(jnp.bfloat16)
    return jnp.einsum('cril,cle->crie', att_prob, v_val, preferred_element_type=jnp.float32).astype(jnp.bfloat16)


def swiglu(gate_val, up_val):
    return (jax.nn.silu(gate_val.astype(jnp.float32)) * up_val.astype(jnp.float32)).astype(jnp.bfloat16)


def matmul_f32(form, left, right):
    return jnp.einsum(form, left, right, preferred_element_type=jnp.float32)


def gather_rows(w_part):
    return lax.all_gather(w_part, 'fsdp', axis=0, tiled=True)


def gather_cols(w_part):
    return lax.all_gather(w_part, 'fsdp', axis=1, tiled=True)


def scatter_rows(grad_full):
    return lax.psum_scatter(grad_full, 'fsdp', scatter_dimension=0, tiled=True)


def scatter_cols(grad_full):
    return lax.psum_scatter(grad_full, 'fsdp', scatter_dimension=1, tiled=True)


def solution(mesh):
    def device_step(x_in, dy_out, ln_gain, w_q, w_k, w_v, w_o, w_gate, w_up, w_down):
        n_batch, seq_len, _ = x_in.shape
        head_dim = w_k.shape[1]
        gain_full = lax.all_gather(ln_gain, 'fsdp', tiled=True)
        x_f32 = x_in.astype(jnp.float32)
        h_norm, norm_pull = jax.vjp(layer_norm, x_f32, gain_full)
        wq_full = gather_rows(w_q)
        wk_full = gather_rows(w_k)
        wv_full = gather_rows(w_v)
        wg_full = gather_rows(w_gate)
        wu_full = gather_rows(w_up)
        q_raw = matmul_f32('bsd,de->bse', h_norm, wq_full).astype(jnp.bfloat16)
        k_raw = matmul_f32('bsd,de->bse', h_norm, wk_full).astype(jnp.bfloat16)
        v_val = matmul_f32('bsd,de->bse', h_norm, wv_full).astype(jnp.bfloat16)
        gate_val = matmul_f32('bsd,df->bsf', h_norm, wg_full).astype(jnp.bfloat16)
        up_val = matmul_f32('bsd,df->bsf', h_norm, wu_full).astype(jnp.bfloat16)
        q_heads = q_raw.reshape(n_batch, seq_len, -1, head_dim)
        (q_rot, k_rot), rope_pull = jax.vjp(qk_post, q_heads, k_raw)
        att_out, att_pull = jax.vjp(attend, q_rot, k_rot, v_val)
        mlp_act, act_pull = jax.vjp(swiglu, gate_val, up_val)
        att_flat = att_out.reshape(n_batch, seq_len, -1)
        wo_full = gather_cols(w_o)
        wd_full = gather_cols(w_down)
        branch_part = (matmul_f32('bse,ed->bsd', att_flat, wo_full) + matmul_f32('bsf,fd->bsd', mlp_act, wd_full)).astype(jnp.bfloat16)
        branch_sum = lax.psum(branch_part, 'tp')
        y_out = (x_f32 + branch_sum.astype(jnp.float32)).astype(jnp.bfloat16)

        wo_back = gather_cols(w_o)
        wd_back = gather_cols(w_down)
        grad_wo = scatter_cols(matmul_f32('bse,bsd->ed', att_flat, dy_out))
        grad_wdown = scatter_cols(matmul_f32('bsf,bsd->fd', mlp_act, dy_out))
        d_att = matmul_f32('bsd,ed->bse', dy_out, wo_back).astype(jnp.bfloat16).reshape(n_batch, seq_len, -1, head_dim)
        d_act = matmul_f32('bsd,fd->bsf', dy_out, wd_back).astype(jnp.bfloat16)
        d_gate, d_up = act_pull(d_act)
        d_qrot, dk_part, dv_part = att_pull(d_att)
        kv_sum = lax.psum(jnp.concatenate([dk_part, dv_part], axis=-1).astype(jnp.float32), 'tp')
        d_krot = kv_sum[..., :head_dim].astype(jnp.bfloat16)
        d_val = kv_sum[..., head_dim:].astype(jnp.bfloat16)
        d_qraw, d_kraw = rope_pull((d_qrot, d_krot))
        d_qflat = d_qraw.reshape(n_batch, seq_len, -1)
        grad_wq = scatter_rows(matmul_f32('bsd,bse->de', h_norm, d_qflat))
        grad_wk = scatter_rows(matmul_f32('bsd,bse->de', h_norm, d_kraw))
        grad_wv = scatter_rows(matmul_f32('bsd,bse->de', h_norm, d_val))
        grad_wgate = scatter_rows(matmul_f32('bsd,bsf->df', h_norm, d_gate))
        grad_wup = scatter_rows(matmul_f32('bsd,bsf->df', h_norm, d_up))
        wq_back = gather_rows(w_q)
        wk_back = gather_rows(w_k)
        wv_back = gather_rows(w_v)
        wg_back = gather_rows(w_gate)
        wu_back = gather_rows(w_up)
        dh_part = (matmul_f32('bse,de->bsd', d_qflat, wq_back) + matmul_f32('bsf,df->bsd', d_gate, wg_back) + matmul_f32('bsf,df->bsd', d_up, wu_back)).astype(jnp.bfloat16)
        dh_sum = lax.psum(dh_part, 'tp')
        dh_full = (dh_sum.astype(jnp.float32) + matmul_f32('bse,de->bsd', d_kraw, wk_back) + matmul_f32('bse,de->bsd', d_val, wv_back)).astype(jnp.bfloat16)
        dx_norm, gain_part = norm_pull(dh_full)
        grad_x = (dy_out.astype(jnp.float32) + dx_norm).astype(jnp.bfloat16)
        grad_gain = lax.psum_scatter(gain_part, 'fsdp', scatter_dimension=0, tiled=True)
        return (y_out, grad_x, grad_gain, grad_wq, grad_wk, grad_wv, grad_wo, grad_wgate, grad_wup, grad_wdown)

    act_spec = P('fsdp', None, None)
    row_spec = P('fsdp', 'tp')
    kv_spec = P('fsdp', None)
    col_spec = P('tp', 'fsdp')
    in_specs = (act_spec, act_spec, P('fsdp'), row_spec, kv_spec, kv_spec, col_spec, row_spec, row_spec, col_spec)
    out_specs = (act_spec, act_spec, P('fsdp'), row_spec, kv_spec, kv_spec, col_spec, row_spec, row_spec, col_spec)
    return jax.shard_map(device_step, mesh=mesh, in_specs=in_specs, out_specs=out_specs, check_vma=False)
```

profile of v0, /device:TPU:0, one launch (start us, length us, event | category | flops | bytes accessed | tf_op | source)
XLA Modules:
  0.0 1051.8 jit_solution(14216712254668672030)
XLA Ops:
  12.4 68.8 %all-reduce.4 = f32[768]{0:T(1024)S(1)} all-reduce(f32[768]{0:T(1024)S(1)} %dynamic-update-slice), channel_id=1, replica_groups=mesh['tp'=4,'fsdp'=32] {'fsdp'}, use_global_device_ids=true, to_apply=%add.4 | all-reduce | flops 768 | bytes 6144
  86.9 21.6 %all_gather.33 = bf16[768,64]{1,0:T(8,128)(2,1)S(1)} all-gather(bf16[24,64]{1,0:T(8,128)(2,1)S(1)} %copy-done.37), channel_id=1, replica_groups=mesh['tp'=4,'fsdp'=32] {'fsdp'}, dimensions={0}, use_global_device_ids=true | all-gather | bytes 101376 | tf_op jit(solution)/shard_map/all_gather | solution.py:55
  108.5 24.7 %all_gather.34 = bf16[768,64]{1,0:T(8,128)(2,1)S(1)} all-gather(bf16[24,64]{1,0:T(8,128)(2,1)S(1)} %copy-done.38), channel_id=1, replica_groups=mesh['tp'=4,'fsdp'=32] {'fsdp'}, dimensions={0}, use_global_device_ids=true | all-gather | bytes 101376 | tf_op jit(solution)/shard_map/all_gather | solution.py:55
  133.2 22.1 %all_gather.32 = bf16[768,192]{1,0:T(8,128)(2,1)S(1)} all-gather(bf16[24,192]{1,0:T(8,128)(2,1)S(1)} %copy-done.35), channel_id=1, replica_groups=mesh['tp'=4,'fsdp'=32] {'fsdp'}, dimensions={0}, use_global_device_ids=true | all-gather | bytes 304128 | tf_op jit(solution)/shard_map/all_gather | solution.py:55
  155.3 24.7 %all_gather.35 = bf16[192,768]{0,1:T(8,128)(2,1)S(1)} all-gather(bf16[192,24]{0,1:T(8,128)(2,1)S(1)} %copy-done.36), channel_id=1, replica_groups=mesh['tp'=4,'fsdp'=32] {'fsdp'}, dimensions={1}, use_global_device_ids=true | all-gather | bytes 304128 | tf_op jit(solution)/shard_map/all_gather | solution.py:59
  190.8 8.4 fusion.92
  204.2 6.8 fusion.13
  211.1 8.2 convert_multiply_fusion.8
  221.0 9.2 convolution_convert_fusion
  230.1 7.9 convolution_convert_fusion.1
  238.0 12.8 %fusion.24 = (bf16[12,256,768]{2,1,0:T(8,128)(2,1)}, bf16[12,256,768]{2,1,0:T(8,128)(2,1)S(1)}) fusion(bf16[12,256,768]{2,1,0:T(8,128)(2,1)} %convolution_convert_fusion.1, bf16[12,256,768]{2,1,0:T(8,128)(2,1)} %convolution_convert_fusion, bf16[768,768]{1,0:T(8,128)(2,1)} %all-gather.4.cloned.1.call-done, bf16[12,256,768]{2,1,0:T(8,128)(2,1)} %param.10, ...), kind=kOutput, calls=%fused_computation.39 | convolution fusion | flops 3671064576 | bytes 24800256 | tf_op jit(solution)/shard_map/bsd,df->bsf/dot_general | solution.py:51
  250.8 5.8 fusion.37
  260.4 8.7 fusion.39
  269.1 5.9 fusion.42
  284.2 6.2 fusion.32
  290.5 61.8 %all-reduce.13 = bf16[12,256,128]{1,2,0:T(8,128)(2,1)S(1)} all-reduce(f32[12,256,128]{1,2,0:T(8,128)S(1)} %maximum_convert_fusion), channel_id=1, replica_groups=mesh['tp'=4,'fsdp'=32] {'tp'}, use_global_device_ids=true, to_apply=%region_7.8 | all-reduce | flops 393216 | bytes 2359296 | tf_op jit(solution)/shard_map/psum | solution.py:106
  352.3 5.5 convolution_bitcast_fusion.7
  364.6 5.7 convolution_bitcast_fusion.4
  375.7 9.4 convolution_bitcast_fusion.2
  385.2 12.0 %convolution_bitcast_fusion.1 = f32[768,768]{1,0:T(8,128)} fusion(bf16[12,256,768]{2,1,0:T(8,128)(2,1)} %convolution_convert_fusion, bf16[12,256,768]{2,1,0:T(8,128)(2,1)} %copy-done.44, bf16[12,256,768]{2,1,0:T(8,128)(2,1)} %param.10, f32[768]{0:T(1024)S(1)} %copy-done.30, f32[12,256]{1,0:T(8,128)S(1)} %copy-done.25, f32[12,256]{1,0:T(8,128)S(1)} %broadcast_multiply_fusion), kind=kOutput, calls=%fused_computation.60 | convolution fusion | flops 3654549504 | bytes 16542720 | tf_op jit(solution)/shard_map/bsd,bsf->df/dot_general | solution.py:51
  403.3 11.1 %convolution_bitcast_fusion = f32[768,768]{0,1:T(8,128)} fusion(bf16[12,256,768]{2,1,0:T(8,128)(2,1)} %param.11, bf16[12,256,768]{2,1,0:T(8,128)(2,1)} %convolution_convert_fusion.1, bf16[12,256,768]{2,1,0:T(8,128)(2,1)} %copy-done.44), kind=kOutput, calls=%fused_computation.59 | convolution fusion | flops 3642753024 | bytes 16515072 | tf_op jit(solution)/shard_map/bsf,bsd->fd/dot_general | solution.py:51
  414.4 65.2 %all-reduce.12.cloned.1.call-done = (bf16[12,256,768]{2,1,0:T(8,128)(2,1)}, bf16[12,256,768]{2,1,0:T(8,128)(2,1)}) async-done(((bf16[12,256,768]{2,1,0:T(8,128)(2,1)}, bf16[12,256,768]{2,1,0:T(8,128)(2,1)}), (bf16[12,256,768]{2,1,0:T(8,128)(2,1)}, bf16[12,256,768]{2,1,0:T(8,128)(2,1)})) %all-reduce.12.cloned.1.call-update) | async-done | bytes 9437200 | tf_op jit(solution)/shard_map/psum | solution.py:95
  479.6 8.1 fusion.17
  487.7 8.0 fusion.15
  495.7 67.0 %all-reduce.5 = f32[768]{0:T(1024)S(1)} all-reduce(f32[768]{0:T(1024)S(1)} %get-tuple-element.10), channel_id=2, replica_groups=mesh['tp'=4,'fsdp'=32] {'fsdp'}, use_global_device_ids=true, to_apply=%region_11.12.clone | all-reduce | flops 768 | bytes 6144
  563.3 12.6 %add_convert_fusion = (bf16[12,256,768]{2,1,0:T(8,128)(2,1)}, bf16[12,256,768]{2,1,0:T(8,128)(2,1)}) fusion(bf16[12,256,768]{2,1,0:T(8,128)(2,1)} %param.11, bf16[12,256,768]{2,1,0:T(8,128)(2,1)} %param.10, bf16[12,256,768]{2,1,0:T(8,128)(2,1)} %copy-done.1, f32[12,256]{1,0:T(8,128)S(1)} %negate_multiply_fusion, f32[12,256]{1,0:T(8,128)S(1)} %multiply_multiply_fusion, ...), kind=kLoop, calls=%fused_computation.40 | loop fusion | flops 35389440 | bytes 28363776 | tf_op jit(solution)/shard_map/convert_element_type | solution.py:125
  575.9 57.7 %reduce-scatter.22.cloned.1.call-done = f32[24,64]{1,0:T(8,128)} async-done(((f32[768,64]{1,0:T(8,128)}), f32[24,64]{1,0:T(8,128)}) %reduce-scatter.22.cloned.1.call-update) | async-done | bytes 6160
  633.6 81.3 %reduce-scatter.12.cloned.1.call-done = f32[24,192]{1,0:T(8,128)} async-done(((f32[768,192]{1,0:T(8,128)}), f32[24,192]{1,0:T(8,128)}) %reduce-scatter.12.cloned.1.call-update) | async-done | bytes 18448 | tf_op jit(solution)/shard_map/reduce_scatter | solution.py:63
  714.9 81.3 %reduce-scatter.14.cloned.1.call-done = f32[192,24]{0,1:T(8,128)} async-done(((f32[192,768]{0,1:T(8,128)}), f32[192,24]{0,1:T(8,128)}) %reduce-scatter.14.cloned.1.call-update) | async-done | bytes 18448 | tf_op jit(solution)/shard_map/reduce_scatter | solution.py:67
  796.2 83.0 %reduce-scatter.16.cloned.1.call-done = f32[24,768]{1,0:T(8,128)} async-done(((f32[768,768]{1,0:T(8,128)}), f32[24,768]{1,0:T(8,128)}) %reduce-scatter.16.cloned.1.call-update) | async-done | bytes 73744 | tf_op jit(solution)/shard_map/reduce_scatter | solution.py:63
  879.2 82.8 %reduce-scatter.18.cloned.1.call-done = f32[24,768]{1,0:T(8,128)} async-done(((f32[768,768]{1,0:T(8,128)}), f32[24,768]{1,0:T(8,128)}) %reduce-scatter.18.cloned.1.call-update) | async-done | bytes 73744 | tf_op jit(solution)/shard_map/reduce_scatter | solution.py:63
  962.0 83.0 %reduce-scatter.20.cloned.1.call-done = f32[768,24]{0,1:T(8,128)} async-done(((f32[768,768]{0,1:T(8,128)}), f32[768,24]{0,1:T(8,128)}) %reduce-scatter.20.cloned.1.call-update) | async-done | bytes 73744 | tf_op jit(solution)/shard_map/reduce_scatter | solution.py:67
  (150 shorter events, 58.5 us)
Async XLA Ops:
  7.2 213.8 %all-gather.8.cloned.1.call-start = ((), (), s32[]{:S(2)}) async-start(), calls=%async_computation.9 | async-start | bytes 1216512 | tf_op jit(solution)/shard_map/all_gather | solution.py:59
  7.9 222.2 %all-gather.6.cloned.1.call-start = ((), (), s32[]{:S(2)}) async-start(), calls=%async_computation.8 | async-start | bytes 1216512 | tf_op jit(solution)/shard_map/all_gather | solution.py:55
  8.7 229.3 %all-gather.4.cloned.1.call-start = ((), (), s32[]{:S(2)}) async-start(), calls=%async_computation.7 | async-start | bytes 1216512 | tf_op jit(solution)/shard_map/all_gather | solution.py:55
  9.4 470.2 %all-reduce.12.cloned.1.call-start = ((), (), s32[]{:S(2)}) async-start(), calls=%async_computation.17 | async-start | bytes 18874368 | tf_op jit(solution)/shard_map/psum | solution.py:95
  81.2 156.8 %copy-start.28 = (f32[768]{0:T(1024)}, f32[768]{0:T(1024)S(1)}, u32[]{:S(2)}) copy-start(f32[768]{0:T(1024)S(1)} %all-reduce.4) | copy-start | bytes 9220
  81.2 27.3 %copy-start.38 = (bf16[24,64]{1,0:T(8,128)(2,1)S(1)}, bf16[24,64]{1,0:T(8,128)(2,1)}, u32[]{:S(2)}) copy-start(bf16[24,64]{1,0:T(8,128)(2,1)} %param.15) | copy-start | bytes 9220
  81.2 52.0 %copy-start.35 = (bf16[24,192]{1,0:T(8,128)(2,1)S(1)}, bf16[24,192]{1,0:T(8,128)(2,1)}, u32[]{:S(2)}) copy-start(bf16[24,192]{1,0:T(8,128)(2,1)} %param.13) | copy-start | bytes 27652
  81.2 74.1 %copy-start.36 = (bf16[192,24]{0,1:T(8,128)(2,1)S(1)}, bf16[192,24]{0,1:T(8,128)(2,1)}, u32[]{:S(2)}) copy-start(bf16[192,24]{0,1:T(8,128)(2,1)} %param.16) | copy-start | bytes 27652
  86.6 96.8 %copy-start.26 = (f32[12,256]{1,0:T(8,128)}, f32[12,256]{1,0:T(8,128)S(1)}, u32[]{:S(2)}) copy-start(f32[12,256]{1,0:T(8,128)S(1)} %fusion.16) | copy-start | bytes 36868
  86.7 151.3 %copy-start.23 = (f32[12,256]{1,0:T(8,128)}, f32[12,256]{1,0:T(8,128)S(1)}, u32[]{:S(2)}) copy-start(f32[12,256]{1,0:T(8,128)S(1)} %fusion.61) | copy-start | bytes 36868
  86.9 132.4 %copy-start.13 = (f32[256,32]{0,1:T(8,128)}, f32[256,32]{0,1:T(8,128)S(1)}, u32[]{:S(2)}) copy-start(f32[256,32]{0,1:T(8,128)S(1)} %get-tuple-element.28) | copy-start | bytes 98308
  86.9 132.4 %copy-start.15 = (f32[256,32]{0,1:T(8,128)}, f32[256,32]{0,1:T(8,128)S(1)}, u32[]{:S(2)}) copy-start(f32[256,32]{0,1:T(8,128)S(1)} %get-tuple-element.29) | copy-start | bytes 98308
  108.5 74.9 %copy-start.19 = (bf16[768,64]{1,0:T(8,128)(2,1)}, bf16[768,64]{1,0:T(8,128)(2,1)S(1)}, u32[]{:S(2)}) copy-start(bf16[768,64]{1,0:T(8,128)(2,1)S(1)} %all_gather.33) | copy-start | bytes 294916
  133.2 50.2 %copy-start.17 = (bf16[768,64]{1,0:T(8,128)(2,1)}, bf16[768,64]{1,0:T(8,128)(2,1)S(1)}, u32[]{:S(2)}) copy-start(bf16[768,64]{1,0:T(8,128)(2,1)S(1)} %all_gather.34) | copy-start | bytes 294916
  190.8 8.4 copy-start.9
  190.8 8.4 copy-start.11
  211.0 8.9 copy-start.2
  211.1 8.2 copy-start.33
  220.9 35.7 %copy-start.5 = (bf16[12,256,3,64]{1,3,2,0:T(8,128)(2,1)}, bf16[12,256,3,64]{1,3,2,0:T(8,128)(2,1)S(1)}, u32[]{:S(2)}) copy-start(bf16[12,256,3,64]{1,3,2,0:T(8,128)(2,1)S(1)} %convolution_convert_fusion.4) | copy-start | bytes 3538948
  238.0 12.8 %copy-start.39 = (bf16[768,768]{0,1:T(8,128)(2,1)S(1)}, bf16[768,768]{0,1:T(8,128)(2,1)}, u32[]{:S(2)}) copy-start(bf16[768,768]{0,1:T(8,128)(2,1)} %all-gather.8.cloned.1.call-done) | copy-start | bytes 3538948
  238.0 12.8 %copy-start.43 = (bf16[12,256,768]{2,1,0:T(8,128)(2,1)S(1)}, bf16[12,256,768]{2,1,0:T(8,128)(2,1)}, u32[]{:S(2)}) copy-start(bf16[12,256,768]{2,1,0:T(8,128)(2,1)} %convolution_convert_fusion.1) | copy-start | bytes 14155780
  260.4 8.7 copy-start.41
  278.9 297.1 %reduce-scatter.24.cloned.1.call-start = ((), (), s32[]{:S(2)}) async-start(), calls=%async_computation.16 | async-start | bytes 405504
  357.9 275.8 %reduce-scatter.22.cloned.1.call-start = ((), (), s32[]{:S(2)}) async-start(), calls=%async_computation.15 | async-start | bytes 405504
  364.4 350.6 %reduce-scatter.12.cloned.1.call-start = ((), (), s32[]{:S(2)}) async-start(), calls=%async_computation.10 | async-start | bytes 811008 | tf_op jit(solution)/shard_map/reduce_scatter | solution.py:63
  370.4 425.8 %reduce-scatter.14.cloned.1.call-start = ((), (), s32[]{:S(2)}) async-start(), calls=%async_computation.11 | async-start | bytes 811008 | tf_op jit(solution)/shard_map/reduce_scatter | solution.py:67
  375.7 503.5 %reduce-scatter.16.cloned.1.call-start = ((), (), s32[]{:S(2)}) async-start(), calls=%async_computation.12 | async-start | bytes 2433024 | tf_op jit(solution)/shard_map/reduce_scatter | solution.py:63
  385.1 13.0 %copy-start.8 = (f32[12,256,32]{1,2,0:T(8,128)S(1)}, f32[12,256,32]{1,2,0:T(8,128)}, u32[]{:S(2)}) copy-start(f32[12,256,32]{1,2,0:T(8,128)} %copy-done.7) | copy-start | bytes 1179652
  385.2 13.0 %copy-start.20 = (bf16[768,64]{1,0:T(8,128)(2,1)S(1)}, bf16[768,64]{1,0:T(8,128)(2,1)}, u32[]{:S(2)}) copy-start(bf16[768,64]{1,0:T(8,128)(2,1)} %copy-done.19) | copy-start | bytes 294916
  385.2 576.9 %reduce-scatter.18.cloned.1.call-start = ((), (), s32[]{:S(2)}) async-start(), calls=%async_computation.13 | async-start | bytes 2433024 | tf_op jit(solution)/shard_map/reduce_scatter | solution.py:63
  397.2 647.8 %reduce-scatter.20.cloned.1.call-start = ((), (), s32[]{:S(2)}) async-start(), calls=%async_computation.14 | async-start | bytes 2433024 | tf_op jit(solution)/shard_map/reduce_scatter | solution.py:67
  403.3 76.3 %copy-start.18 = (bf16[768,64]{1,0:T(8,128)(2,1)S(1)}, bf16[768,64]{1,0:T(8,128)(2,1)}, u32[]{:S(2)}) copy-start(bf16[768,64]{1,0:T(8,128)(2,1)} %copy-done.17) | copy-start | bytes 294916
  (24 other events, 124.5 us)
Sparse Core Ops, SparseCore 0:
  10.3 45.3 all-gather.7
  58.0 42.1 all-gather.5
  102.5 42.0 all-gather.3
  279.0 200.5 all-reduce.11
  483.5 73.5 reduce-scatter.23
  560.9 72.6 reduce-scatter.21
  637.7 77.1 reduce-scatter.11
  719.0 77.1 reduce-scatter.13
  800.4 78.8 reduce-scatter.15
  883.2 78.8 reduce-scatter.17
  966.2 78.8 reduce-scatter.19
where the time goes:
time: 1060 us; the launch traced here: 1050 us
  waiting for transfers between devices  537 us (51%)
  blocking collectives  291 us (27%)
  matrix products  173 us (16%)
  other arithmetic  29.1 us (3%)
  between operations  16.2 us (2%)
    reduce_scatter x3, waiting for transfers between devices, scatter_rows(): return lax.psum_scatter(grad_full, 'fsdp', scatter_dimension=0, tiled=True)  247 us
    reduce_scatter x2, waiting for transfers between devices, scatter_cols(): return lax.psum_scatter(grad_full, 'fsdp', scatter_dimension=1, tiled=True)  164 us
    dot_general x21, matrix products, matmul_f32(): return jnp.einsum(form, left, right, preferred_element_type=jnp.float32)  139 us
    unnamed x2, blocking collectives  136 us
    all_gather x3, blocking collectives, gather_rows(): return lax.all_gather(w_part, 'fsdp', axis=0, tiled=True)  68.4 us
    psum x1, waiting for transfers between devices, device_step(): branch_sum = lax.psum(branch_part, 'tp')  65.2 us
    psum x1, blocking collectives, device_step(): lax.psum(jnp.concatenate([dk_part, dv_part], axis=-1).astype(jnp.float32)...  61.8 us
    unnamed x13, waiting for transfers between devices  59.9 us
  transfers between devices with their start and end apart: 11, of which 7 were waited for; matrix products, arithmetic and copies ran while one was open for 16% of the time, Pallas kernels for 0%

commit v1 on v0

v1 whole, which is shorter than its diff:
```python
import math
import jax
import jax.numpy as jnp
from jax import lax
from jax.sharding import PartitionSpec as P


def layer_norm(x_f32, gain):
    x_mean = jnp.mean(x_f32, axis=-1, keepdims=True)
    x_cent = x_f32 - x_mean
    x_var = jnp.mean(x_cent * x_cent, axis=-1, keepdims=True)
    return (x_cent * lax.rsqrt(x_var + 1e-5) * gain).astype(jnp.bfloat16)


def rotate(vals, cos_t, sin_t):
    half_dim = vals.shape[-1] // 2
    first = vals[..., :half_dim]
    second = vals[..., half_dim:]
    return jnp.concatenate([first * cos_t - second * sin_t, second * cos_t + first * sin_t], axis=-1)


def qk_post(q_raw, k_raw):
    seq_len = k_raw.shape[1]
    head_dim = k_raw.shape[2]
    half_dim = head_dim // 2
    inv_freq = jnp.power(10000.0, -2.0 * jnp.arange(half_dim, dtype=jnp.float32) / head_dim)
    angle = jnp.arange(seq_len, dtype=jnp.float32)[:, None] * inv_freq[None, :]
    cos_t = jnp.cos(angle)
    sin_t = jnp.sin(angle)
    q_rot = rotate(q_raw.astype(jnp.float32), cos_t[:, None, :], sin_t[:, None, :]) * (1.0 / math.sqrt(head_dim))
    k_rot = rotate(k_raw.astype(jnp.float32), cos_t, sin_t)
    return q_rot.astype(jnp.bfloat16), k_rot.astype(jnp.bfloat16)


def attend(q_rot, k_rot, v_val):
    seq_len = q_rot.shape[1]
    causal = lax.broadcasted_iota(jnp.int32, (seq_len, 1, seq_len), 0) >= lax.broadcasted_iota(jnp.int32, (seq_len, 1, seq_len), 2)
    scores = jnp.einsum('crie,cle->cril', q_rot, k_rot, preferred_element_type=jnp.float32)
    scores = jnp.where(causal, scores, -1e30)
    row_max = lax.stop_gradient(jnp.max(scores, axis=-1, keepdims=True))
    exp_val = jnp.exp(scores - row_max)
    att_prob = (exp_val / jnp.sum(exp_val, axis=-1, keepdims=True)).astype(jnp.bfloat16)
    return jnp.einsum('cril,cle->crie', att_prob, v_val, preferred_element_type=jnp.float32).astype(jnp.bfloat16)


def swiglu(gate_val, up_val):
    return (jax.nn.silu(gate_val.astype(jnp.float32)) * up_val.astype(jnp.float32)).astype(jnp.bfloat16)


def matmul_f32(form, left, right):
    return jnp.einsum(form, left, right, preferred_element_type=jnp.float32)


def solution(mesh):
    n_tp = mesh.shape['tp']
    n_fsdp = mesh.shape['fsdp']
    both = ('tp', 'fsdp')

    def device_step(x_in, dy_out, ln_gain, w_q, w_k, w_v, w_o, w_gate, w_up, w_down):
        bf16 = jnp.bfloat16
        f32 = jnp.float32
        n_batch, seq_len, width = x_in.shape
        head_dim = w_k.shape[1]
        rows = w_q.shape[0]
        nq = w_q.shape[1]
        nf = w_gate.shape[1]
        mine = n_batch // n_tp
        tp = lax.axis_index('tp')
        gain_hi = lax.reduce_precision(ln_gain, 8, 7)
        gain_mid = lax.reduce_precision(ln_gain - gain_hi, 8, 7)
        gain_lo = ln_gain - gain_hi - gain_mid
        gain_cols = jnp.stack([gain_hi, gain_mid, gain_lo], axis=1).astype(bf16)
        packed = jnp.concatenate([w_q, w_gate, w_up, w_o.T, w_down.T, w_k, w_v, jnp.pad(gain_cols, ((0, 0), (0, 125)))], axis=1)
        cuts = [0, nq, nq + nf, nq + 2 * nf, 2 * nq + 2 * nf, 2 * nq + 3 * nf]
        last = cuts[-1]
        full = lax.all_gather(packed, both, axis=0, tiled=True).reshape(n_tp, n_fsdp * rows, packed.shape[1])
        wq_t = full[:, :, cuts[0]:cuts[1]]
        wg_t = full[:, :, cuts[1]:cuts[2]]
        wu_t = full[:, :, cuts[2]:cuts[3]]
        wo_t = full[:, :, cuts[3]:cuts[4]]
        wd_t = full[:, :, cuts[4]:cuts[5]]
        wk_full = full[0, :, last:last + head_dim]
        wv_full = full[0, :, last + head_dim:last + 2 * head_dim]
        gain3 = full[0, :, last + 2 * head_dim:last + 2 * head_dim + 3].astype(f32)
        gain_full = gain3[:, 0] + gain3[:, 1] + gain3[:, 2]

        x_my = lax.dynamic_slice_in_dim(x_in, tp * mine, mine, 0)
        dy_my = lax.dynamic_slice_in_dim(dy_out, tp * mine, mine, 0)
        tokens = mine * seq_len
        x_f32 = x_my.reshape(tokens, width).astype(f32)
        dy_tok = dy_my.reshape(tokens, width)
        h_norm, norm_pull = jax.vjp(layer_norm, x_f32, gain_full)
        q_raw = matmul_f32('md,tde->mte', h_norm, wq_t).astype(bf16)
        k_raw = matmul_f32('md,de->me', h_norm, wk_full).astype(bf16)
        v_val = matmul_f32('md,de->me', h_norm, wv_full).astype(bf16)
        gate_val = matmul_f32('md,tdf->tmf', h_norm, wg_t).astype(bf16)
        up_val = matmul_f32('md,tdf->tmf', h_norm, wu_t).astype(bf16)
        q_heads = q_raw.reshape(mine, seq_len, -1, head_dim)
        (q_rot, k_rot), rope_pull = jax.vjp(qk_post, q_heads, k_raw.reshape(mine, seq_len, head_dim))
        att_out, att_pull = jax.vjp(attend, q_rot, k_rot, v_val.reshape(mine, seq_len, head_dim))
        mlp_act, act_pull = jax.vjp(swiglu, gate_val, up_val)
        att_flat = att_out.reshape(tokens, n_tp, nq)
        branch = matmul_f32('mte,tde->md', att_flat, wo_t) + matmul_f32('tmf,tdf->md', mlp_act, wd_t)
        y_my = (x_f32 + branch).astype(bf16).reshape(mine, seq_len, width)
        y_out = lax.all_gather(y_my, 'tp', axis=0, tiled=True)

        d_att = matmul_f32('md,tde->mte', dy_tok, wo_t).astype(bf16).reshape(mine, seq_len, -1, head_dim)
        d_act = matmul_f32('md,tdf->tmf', dy_tok, wd_t).astype(bf16)
        d_gate, d_up = act_pull(d_act)
        d_qrot, d_krot, d_val = att_pull(d_att)
        d_qraw, d_kraw = rope_pull((d_qrot, d_krot))
        d_qflat = d_qraw.reshape(tokens, n_tp, nq)
        d_kflat = d_kraw.reshape(tokens, head_dim)
        d_vflat = d_val.reshape(tokens, head_dim)
        dh_full = (matmul_f32('mte,tde->md', d_qflat, wq_t) + matmul_f32('tmf,tdf->md', d_gate, wg_t) + matmul_f32('tmf,tdf->md', d_up, wu_t)
                   + matmul_f32('me,de->md', d_kflat, wk_full) + matmul_f32('me,de->md', d_vflat, wv_full)).astype(bf16)
        dx_norm, gain_part = norm_pull(dh_full)
        gx_my = (dy_tok.astype(f32) + dx_norm).astype(bf16).reshape(mine, seq_len, width)
        grad_x = lax.all_gather(gx_my, 'tp', axis=0, tiled=True)
        g_q = matmul_f32('md,mte->dte', h_norm, d_qflat)
        g_g = matmul_f32('md,tmf->dtf', h_norm, d_gate)
        g_u = matmul_f32('md,tmf->dtf', h_norm, d_up)
        g_o = matmul_f32('md,mte->dte', dy_tok, att_flat)
        g_d = matmul_f32('md,tmf->dtf', dy_tok, mlp_act)
        g_k = matmul_f32('md,me->de', h_norm, d_kflat)
        g_v = matmul_f32('md,me->de', h_norm, d_vflat)
        small = jnp.concatenate([g_k, g_v, jnp.pad(gain_part[:, None], ((0, 0), (0, 127)))], axis=1)
        small = jnp.broadcast_to(small[:, None], (width, n_tp, small.shape[1]))
        g_all = jnp.concatenate([g_q, g_g, g_u, g_o, g_d, small], axis=2).reshape(width, -1)
        g_row = lax.psum_scatter(g_all, 'fsdp', scatter_dimension=0, tiled=True)
        g_row = jnp.swapaxes(g_row.reshape(rows, n_tp, -1), 0, 1).reshape(n_tp * rows, -1)
        g_loc = lax.psum_scatter(g_row, 'tp', scatter_dimension=0, tiled=True)
        grad_wq = g_loc[:, cuts[0]:cuts[1]]
        grad_wgate = g_loc[:, cuts[1]:cuts[2]]
        grad_wup = g_loc[:, cuts[2]:cuts[3]]
        grad_wo = g_loc[:, cuts[3]:cuts[4]].T
        grad_wdown = g_loc[:, cuts[4]:cuts[5]].T
        grad_wk = g_loc[:, last:last + head_dim]
        grad_wv = g_loc[:, last + head_dim:last + 2 * head_dim]
        grad_gain = g_loc[:, last + 2 * head_dim]
        return (y_out, grad_x, grad_gain, grad_wq, grad_wk, grad_wv, grad_wo, grad_wgate, grad_wup, grad_wdown)

    act_spec = P('fsdp', None, None)
    row_spec = P('fsdp', 'tp')
    kv_spec = P('fsdp', None)
    col_spec = P('tp', 'fsdp')
    in_specs = (act_spec, act_spec, P('fsdp'), row_spec, kv_spec, kv_spec, col_spec, row_spec, row_spec, col_spec)
    out_specs = (act_spec, act_spec, P('fsdp'), row_spec, kv_spec, kv_spec, col_spec, row_spec, row_spec, col_spec)
    return jax.shard_map(device_step, mesh=mesh, in_specs=in_specs, out_specs=out_specs, check_vma=False)
```

time: 1060 us -> 687 us (0.65)
  blocking collectives: 291 us -> 0 us
  waiting for transfers between devices: 537 us -> 378 us
  local copies, waits for them, and re-layouts: 5.4 us -> 106 us
  other arithmetic: 29.1 us -> 18.1 us
    reduce_scatter x5 -> x0, waiting for transfers between devices: 411 us -> none  [the longest x3 247 us: scatter_rows(): return lax.psum_scatter(grad_full, 'fsdp', scatter_dimension=0, tiled=True)]
    all_gather x3, waiting for transfers between devices: 0.02 us -> 178 us  [the longest x1 80.3 us: device_step(): lax.all_gather(packed, both, axis=0, tiled=True)]
    unnamed x13 -> x7, waiting for transfers between devices: 59.9 us -> 200 us
    unnamed x2 -> x0, blocking collectives: 136 us -> none
    all_gather x4 -> x0, blocking collectives: 93.1 us -> none  [the longest x3 68.4 us: gather_rows(): return lax.all_gather(w_part, 'fsdp', axis=0, tiled=True)]
    psum x1 -> x0, waiting for transfers between devices: 65.2 us -> none  [device_step(): branch_sum = lax.psum(branch_part, 'tp')]
    psum x1 -> x0, blocking collectives: 61.8 us -> none  [device_step(): lax.psum(jnp.concatenate([dk_part, dv_part], axis=-1).astype(jnp.float32)...]
    unnamed x94 -> x93, local copies, waits for them, and re-layouts: 5.4 us -> 64.9 us
  transfers between devices with their start and end apart: 11 -> 5, of which waited for: 7 -> 5; matrix products, arithmetic and copies ran while one was open for 16% -> 6% of each run, Pallas kernels for 0% -> 0%
where the time goes in v1:
time: 687 us; the launch traced here: 682 us
  waiting for transfers between devices  378 us (55%)
  matrix products  165 us (24%)
  local copies, waits for them, and re-layouts  106 us (15%)
  other arithmetic  18.1 us (3%)
  between operations  15.2 us (2%)
    unnamed x7, waiting for transfers between devices  200 us
    dot_general x17, matrix products, matmul_f32(): return jnp.einsum(form, left, right, preferred_element_type=jnp.float32)  125 us
    all_gather x1, waiting for transfers between devices, device_step(): lax.all_gather(packed, both, axis=0, tiled=True)  80.3 us
    unnamed x93, local copies, waits for them, and re-layouts  64.9 us
    all_gather x1, waiting for transfers between devices, device_step(): grad_x = lax.all_gather(gx_my, 'tp', axis=0, tiled=True)  55 us
    all_gather x1, waiting for transfers between devices, device_step(): y_out = lax.all_gather(y_my, 'tp', axis=0, tiled=True)  42.9 us
  transfers between devices with their start and end apart: 5, of which 5 were waited for; matrix products, arithmetic and copies ran while one was open for 6% of the time, Pallas kernels for 0%

profile of v1, /device:TPU:0, one launch (start us, length us, event | category | flops | bytes accessed | tf_op | source)
XLA Modules:
  0.0 681.9 jit_solution(15089660143678186127)
XLA Ops:
  15.4 80.3 %all-gather.4.cloned.1.call-done = bf16[3072,2944]{1,0:T(8,128)(2,1)} async-done(((bf16[24,2944]{1,0:T(8,128)(2,1)}), bf16[3072,2944]{1,0:T(8,128)(2,1)}) %all-gather.4.cloned.1.call-update) | async-done | bytes 18087952 | tf_op jit(solution)/shard_map/all_gather | solution.py:76
  96.7 4.6 fusion.115
  106.8 12.7 %fusion.34 = bf16[4,768,768]{2,1,0:T(8,128)(2,1)} fusion(bf16[4,768,2944]{2,1,0:T(8,128)(2,1)} %bitcast.265, bf16[768,768]{1,0:T(8,128)(2,1)S(1)} %fusion.55), kind=kOutput, calls=%fused_computation.48 | convolution fusion | flops 3626237952 | bytes 10616832 | tf_op jit(solution)/shard_map/md,tdf->tmf/dot_general | solution.py:51
  119.6 12.3 %fusion.31 = bf16[4,768,768]{2,1,0:T(8,128)(2,1)} fusion(bf16[4,768,2944]{2,1,0:T(8,128)(2,1)} %bitcast.266, bf16[768,768]{1,0:T(8,128)(2,1)S(1)} %fusion.55), kind=kOutput, calls=%fused_computation.47 | convolution fusion | flops 3626237952 | bytes 10616832 | tf_op jit(solution)/shard_map/md,tdf->tmf/dot_general | solution.py:51
  137.8 2.7 fusion.124
  142.2 4.5 reshape.332
  151.9 8.8 %fusion.119 = (f32[3,256,12]{1,2,0:T(8,128)}, f32[3,256,12,256]{1,3,2,0:T(8,128)}) fusion(pred[256,256]{0,1:T(8,128)(4,1)} %iota_compare_fusion.1, bf16[3,256,32]{1,2,0:T(8,128)(2,1)} %get-tuple-element.32, bf16[3,256,32]{1,2,0:T(8,128)(2,1)} %get-tuple-element.31, f32[3,256,12,32]{1,3,2,0:T(8,128)} %get-tuple-element.19, ...), kind=kOutput, calls=%fused_computation.168 | convolution fusion | flops 311034112 | bytes 11997184 | tf_op jit(solution)/shard_map/jvp()/sub | solution.py:41
  163.7 2.6 copy.150
  170.8 8.9 %fusion.5 = (f32[3,256,12]{1,2,0:T(8,128)S(1)}, bf16[3,256,12,256]{1,3,2,0:T(8,128)(2,1)S(1)}, bf16[3,256,12,256]{1,3,2,0:T(8,128)(2,1)}) fusion(f32[3,256,12,256]{1,3,2,0:T(8,128)} %get-tuple-element.45, f32[3,256,12]{1,2,0:T(8,128)} %multiply_divide_fusion, f32[3,256,12]{1,2,0:T(8,128)} %get-tuple-element.44, bf16[3,256,64,1]{1,0,2,3:T(4,128)(2,1)} %bitcast.276, ...), kind=kOutput, calls=%fused_computation.8 | convolution fusion | flops 318495744 | bytes 20262912 | tf_op jit(solution)/shard_map/transpose(jvp(cril,cle->crie))/dot_general | solution.py:43
  182.7 6.2 fusion.70
  188.9 6.1 convert_multiply_fusion.3
  199.2 3.0 fusion.78
  202.3 2.9 fusion.79
  205.1 7.9 %fusion.37 = bf16[4,768,768]{2,1,0:T(8,128)(2,1)} fusion(bf16[768,768,1]{1,0,2:T(8,128)(2,1)S(1)} %bitcast.247, bf16[4,768,2944]{2,1,0:T(8,128)(2,1)} %bitcast.269), kind=kOutput, calls=%fused_computation.49 | convolution fusion | flops 3626237952 | bytes 10616832 | tf_op jit(solution)/shard_map/md,tdf->tmf/dot_general | solution.py:51
  215.8 3.3 reshape.323
  219.0 4.3 fusion.100
  223.4 13.9 %fusion.25 = f32[768,768,1]{1,0,2:T(8,128)} fusion(bf16[4,768,2944]{2,1,0:T(8,128)(2,1)} %bitcast.271, bf16[4,768,768]{2,1,0:T(8,128)(2,1)} %fusion.37, bf16[4,768,768]{2,1,0:T(8,128)(2,1)} %fusion.31), kind=kOutput, calls=%fused_computation.38 | convolution fusion | flops 3642753024 | bytes 16515072 | tf_op jit(solution)/shard_map/tmf,tdf->md/dot_general | solution.py:51
  237.3 19.1 %fusion.42 = (f32[768]{0:T(1024)S(1)}, bf16[768,768]{1,0:T(8,128)(2,1)S(1)}) fusion(bf16[3,256,768]{2,1,0:T(8,128)(2,1)S(1)} %get-tuple-element.13, f32[768]{0:T(1024)S(1)} %fusion.76, f32[768]{0:T(1024)S(1)} %div.83, f32[768,768]{1,0:T(8,128)} %fusion.78, f32[768,768]{1,0:T(8,128)} %fusion.79, f32[768,768,1]{1,0,2:T(8,128)} %fusion.25, ...), kind=kOutput, calls=%fused_computation.53 | convolution fusion | flops 3663396096 | bytes 30680064 | tf_op jit(solution)/shard_map/tmf,tdf->md/dot_general | solution.py:51
  260.2 12.1 %convolution_dynamic-update-slice_fusion.2 = f32[768,4,2944]{0,2,1:T(8,128)} fusion(f32[768,4,2944]{0,2,1:T(8,128)} %constant_dynamic-update-slice_fusion.1, bf16[768,768]{1,0:T(8,128)(2,1)S(1)} %copy-done.10, bf16[4,768,768]{2,1,0:T(8,128)(2,1)} %fusion.31, bf16[4,768,768]{2,1,0:T(8,128)(2,1)} %fusion.34, bf16[4,768,768]{2,1,0:T(8,128)(2,1)} %fusion.37), kind=kOutput, calls=%fused_computation.31 | convolution fusion | flops 3656908800 | bytes 24772608 | tf_op jit(solution)/shard_map/md,tmf->dtf/dot_general | solution.py:51
  272.4 7.4 %convolution_dynamic-update-slice_fusion.1 = f32[768,4,2944]{0,2,1:T(8,128)} fusion(f32[768,4,2944]{0,2,1:T(8,128)} %convolution_dynamic-update-slice_fusion.2, bf16[768,768]{1,0:T(8,128)(2,1)S(1)} %copy-done.10, bf16[4,768,768]{2,1,0:T(8,128)(2,1)S(1)} %bitcast.287, bf16[4,768,768]{2,1,0:T(8,128)(2,1)S(1)} %bitcast.285), kind=kOutput, calls=%fused_computation.30 | convolution fusion | flops 3642753024 | bytes 20054016 | tf_op jit(solution)/shard_map/md,tmf->dtf/dot_general | solution.py:51
  283.6 7.0 %convolution_dynamic-update-slice_fusion = f32[768,4,2944]{0,2,1:T(8,128)} fusion(f32[768,4,2944]{0,2,1:T(8,128)} %constant_dynamic-update-slice_fusion, bf16[768,768,1]{1,0,2:T(8,128)(2,1)S(1)} %bitcast.249, bf16[4,768,768]{2,1,0:T(8,128)(2,1)S(1)} %bitcast.283, bf16[4,768,768]{2,1,0:T(8,128)(2,1)S(1)} %bitcast.285), kind=kOutput, calls=%fused_computation.29 | convolution fusion | flops 3642753024 | bytes 20054016 | tf_op jit(solution)/shard_map/md,tmf->dtf/dot_general | solution.py:51
  294.6 36.3 %copy.143 = f32[768,11776]{1,0:T(8,128)} copy(f32[768,11776]{0,1:T(8,128)} %bitcast.237) | data formatting | bytes 72351744
  331.0 2.7 reshape.319
  333.7 4.0 fusion.98
  337.7 12.5 %fusion.49 = bf16[768,768]{1,0:T(8,128)(2,1)} fusion(f32[768,768,1]{1,0,2:T(8,128)S(1)} %fusion.98, bf16[3,256,768]{2,1,0:T(8,128)(2,1)S(1)} %get-tuple-element.13, bf16[4,768,2944]{2,1,0:T(8,128)(2,1)} %bitcast.274, bf16[4,768,768]{2,1,0:T(8,128)(2,1)} %fusion.34, bf16[4,768,768]{2,1,0:T(8,128)(2,1)} %fusion.31), kind=kOutput, calls=%fused_computation.64 | convolution fusion | flops 3645112320 | bytes 18874368 | tf_op jit(solution)/shard_map/tmf,tdf->md/dot_general | solution.py:51
  353.1 150.1 %reduce-scatter.4.cloned.1.call-done = f32[24,11776]{1,0:T(8,128)} async-done(((f32[768,11776]{1,0:T(8,128)}), f32[24,11776]{1,0:T(8,128)}) %reduce-scatter.4.cloned.1.call-update) | async-done | bytes 1130512
  503.2 4.9 copy.144
  508.1 5.3 copy.123
  514.6 42.9 %all-gather.6.cloned.1.call-done = bf16[12,256,768]{2,1,0:T(8,128)(2,1)} async-done(((bf16[3,256,768]{2,1,0:T(8,128)(2,1)}), bf16[12,256,768]{2,1,0:T(8,128)(2,1)}) %all-gather.6.cloned.1.call-update) | async-done | bytes 4718608 | tf_op jit(solution)/shard_map/all_gather | solution.py:105
  557.5 55.0 %all-gather.8.cloned.1.call-done = bf16[12,256,768]{2,1,0:T(8,128)(2,1)} async-done(((bf16[3,256,768]{2,1,0:T(8,128)(2,1)}), bf16[12,256,768]{2,1,0:T(8,128)(2,1)}) %all-gather.8.cloned.1.call-update) | async-done | bytes 4718608 | tf_op jit(solution)/shard_map/all_gather | solution.py:119
  612.5 49.3 %all-reduce.9.cloned.1.call-done = f32[96,2944]{1,0:T(8,128)} async-done(((f32[96,2944]{1,0:T(8,128)}), f32[96,2944]{1,0:T(8,128)}) %all-reduce.9.cloned.1.call-update) | async-done | bytes 1130512
  667.9 5.0 copy.186
  (160 shorter events, 68.1 us)
Async XLA Ops:
  7.2 88.5 %all-gather.4.cloned.1.call-start = ((), (), s32[]{:S(2)}) async-start(), calls=%async_computation.1 | async-start | bytes 18229248 | tf_op jit(solution)/shard_map/all_gather | solution.py:76
  9.7 493.5 %reduce-scatter.4.cloned.1.call-start = ((), (), s32[]{:S(2)}) async-start(), calls=%async_computation.4 | async-start | bytes 37306368
  12.3 89.0 %copy-start.28 = (f32[768]{0:T(1024)}, f32[768]{0:T(1024)S(1)}, u32[]{:S(2)}) copy-start(f32[768]{0:T(1024)S(1)} %add.89) | copy-start | bytes 9220
  12.3 94.1 %copy-start.23 = (f32[768]{0:T(1024)}, f32[768]{0:T(1024)S(1)}, u32[]{:S(2)}) copy-start(f32[768]{0:T(1024)S(1)} %rsqrt.13) | copy-start | bytes 9220
  14.4 151.9 %copy-start.3 = (bf16[3,256,768]{2,1,0:T(8,128)(2,1)}, bf16[3,256,768]{2,1,0:T(8,128)(2,1)S(1)}, u32[]{:S(2)}) copy-start(bf16[3,256,768]{2,1,0:T(8,128)(2,1)S(1)} %constant_dynamic-slice_fusion) | copy-start | bytes 3538948
  96.7 5.1 copy-start.30
  106.8 12.8 %copy-start.9 = (bf16[768,768]{1,0:T(8,128)(2,1)}, bf16[768,768]{1,0:T(8,128)(2,1)S(1)}, u32[]{:S(2)}) copy-start(bf16[768,768]{1,0:T(8,128)(2,1)S(1)} %fusion.55) | copy-start | bytes 3538948
  170.8 8.9 %copy-start.21 = (bf16[3,256,64]{1,0,2:T(4,128)(2,1)S(1)}, bf16[3,256,64]{1,0,2:T(4,128)(2,1)}, u32[]{:S(2)}) copy-start(bf16[3,256,64]{1,0,2:T(4,128)(2,1)} %reshape.318) | copy-start | bytes 294916
  182.7 6.2 copy-start.26
  182.7 6.2 copy-start.27
  188.9 6.1 copy-start.14
  188.9 6.1 copy-start.16
  199.2 5.9 copy-start.4
  237.3 19.1 %copy-start.29 = (f32[768]{0:T(1024)S(1)}, f32[768]{0:T(1024)}, u32[]{:S(2)}) copy-start(f32[768]{0:T(1024)} %copy-done.28) | copy-start | bytes 9220
  237.3 19.1 %copy-start.1 = (bf16[3,256,12,64]{1,0,3,2:T(4,128)(2,1)S(1)}, bf16[3,256,12,64]{1,0,3,2:T(4,128)(2,1)}, u32[]{:S(2)}) copy-start(bf16[3,256,12,64]{1,0,3,2:T(4,128)(2,1)} %copy.112) | copy-start | bytes 3538948
  256.4 34.3 %copy-start.7 = (bf16[768,768]{1,0:T(8,128)(2,1)}, bf16[768,768]{1,0:T(8,128)(2,1)S(1)}, u32[]{:S(2)}) copy-start(bf16[768,768]{1,0:T(8,128)(2,1)S(1)} %get-tuple-element.48) | copy-start | bytes 3538948
  256.7 15.6 %slice-start.4 = ((s8[4718592]{0:T(1024)(128)(4,1)}), s8[4194304]{0:T(1024)(128)(4,1)S(1)}, s32[]{:S(2)}) async-start(s8[4718592]{0:T(1024)(128)(4,1)} %bitcast.284), calls=%async_computation.10 | async-start | bytes 8388608
  257.8 14.5 %slice-start.6 = ((s8[4718592]{0:T(1024)(128)(4,1)}), s8[4194304]{0:T(1024)(128)(4,1)S(1)}, s32[]{:S(2)}) async-start(s8[4718592]{0:T(1024)(128)(4,1)} %bitcast.286), calls=%async_computation.12 | async-start | bytes 8388608
  260.2 12.1 %slice-start.5 = ((s8[4718592]{0:T(1024)(128)(4,1)}), s8[524288]{0:T(1024)(128)(4,1)S(1)}, s32[]{:S(2)}) async-start(s8[4718592]{0:T(1024)(128)(4,1)} %bitcast.284), calls=%async_computation.11 | async-start | bytes 1048576
  260.2 12.1 %slice-start.7 = ((s8[4718592]{0:T(1024)(128)(4,1)}), s8[524288]{0:T(1024)(128)(4,1)S(1)}, s32[]{:S(2)}) async-start(s8[4718592]{0:T(1024)(128)(4,1)} %bitcast.286), calls=%async_computation.13 | async-start | bytes 1048576
  260.2 23.4 %slice-start.2 = ((s8[4718592]{0:T(1024)(128)(4,1)}), s8[4194304]{0:T(1024)(128)(4,1)S(1)}, s32[]{:S(2)}) async-start(s8[4718592]{0:T(1024)(128)(4,1)} %bitcast.282), calls=%async_computation.8 | async-start | bytes 8388608
  272.3 7.4 %copy-start = (bf16[3,256,12,64]{1,0,3,2:T(4,128)(2,1)S(1)}, bf16[3,256,12,64]{1,0,3,2:T(4,128)(2,1)}, u32[]{:S(2)}) copy-start(bf16[3,256,12,64]{1,0,3,2:T(4,128)(2,1)} %copy.104) | copy-start | bytes 3538948
  272.3 11.3 %slice-start.3 = ((s8[4718592]{0:T(1024)(128)(4,1)}), s8[524288]{0:T(1024)(128)(4,1)S(1)}, s32[]{:S(2)}) async-start(s8[4718592]{0:T(1024)(128)(4,1)} %bitcast.282), calls=%async_computation.9 | async-start | bytes 1048576
  283.6 7.1 %copy-start.24 = (f32[768]{0:T(1024)S(1)}, f32[768]{0:T(1024)}, u32[]{:S(2)}) copy-start(f32[768]{0:T(1024)} %copy-done.23) | copy-start | bytes 9220
  331.0 226.5 %all-gather.6.cloned.1.call-start = ((), (), s32[]{:S(2)}) async-start(), calls=%async_computation.2 | async-start | bytes 5898240 | tf_op jit(solution)/shard_map/all_gather | solution.py:105
  337.7 13.3 %copy-start.6 = (bf16[3,256,768]{2,1,0:T(8,128)(2,1)S(1)}, bf16[3,256,768]{2,1,0:T(8,128)(2,1)}, u32[]{:S(2)}) copy-start(bf16[3,256,768]{2,1,0:T(8,128)(2,1)} %copy-done.3) | copy-start | bytes 3538948
  337.7 13.3 %copy-start.8 = (bf16[768,768]{1,0:T(8,128)(2,1)S(1)}, bf16[768,768]{1,0:T(8,128)(2,1)}, u32[]{:S(2)}) copy-start(bf16[768,768]{1,0:T(8,128)(2,1)} %copy-done.7) | copy-start | bytes 3538948
  350.3 262.2 %all-gather.8.cloned.1.call-start = ((), (), s32[]{:S(2)}) async-start(), calls=%async_computation.3 | async-start | bytes 5898240 | tf_op jit(solution)/shard_map/all_gather | solution.py:119
  353.0 308.8 %all-reduce.9.cloned.1.call-start = ((), (), s32[]{:S(2)}) async-start(), calls=%async_computation.5 | async-start | bytes 2260992
  508.1 5.3 copy-start.31
  667.9 5.0 slice-start
  667.9 5.0 slice-start.1
  (13 other events, 26.0 us)
Sparse Core Ops, SparseCore 0:
  11.5 84.1 all-gather.3
  331.1 172.0 reduce-scatter.3
  505.4 51.9 all-gather.5
  559.6 52.9 all-gather.7
  614.7 47.0 all-reduce.8

commit v2 on v0

v2 whole, which is shorter than its diff:
```python
import jax
import jax.numpy as jnp
from jax import lax
from jax.sharding import PartitionSpec as P
from jax.experimental import pallas as pl
from jax.experimental.pallas import tpu as pltpu


N0, N1, N2, N3 = range(4)
RING = 4
SUB = 8
LANES = 128
PAIR = 256
KIB = 1024
ALL = Ellipsis
KV_AT = 1152
MESH_ID = pl.DeviceIdType.MESH


def gather_kernel(p_ref, g_ref, lsem, s1, r1, s2, r2, s3, r3, ds, dr):
    t = lax.axis_index('tp')
    f = lax.axis_index('fsdp')
    c = lax.rem(f, N2)
    at = {'x': t, 'y': lax.rem(lax.div(f, N2), RING), 'z': lax.div(f, SUB)}

    def up(i, d):
        return lax.rem(i + d, RING)

    def dev(where, cc):
        return {'tp': where['x'], 'fsdp': (where['z'] * RING + where['y']) * N2 + cc}

    def peer(axis, d):
        return dev({**at, axis: up(at[axis], d)}, c)

    partner = dev(at, N1 - c)
    barrier = pltpu.get_barrier_semaphore()
    greeted = [partner] + [peer(axis, d) for axis in 'xyz' for d in (N1, N2, N3)]
    for who in greeted:
        pl.semaphore_signal(barrier, inc=N1, device_id=who, device_id_type=MESH_ID)
    own = pltpu.make_async_copy(p_ref, g_ref.at[:, at['x'], at['z'], at['y'], c], lsem.at[N0])
    own.start()
    pl.semaphore_wait(barrier, len(greeted))

    sent = []

    def push(src, dst, s_sem, r_sem, who):
        copy = pltpu.make_async_remote_copy(src_ref=src, dst_ref=dst, send_sem=s_sem, recv_sem=r_sem, device_id=who, device_id_type=MESH_ID)
        copy.start()
        sent.append(copy)

    def landed(ref, s_sem, r_sem):
        pltpu.make_async_remote_copy(src_ref=ref, dst_ref=ref, send_sem=s_sem, recv_sem=r_sem, device_id=partner, device_id_type=MESH_ID).wait_recv()

    def view(k, h, fixed, core):
        spot = [fixed.get(axis, slice(None)) for axis in 'xzy']
        return g_ref.at[h, spot[N0], spot[N1], spot[N2], core, k]

    orders = ('xyz', 'yzx', 'zxy')
    both = slice(None)
    across = []

    def share(k, h, fixed, n):
        push(view(k, h, fixed, c), view(k, h, fixed, c), ds.at[k, n], dr.at[k, n], partner)
        across.append((k, h, fixed, n))

    def ring_start(k, axis, fixed, ss, rr):
        here = {**fixed, axis: at[axis]}
        for n in range(N2):
            push(view(k, n, here, c), view(k, n, here, c), ss.at[k, n], rr.at[k, n], peer(axis, N1))
            push(view(k, N1 - n, here, c), view(k, N1 - n, here, c), ss.at[k, N3 - n], rr.at[k, N3 - n], peer(axis, N3))

    def ring_forward(k, axis, fixed, ss, rr):
        for h, d, n in ((N0, N3, N0), (N1, N1, N3)):
            there = {**fixed, axis: up(at[axis], d)}
            landed(view(k, h, there, c), ss.at[k, n], rr.at[k, n])
            push(view(k, h, there, c), view(k, h, there, c), ss.at[k, RING + h], rr.at[k, RING + h], peer(axis, RING - d))

    def ring_share(k, axis, fixed, ss, rr, base):
        for m, (h, d, n) in enumerate(((N0, N3, N0), (N1, N1, N3), (N1, N3, N1), (N0, N1, N2), (N0, N2, RING), (N1, N2, 5))):
            there = {**fixed, axis: up(at[axis], d)}
            if n not in (N0, N3):
                landed(view(k, h, there, c), ss.at[k, n], rr.at[k, n])
            share(k, h, there, base + m)

    for k, order in enumerate(orders):
        for d in (N1, N3, N2):
            push(p_ref.at[:, k], view(k, both, at, c), s1.at[k, d - N1], r1.at[k, d - N1], peer(order[N0], d))
    own.wait()
    second = []
    third = []
    for k, order in enumerate(orders):
        for d in (N1, N3, N2):
            landed(view(k, both, {**at, order[N0]: up(at[order[N0]], RING - d)}, c), s1.at[k, d - N1], r1.at[k, d - N1])
        fixed = {order[N2]: at[order[N2]]}
        second.append((k, order[N1], fixed, s2, r2))
        third.append((k, order[N2], {}, s3, r3))
        ring_start(*second[k])
    for k, order in enumerate(orders):
        here = {order[N1]: at[order[N1]], order[N2]: at[order[N2]]}
        share(k, N0, here, N0)
        share(k, N1, here, N1)
    for k in range(N3):
        ring_forward(*second[k])
    for k in range(N3):
        ring_share(*second[k], N2)
        ring_start(*third[k])
    for k in range(N3):
        ring_forward(*third[k])
    for k in range(N3):
        ring_share(*third[k], SUB)
    for k, h, fixed, n in across:
        landed(view(k, h, fixed, N1 - c), ds.at[k, n], dr.at[k, n])
    for copy in sent:
        copy.wait_send()


def gather_weights(packed):
    dma = pltpu.SemaphoreType.DMA
    any_spec = pl.BlockSpec(memory_space=pl.ANY)
    wide = packed.shape[N2]
    return pl.pallas_call(
        gather_kernel,
        name='gather_weights',
        out_shape=jax.ShapeDtypeStruct((N2, RING, RING, RING, N2, N3, SUB, wide), packed.dtype),
        in_specs=[any_spec],
        out_specs=any_spec,
        scratch_shapes=[dma((N1,)), dma((N3, N3)), dma((N3, N3)), dma((N3, 6)), dma((N3, 6)), dma((N3, 6)), dma((N3, 6)), dma((N3, 14)), dma((N3, 14))],
        compiler_params=pltpu.CompilerParams(collective_id=N2, has_side_effects=True, vmem_limit_bytes=32 * KIB * KIB),
    )(packed.reshape(N2, N3, SUB, wide))


NT = (((N1,), (N1,)), ((), ()))
NN = (((N1,), (N0,)), ((), ()))
TN = (((N0,), (N0,)), ((), ()))


def dot(left, right, dims=NN):
    return lax.dot_general(left, right, dims, preferred_element_type=jnp.float32)


def proj_kernel(x_ref, dy_ref, gain_ref, w0_ref, w1_ref, wkv_ref, h_out, q_out, kv_out, do_out, act_out, dg_out, du_out):
    f32 = jnp.float32
    bf16 = jnp.bfloat16
    tokens = x_ref.shape[N0]

    @pl.when(pl.program_id(N0) == N0)
    def _():
        def norm(n, carry):
            at = pl.ds(n * LANES, LANES)
            x_f32 = x_ref[at, :].astype(f32)
            x_cent = x_f32 - jnp.mean(x_f32, axis=-N1, keepdims=True)
            x_var = jnp.mean(x_cent * x_cent, axis=-N1, keepdims=True)
            h_out[at, :] = (x_cent * lax.rsqrt(x_var + 1e-5) * gain_ref[ALL]).astype(bf16)
            return carry
        lax.fori_loop(N0, tokens // LANES, norm, N0)
        kv_out[ALL] = dot(h_out[ALL], wkv_ref[ALL]).astype(bf16)

    for n in range(N3):
        cols = slice(n * PAIR, n * PAIR + PAIR)
        gate = dot(h_out[ALL], w0_ref[N0, N0, :, cols]).astype(bf16).astype(f32)
        up = dot(h_out[ALL], w1_ref[N0, N0, :, cols]).astype(bf16).astype(f32)
        if n == N0:
            d_low = dot(dy_ref[ALL], w0_ref[N0, N0, :, 1280:1408])
            d_act = jnp.concatenate([d_low, dot(dy_ref[ALL], w1_ref[N0, N0, :, 768:896])], axis=N1)
        else:
            d_act = dot(dy_ref[ALL], w1_ref[N0, N0, :, 640 + n * PAIR:896 + n * PAIR])
        d_act = d_act.astype(bf16).astype(f32)
        sig = jax.nn.sigmoid(gate)
        silu = gate * sig
        act_out[N0, :, cols] = (silu * up).astype(bf16)
        du_out[N0, :, cols] = (d_act * silu).astype(bf16)
        dg_out[N0, :, cols] = (d_act * up * (sig * (1.0 + gate * (1.0 - sig)))).astype(bf16)
    q_out[N0] = dot(h_out[ALL], w0_ref[N0, N0, :, 768:KIB]).astype(bf16)
    do_out[N0] = dot(dy_ref[ALL], w0_ref[N0, N0, :, 896:1152]).astype(bf16)


def att_kernel(q_ref, kv_ref, do_ref, cq_ref, sq_ref, ck_ref, sk_ref, o_out, dq_out, dkv_out, dk_lo, dk_hi, dv_lo, dv_hi):
    f32 = jnp.float32
    bf16 = jnp.bfloat16
    seq_len = kv_ref.shape[N0]
    lane = lax.broadcasted_iota(jnp.int32, (seq_len, LANES), N1)
    low = lane < 64
    first = lax.rem(lane, 64) < 32
    causal = lax.broadcasted_iota(jnp.int32, (seq_len, seq_len), N0) >= lax.broadcasted_iota(jnp.int32, (seq_len, seq_len), N1)

    def other(vals):
        return jnp.where(first, pltpu.roll(vals, 96, N1), pltpu.roll(vals, 32, N1))

    kv_f32 = kv_ref[ALL].astype(f32)
    kv_rot = kv_f32 * ck_ref[ALL] + other(kv_f32) * sk_ref[ALL]
    zero = jnp.zeros_like(kv_rot)
    k_lo = jnp.where(low, kv_rot, zero)
    v_hi = jnp.where(low, zero, kv_rot)
    k_hi = pltpu.roll(k_lo, 64, N1).astype(bf16)
    v_lo = pltpu.roll(v_hi, 64, N1).astype(bf16)
    k_lo = k_lo.astype(bf16)
    v_hi = v_hi.astype(bf16)
    for ref in (dk_lo, dk_hi, dv_lo, dv_hi):
        ref[ALL] = jnp.zeros_like(ref)

    def head(q_tile, k_part, v_part, do_tile):
        scores = jnp.where(causal, dot(q_tile, k_part, NT), -1e30)
        exp_val = jnp.exp(scores - jnp.max(scores, axis=-N1, keepdims=True))
        prob = exp_val / jnp.sum(exp_val, axis=-N1, keepdims=True)
        d_prob = dot(do_tile, v_part, NT).astype(bf16).astype(f32)
        d_score = prob * (d_prob - jnp.sum(d_prob * prob, axis=-N1, keepdims=True))
        return prob.astype(bf16), d_score.astype(bf16)

    def block(tt, carry):
        tiles = []
        for n in range(N2):
            cols = slice(n * LANES, n * LANES + LANES)
            vals = q_ref[tt, :, cols].astype(f32)
            tiles.append(((vals * cq_ref[ALL] + other(vals) * sq_ref[ALL]) * 0.125).astype(bf16))
        do0 = do_ref[tt, :, N0:LANES]
        do1 = do_ref[tt, :, LANES:PAIR]
        p0, s0 = head(tiles[N0], k_lo, v_hi, do0)
        p1, s1 = head(tiles[N0], k_hi, v_lo, do1)
        p2, s2 = head(tiles[N1], k_lo, v_hi, do1)
        o_out[tt, :, N0:LANES] = dot(p0, v_hi).astype(bf16)
        o_out[tt, :, LANES:PAIR] = (dot(p1, v_lo) + dot(p2, v_hi)).astype(bf16)
        dv_hi[ALL] += dot(p0, do0, TN) + dot(p2, do1, TN)
        dv_lo[ALL] += dot(p1, do1, TN)
        dk_lo[ALL] += dot(s0, tiles[N0], TN) + dot(s2, tiles[N1], TN)
        dk_hi[ALL] += dot(s1, tiles[N0], TN)
        for n, grad in ((N0, dot(s0, k_lo) + dot(s1, k_hi)), (N1, dot(s2, k_lo))):
            grad = grad.astype(bf16).astype(f32) * 0.125
            dq_out[tt, :, n * LANES:n * LANES + LANES] = (grad * cq_ref[ALL] - other(grad) * sq_ref[ALL]).astype(bf16)
        return carry
    lax.fori_loop(N0, q_ref.shape[N0], block, N0)
    dk = (dk_lo[ALL] + pltpu.roll(dk_hi[ALL], 64, N1)).astype(bf16).astype(f32)
    dk_raw = dk * ck_ref[ALL] - other(dk) * sk_ref[ALL]
    dv = dv_hi[ALL] + pltpu.roll(dv_lo[ALL], 64, N1)
    dkv_out[ALL] = jnp.where(low, dk_raw, dv).astype(bf16)


def back_kernel(x_ref, dy_ref, gain_ref, w0_ref, w1_ref, wkv_ref, o_ref, act_ref, dq_ref, dg_ref, du_ref, dkv_ref, y_out, gx_out, gain_out, y_acc, dh_acc):
    f32 = jnp.float32
    bf16 = jnp.bfloat16
    step = pl.program_id(N0)
    tokens = x_ref.shape[N0]
    y_part = dot(o_ref[N0], w0_ref[N0, N0, :, 896:1152], NT) + dot(act_ref[N0, :, N0:LANES], w0_ref[N0, N0, :, 1280:1408], NT) + dot(act_ref[N0, :, LANES:768], w1_ref[N0, N0, :, 768:1408], NT)
    dh_part = dot(dq_ref[N0], w0_ref[N0, N0, :, 768:KIB], NT) + dot(dg_ref[N0], w0_ref[N0, N0, :, N0:768], NT) + dot(du_ref[N0], w1_ref[N0, N0, :, N0:768], NT)

    @pl.when(step == N0)
    def _():
        y_acc[ALL] = y_part
        dh_acc[ALL] = dh_part + dot(dkv_ref[ALL], wkv_ref[ALL], NT)

    @pl.when(step > N0)
    def _():
        y_acc[ALL] += y_part
        dh_acc[ALL] += dh_part

    @pl.when(step == pl.num_programs(N0) - N1)
    def _():
        gain_out[ALL] = jnp.zeros_like(gain_out)

        def finish(n, carry):
            at = pl.ds(n * LANES, LANES)
            x_f32 = x_ref[at, :].astype(f32)
            y_out[at, :] = (x_f32 + y_acc[at, :]).astype(bf16)
            x_cent = x_f32 - jnp.mean(x_f32, axis=-N1, keepdims=True)
            rstd = lax.rsqrt(jnp.mean(x_cent * x_cent, axis=-N1, keepdims=True) + 1e-5)
            x_hat = x_cent * rstd
            dh = dh_acc[at, :].astype(bf16).astype(f32)
            gain_out[ALL] += jnp.sum(dh * x_hat, axis=N0, keepdims=True)
            d_hat = dh * gain_ref[ALL]
            dx = rstd * (d_hat - jnp.mean(d_hat, axis=-N1, keepdims=True) - x_hat * jnp.mean(d_hat * x_hat, axis=-N1, keepdims=True))
            gx_out[at, :] = (dy_ref[at, :].astype(f32) + dx).astype(bf16)
            return carry
        lax.fori_loop(N0, tokens // LANES, finish, N0)


def wgrad_kernel(ht_ref, dyt_ref, gcol_ref, o_ref, act_ref, dq_ref, dg_ref, du_ref, dkv_ref, own_out, oth_out):
    f32 = jnp.float32
    tt = pl.program_id(N0)
    lane = lax.broadcasted_iota(jnp.int32, (LANES, LANES), N1)

    def chunk(n, carry):
        at = pl.ds(n * LANES, LANES)
        for cls, out in ((N0, own_out), (N1, oth_out)):
            ht = ht_ref[cls, at, :]
            dyt = dyt_ref[cls, at, :]
            for k in range(N3):
                cols = slice(k * PAIR, k * PAIR + PAIR)
                out[N0, N0, at, cols] = dot(ht, dg_ref[N0, :, cols]).astype(out.dtype)
                out[N1, N0, at, cols] = dot(ht, du_ref[N0, :, cols]).astype(out.dtype)
            g_q = dot(ht, dq_ref[N0])
            g_o = dot(dyt, o_ref[N0])
            out[N0, N0, at, 768:896] = g_q[:, N0:LANES].astype(out.dtype)
            out[N0, N0, at, 896:KIB] = (g_q[:, LANES:PAIR] + g_o[:, N0:LANES]).astype(out.dtype)
            out[N0, N0, at, KIB:1152] = g_o[:, LANES:PAIR].astype(out.dtype)
            g_kv = pltpu.roll(dot(ht, dkv_ref[ALL]), lax.rem(LANES - 32 * tt, LANES), N1)
            out[N0, N0, at, 1152:1280] = (jnp.where(lane < 32, g_kv, 0.0) + gcol_ref[cls, at, :]).astype(out.dtype)
            out[N0, N0, at, 1280:1408] = dot(dyt, act_ref[N0, :, N0:LANES]).astype(out.dtype)
            for lo, hi in ((LANES, 384), (384, 640), (640, 768)):
                out[N1, N0, at, lo + 640:hi + 640] = dot(dyt, act_ref[N0, :, lo:hi]).astype(out.dtype)
        return carry
    lax.fori_loop(N0, N3, chunk, N0)


def layer_step(x_tok, dy_tok, gain_row, w_full, w_kv, core, seq_len, head_dim):
    f32 = jnp.float32
    bf16 = jnp.bfloat16
    tokens, width = x_tok.shape
    n_tp = w_full.shape[N1]
    wide = w_full.shape[N3]
    n_seq = tokens // seq_len
    half = width // N2

    def whole(shape):
        return pl.BlockSpec(shape, lambda i: (N0,) * len(shape))

    def per(shape):
        return pl.BlockSpec((N1,) + shape, lambda i: (i,) + (N0,) * len(shape))

    w0_spec = pl.BlockSpec((N1, N1, width, wide), lambda i: (N0, i, N0, N0))
    w1_spec = pl.BlockSpec((N1, N1, width, wide), lambda i: (N1, i, N0, N0))
    tok = whole((tokens, width))
    params = pltpu.CompilerParams(dimension_semantics=('arbitrary',), vmem_limit_bytes=56 * KIB * KIB)
    wide_t = jax.ShapeDtypeStruct((n_tp, tokens, width), bf16)
    pair_t = jax.ShapeDtypeStruct((n_tp, tokens, PAIR), bf16)
    row_t = jax.ShapeDtypeStruct((tokens, width), bf16)
    kv_t = jax.ShapeDtypeStruct((tokens, LANES), bf16)
    h_norm, q_raw, kv_raw, d_o, act, d_gate, d_up = pl.pallas_call(
        proj_kernel, name='proj', grid=(n_tp,),
        in_specs=[tok, tok, whole((N1, width)), w0_spec, w1_spec, whole((width, LANES))],
        out_specs=(tok, per((tokens, PAIR)), whole((tokens, LANES)), per((tokens, PAIR)), per((tokens, width)), per((tokens, width)), per((tokens, width))),
        out_shape=(row_t, pair_t, kv_t, pair_t, wide_t, wide_t, wide_t),
        compiler_params=params,
    )(x_tok, dy_tok, gain_row, w_full, w_full, w_kv)

    half_dim = head_dim // N2
    inv_freq = jnp.power(10000.0, -2.0 * jnp.arange(half_dim, dtype=f32) / head_dim)
    angle = jnp.arange(seq_len, dtype=f32)[:, None] * inv_freq[None, :]
    cos_t = jnp.cos(angle)
    sin_t = jnp.sin(angle)
    cos_h = jnp.concatenate([cos_t, cos_t], axis=N1)
    sin_h = jnp.concatenate([-sin_t, sin_t], axis=N1)
    cos_q = jnp.concatenate([cos_h, cos_h], axis=N1)
    sin_q = jnp.concatenate([sin_h, sin_h], axis=N1)
    cos_k = jnp.concatenate([cos_h, jnp.ones_like(cos_h)], axis=N1)
    sin_k = jnp.concatenate([sin_h, jnp.zeros_like(sin_h)], axis=N1)
    pair_spec = pl.BlockSpec((n_tp, seq_len, PAIR), lambda i: (N0, i, N0))
    kv_spec = pl.BlockSpec((seq_len, LANES), lambda i: (i, N0))
    table = whole((seq_len, LANES))
    att, d_q, d_kv = pl.pallas_call(
        att_kernel, name='attention', grid=(n_seq,),
        in_specs=[pair_spec, kv_spec, pair_spec, table, table, table, table],
        out_specs=(pair_spec, pair_spec, kv_spec),
        out_shape=(pair_t, pair_t, kv_t),
        scratch_shapes=[pltpu.VMEM((seq_len, LANES), f32)] * RING,
        compiler_params=params,
    )(q_raw, kv_raw, d_o, cos_q, sin_q, cos_k, sin_k)

    y_tok, gx_tok, gain_part = pl.pallas_call(
        back_kernel, name='back', grid=(n_tp,),
        in_specs=[tok, tok, whole((N1, width)), w0_spec, w1_spec, whole((width, LANES)), per((tokens, PAIR)), per((tokens, width)), per((tokens, PAIR)),
                  per((tokens, width)), per((tokens, width)), whole((tokens, LANES))],
        out_specs=(tok, tok, whole((N1, width))),
        out_shape=(row_t, row_t, jax.ShapeDtypeStruct((N1, width), f32)),
        scratch_shapes=[pltpu.VMEM((tokens, width), f32)] * N2,
        compiler_params=params,
    )(x_tok, dy_tok, gain_row, w_full, w_full, w_kv, att, act, d_q, d_gate, d_up, d_kv)

    def by_class(vals):
        vals = vals.reshape(16, N2, 24, vals.shape[N1])
        mine = lax.dynamic_index_in_dim(vals, core, N1, keepdims=False)
        theirs = lax.dynamic_index_in_dim(vals, N1 - core, N1, keepdims=False)
        return jnp.stack([mine, theirs]).reshape(N2, half, vals.shape[N3])

    h_t = by_class(h_norm.T)
    dy_t = by_class(dy_tok.T)
    gain_col = jnp.where(jnp.arange(LANES)[None, :] == 32, gain_part.reshape(width, N1), 0.0)
    gain_col = by_class(gain_col)
    class_spec = pl.BlockSpec((N2, N1, half, wide), lambda i: (N0, i, N0, N0))
    own, oth = pl.pallas_call(
        wgrad_kernel, name='wgrad', grid=(n_tp,),
        in_specs=[whole((N2, half, tokens)), whole((N2, half, tokens)), whole((N2, half, LANES)), per((tokens, PAIR)), per((tokens, width)), per((tokens, PAIR)),
                  per((tokens, width)), per((tokens, width)), whole((tokens, LANES))],
        out_specs=(class_spec, class_spec),
        out_shape=(jax.ShapeDtypeStruct((N2, n_tp, half, wide), f32), jax.ShapeDtypeStruct((N2, n_tp, half, wide), bf16)),
        compiler_params=params,
    )(h_t, dy_t, gain_col, att, act, d_q, d_gate, d_up, d_kv)
    return y_tok, gx_tok, own, oth


def sum_kernel(g_ref, gs_ref, gx_ref, w_out, kv_out, gx_out, acc, rp, sa, ra1, ra2, sb, rb1, rb2, sc, rc, kvx, gsem, d2s, d2r, ss, rs, cs, cr, ks, kr, xs, xr, lsem):
    f32 = jnp.float32
    bf16 = jnp.bfloat16
    t = lax.axis_index('tp')
    f = lax.axis_index('fsdp')
    c = lax.rem(f, N2)
    yy = lax.rem(lax.div(f, N2), RING)
    zz = lax.div(f, SUB)

    def dev(tt, zc, yc, cc):
        return {'tp': tt, 'fsdp': (zc * RING + yc) * N2 + cc}

    def up(i, d):
        return lax.rem(i + d, RING)

    partner = dev(t, zz, yy, N1 - c)
    xp = [dev(up(t, d), zz, yy, c) for d in range(RING)]
    z_dev = [dev(t, up(zz, d), yy, c) for d in range(RING)]
    y_dev = [dev(t, zz, up(yy, d), c) for d in range(RING)]
    barrier = pltpu.get_barrier_semaphore()
    peers = [partner, xp[N1], xp[N2], xp[N3], z_dev[N1], z_dev[N3], y_dev[N1], y_dev[N3]]
    for peer in peers:
        pl.semaphore_signal(barrier, inc=N1, device_id=peer, device_id_type=MESH_ID)

    def rcopy(src, dst, s_sem, r_sem, peer):
        return pltpu.make_async_remote_copy(src_ref=src, dst_ref=dst, send_sem=s_sem, recv_sem=r_sem, device_id=peer, device_id_type=MESH_ID)

    ring_a = [zz, yy]
    ring_b = [yy, zz]
    dev_a = [z_dev, y_dev]
    dev_b = [y_dev, z_dev]
    order = [N2, N1, N3, N0]

    def g_view(col, j):
        return g_ref.at[N0, :, j] if col == N0 else g_ref.at[N1, :, :, j]

    def gs_view(col, j):
        return gs_ref.at[N0, :, j] if col == N0 else gs_ref.at[N1, :, :, j]

    load = [[None] * RING for _ in range(N2)]
    pair = [[None] * RING for _ in range(N2)]
    for n, d in enumerate(order):
        for col in range(N2):
            j = up(ring_a[col], d)
            load[col][n] = pltpu.make_async_copy(g_view(col, j), acc.at[col, n], gsem.at[col, n])
            load[col][n].start()
    pl.semaphore_wait(barrier, len(peers))
    for n, d in enumerate(order):
        for col in range(N2):
            j = up(ring_a[col], d)
            pair[col][n] = rcopy(gs_view(col, j), rp.at[col, n], d2s.at[col, n], d2r.at[col, n], partner)
            pair[col][n].start()
    mine = gx_ref.shape[N0]
    my_rows = pl.ds(t * mine, mine)
    x_up = rcopy(gx_ref, gx_out.at[my_rows], xs.at[N0], xr.at[N0], xp[N1])
    x_dn = rcopy(gx_ref, gx_out.at[my_rows], xs.at[N1], xr.at[N1], xp[N3])
    x_up.start()
    x_dn.start()
    x_me = pltpu.make_async_copy(gx_ref, gx_out.at[my_rows], lsem.at[N0])
    x_me.start()

    def each(count, body):
        def step(n, carry):
            body(n)
            return carry
        lax.fori_loop(N0, count, step, N0)

    def arrived(col, n):
        load[col][n].wait()
        pair[col][n].wait_recv()

    sends = []

    def send(src, dst, s_sem, r_sem, peer):
        copy = rcopy(src, dst, s_sem, r_sem, peer)
        copy.start()
        sends.append(copy)
        return copy

    for col in range(N2):
        arrived(col, N0)

        def first(q, col=col):
            tt = lax.div(q, 12)
            a2 = lax.rem(lax.div(q, N3), RING)
            r = lax.rem(q, N3)
            sa[col, N0, a2, tt, r] = (acc[col, N0, tt, a2, r] + rp[col, N0, tt, a2, r].astype(f32)).astype(bf16)
        each(48, first)
        send(sa.at[col, N0, pl.ds(N0, N2)], ra1.at[col, N0], ss.at[col, N0], rs.at[col, N0], dev_a[col][N1])
        send(sa.at[col, N0, pl.ds(N2, N2)], ra1.at[col, N1], ss.at[col, N1], rs.at[col, N1], dev_a[col][N3])
    for col in range(N2):
        for n, base, peer in ((N1, N2, N1), (N2, N0, N3)):
            arrived(col, n)

            def plain(q, col=col, n=n, base=base):
                a2 = base + lax.div(q, 12)
                tt = lax.rem(lax.div(q, N3), RING)
                r = lax.rem(q, N3)
                sa[col, n, a2, tt, r] = (acc[col, n, tt, a2, r] + rp[col, n, tt, a2, r].astype(f32)).astype(bf16)
            each(24, plain)
            send(sa.at[col, n, pl.ds(base, N2)], ra2.at[col, n - N1, pl.ds(base, N2)], ss.at[col, n + N1], rs.at[col, n + N1], dev_a[col][peer])
    for col in range(N2):
        for n, base, peer in ((N1, N0, N1), (N2, N2, N3)):
            rcopy(sa.at[col, N0, pl.ds(N0, N2)], ra1.at[col, n - N1], ss.at[col, n - N1], rs.at[col, n - N1], dev_a[col][peer]).wait_recv()

            def joined(q, col=col, n=n, base=base):
                h = lax.div(q, 12)
                a2 = base + h
                tt = lax.rem(lax.div(q, N3), RING)
                r = lax.rem(q, N3)
                val = acc[col, n, tt, a2, r] + rp[col, n, tt, a2, r].astype(f32) + ra1[col, n - N1, h, tt, r].astype(f32)
                sa[col, n, a2, tt, r] = val.astype(bf16)
            each(24, joined)
            send(sa.at[col, n, pl.ds(base, N2)], ra2.at[col, n - N1, pl.ds(base, N2)], ss.at[col, n + N3], rs.at[col, n + N3], dev_a[col][peer])
    x_up.wait_recv()
    x_dn.wait_recv()
    from_dn = up(t, N3) * mine * N2
    from_up = up(t, N1) * mine * N2
    half_dn = gx_out.at[pl.ds(up(t, N3) * mine, mine), pl.ds(N0, LANES)]
    half_up = gx_out.at[pl.ds(up(t, N1) * mine, mine), pl.ds(LANES, LANES)]
    x_up2 = rcopy(half_dn, half_dn, xs.at[N2], xr.at[N2], xp[N1])
    x_dn2 = rcopy(half_up, half_up, xs.at[N3], xr.at[N3], xp[N3])
    x_up2.start()
    x_dn2.start()
    for col in range(N2):
        arrived(col, N3)
        for n, base, s in ((N1, N2, N2), (N2, N0, N3), (N1, N0, RING), (N2, N2, 5)):
            rcopy(sa.at[col, n, pl.ds(base, N2)], ra2.at[col, n - N1, pl.ds(base, N2)], ss.at[col, s], rs.at[col, s], partner).wait_recv()

        def own(q, col=col):
            a2 = lax.div(q, 12)
            tt = lax.rem(lax.div(q, N3), RING)
            r = lax.rem(q, N3)
            val = acc[col, N3, tt, a2, r] + rp[col, N3, tt, a2, r].astype(f32) + ra2[col, N0, a2, tt, r].astype(f32) + ra2[col, N1, a2, tt, r].astype(f32)
            acc[col, N3, tt, a2, r] = val
        each(48, own)
        far = up(ring_b[col], N2)

        def first_b(q, col=col, far=far):
            tt = lax.div(q, N3)
            r = lax.rem(q, N3)
            sb[col, N0, tt, r] = acc[col, N3, tt, far, r].astype(bf16)
        each(12, first_b)
        send(sb.at[col, N0, pl.ds(N0, N2)], rb1.at[col, N0], ss.at[col, 6], rs.at[col, 6], dev_b[col][N1])
        send(sb.at[col, N0, pl.ds(N2, N2)], rb1.at[col, N1], ss.at[col, 7], rs.at[col, 7], dev_b[col][N3])
        for n, base, peer in ((N1, N2, N1), (N2, N0, N3)):
            pos = up(ring_b[col], peer)

            def plain_b(q, col=col, n=n, base=base, pos=pos):
                tt = base + lax.div(q, N3)
                r = lax.rem(q, N3)
                sb[col, n, tt, r] = acc[col, N3, tt, pos, r].astype(bf16)
            each(6, plain_b)
            send(sb.at[col, n, pl.ds(base, N2)], rb2.at[col, n - N1, pl.ds(base, N2)], ss.at[col, n + 7], rs.at[col, n + 7], dev_b[col][peer])
    for col in range(N2):
        for n, base, peer in ((N1, N0, N1), (N2, N2, N3)):
            rcopy(sb.at[col, N0, pl.ds(N0, N2)], rb1.at[col, n - N1], ss.at[col, n + 5], rs.at[col, n + 5], partner).wait_recv()
            pos = up(ring_b[col], peer)

            def joined_b(q, col=col, n=n, base=base, pos=pos):
                h = lax.div(q, N3)
                tt = base + h
                r = lax.rem(q, N3)
                sb[col, n, tt, r] = (acc[col, N3, tt, pos, r] + rb1[col, n - N1, h, r].astype(f32)).astype(bf16)
            each(6, joined_b)
            send(sb.at[col, n, pl.ds(base, N2)], rb2.at[col, n - N1, pl.ds(base, N2)], ss.at[col, n + 9], rs.at[col, n + 9], dev_b[col][peer])
    for col in range(N2):
        here = ring_b[col]
        for n, base, s in ((N1, N2, SUB), (N2, N0, 9), (N1, N0, 10), (N2, N2, 11)):
            rcopy(sb.at[col, n, pl.ds(base, N2)], rb2.at[col, n - N1, pl.ds(base, N2)], ss.at[col, s], rs.at[col, s], partner).wait_recv()

        def own_b(q, col=col, here=here):
            tt = lax.div(q, N3)
            r = lax.rem(q, N3)
            val = acc[col, N3, tt, here, r] + rb2[col, N0, tt, r].astype(f32) + rb2[col, N1, tt, r].astype(f32)
            acc[col, N3, tt, here, r] = val
            sc[col, tt, r] = val.astype(bf16)
        each(12, own_b)
        for d in (N1, N3, N2):
            to = up(t, d)
            send(sc.at[col, to], rc.at[col, d - N1], cs.at[col, d - N1], cr.at[col, d - N1], xp[d])
        if col == N0:
            def kv_part(q, here=here):
                tt = lax.div(q, N3)
                r = lax.rem(q, N3)
                kvx[t, tt, r] = acc[N0, N3, tt, here, r, :, pl.ds(KV_AT, LANES)]
            each(12, kv_part)
            for d in (N1, N3, N2):
                send(kvx.at[t], kvx.at[t], ks.at[d - N1], kr.at[d - N1], xp[d])
    for col in range(N2):
        here = ring_b[col]
        for d in (N1, N3, N2):
            rcopy(sc.at[col, N0], rc.at[col, d - N1], cs.at[col, d - N1], cr.at[col, d - N1], partner).wait_recv()

        def last(r, col=col, here=here):
            w_out[col, r] = acc[col, N3, t, here, r] + rc[col, N0, r].astype(f32) + rc[col, N1, r].astype(f32) + rc[col, N2, r].astype(f32)
        each(N3, last)
    for d in (N1, N3, N2):
        src = up(t, RING - d)
        rcopy(kvx.at[src], kvx.at[src], ks.at[d - N1], kr.at[d - N1], partner).wait_recv()

    def kv_last(q):
        tt = lax.div(q, N3)
        r = lax.rem(q, N3)
        kv_out[tt, r] = ((kvx[N0, tt, r] + kvx[N1, tt, r]) + kvx[N2, tt, r]) + kvx[N3, tt, r]
    each(12, kv_last)
    for copy in sends:
        copy.wait_send()
    for col in range(N2):
        for n in range(RING):
            pair[col][n].wait_send()
    x_me.wait()
    x_up.wait_send()
    x_dn.wait_send()
    x_up2.wait()
    x_dn2.wait()


def sum_grads(g_pack, g_send, gx_my, n_batch):
    f32 = jnp.float32
    bf16 = jnp.bfloat16
    wide = g_pack.shape[-N1]
    dma = pltpu.SemaphoreType.DMA
    vmem = pl.BlockSpec(memory_space=pltpu.VMEM)
    any_spec = pl.BlockSpec(memory_space=pl.ANY)
    return pl.pallas_call(
        sum_kernel,
        name='sum_grads',
        out_shape=(jax.ShapeDtypeStruct((N2, N3, SUB, wide), f32), jax.ShapeDtypeStruct((RING, N3, SUB, LANES), f32),
                   jax.ShapeDtypeStruct((n_batch,) + gx_my.shape[N1:], bf16)),
        in_specs=[any_spec, any_spec, any_spec],
        out_specs=(vmem, vmem, any_spec),
        scratch_shapes=[
            pltpu.VMEM((N2, RING, RING, RING, N3, SUB, wide), f32), pltpu.VMEM((N2, RING, RING, RING, N3, SUB, wide), bf16),
            pltpu.VMEM((N2, N3, RING, RING, N3, SUB, wide), bf16), pltpu.VMEM((N2, N2, N2, RING, N3, SUB, wide), bf16), pltpu.VMEM((N2, N2, RING, RING, N3, SUB, wide), bf16),
            pltpu.VMEM((N2, N3, RING, N3, SUB, wide), bf16), pltpu.VMEM((N2, N2, N2, N3, SUB, wide), bf16), pltpu.VMEM((N2, N2, RING, N3, SUB, wide), bf16),
            pltpu.VMEM((N2, RING, N3, SUB, wide), bf16), pltpu.VMEM((N2, N3, N3, SUB, wide), bf16), pltpu.VMEM((RING, RING, N3, SUB, LANES), f32),
            dma((N2, RING)), dma((N2, RING)), dma((N2, RING)), dma((N2, 12)), dma((N2, 12)), dma((N2, N3)), dma((N2, N3)), dma((N3,)), dma((N3,)), dma((RING,)), dma((RING,)), dma((N1,)),
        ],
        compiler_params=pltpu.CompilerParams(collective_id=N1, has_side_effects=True, vmem_limit_bytes=60 * KIB * KIB),
    )(g_pack, g_send, gx_my)


def solution(mesh):
    n_tp = mesh.shape['tp']
    n_fsdp = mesh.shape['fsdp']

    def device_step(x_in, dy_out, ln_gain, w_q, w_k, w_v, w_o, w_gate, w_up, w_down):
        bf16 = jnp.bfloat16
        f32 = jnp.float32
        n_batch, seq_len, width = x_in.shape
        head_dim = w_k.shape[N1]
        rows = w_q.shape[N0]
        nq = w_q.shape[N1]
        nf = w_gate.shape[N1]
        part = N2 * head_dim // n_tp
        mine = n_batch // n_tp
        tokens = mine * seq_len
        tp = lax.axis_index('tp')
        core = lax.rem(lax.axis_index('fsdp'), N2)
        gain_hi = lax.reduce_precision(ln_gain, SUB, 7)
        gain_mid = lax.reduce_precision(ln_gain - gain_hi, SUB, 7)
        gain_lo = ln_gain - gain_hi - gain_mid
        gain_cols = jnp.stack([gain_hi, gain_mid, gain_lo], axis=N1).astype(bf16)
        kv_mine = lax.dynamic_slice_in_dim(jnp.concatenate([w_k, w_v], axis=N1), tp * part, part, N1)
        small = jnp.concatenate([kv_mine, gain_cols, jnp.zeros((rows, LANES - part - N3), bf16)], axis=N1)
        down = w_down.T
        packed = jnp.stack([jnp.concatenate([w_gate, w_q, w_o.T, small, down[:, :LANES]], axis=N1), jnp.concatenate([w_up, down[:, LANES:]], axis=N1)])
        wide = packed.shape[N2]
        full = gather_weights(packed).reshape(N2, n_tp, width, wide)
        small_full = full[N0, :, :, KV_AT:KV_AT + LANES]
        w_kv = jnp.concatenate([small_full[n, :, :part] for n in range(n_tp)], axis=N1)
        gain3 = small_full[N0, :, part:part + N3].astype(f32)
        gain_row = (gain3[:, N0] + gain3[:, N1] + gain3[:, N2]).reshape(N1, width)

        x_tok = lax.dynamic_slice_in_dim(x_in, tp * mine, mine, N0).reshape(tokens, width)
        dy_tok = lax.dynamic_slice_in_dim(dy_out, tp * mine, mine, N0).reshape(tokens, width)
        y_tok, gx_tok, g_own, g_oth = layer_step(x_tok, dy_tok, gain_row, full, w_kv, core, seq_len, head_dim)
        y_out = lax.all_gather(y_tok.reshape(mine, seq_len, width), 'tp', axis=N0, tiled=True)
        split = (N2, n_tp, RING, RING, N3, SUB, wide)
        w_sum, kv_sum, grad_x = sum_grads(g_own.reshape(split), g_oth.reshape(split), gx_tok.reshape(mine, seq_len, width), n_batch)
        w0 = w_sum[N0].reshape(rows, wide)
        w1 = w_sum[N1].reshape(rows, wide)
        kv_all = jnp.swapaxes(kv_sum.reshape(n_tp, rows, LANES)[:, :, :part], N0, N1).reshape(rows, N2 * head_dim)
        grad_wgate = w0[:, :nf]
        grad_wq = w0[:, nf:nf + nq]
        grad_wo = w0[:, nf + nq:nf + N2 * nq].T
        grad_wdown = jnp.concatenate([w0[:, wide - LANES:], w1[:, nf:]], axis=N1).T
        grad_wup = w1[:, :nf]
        grad_wk = kv_all[:, :head_dim]
        grad_wv = kv_all[:, head_dim:]
        grad_gain = kv_sum[N0].reshape(rows, LANES)[:, part]
        return (y_out, grad_x, grad_gain, grad_wq, grad_wk, grad_wv, grad_wo, grad_wgate, grad_wup, grad_wdown)

    act_spec = P('fsdp', None, None)
    row_spec = P('fsdp', 'tp')
    kv_spec = P('fsdp', None)
    col_spec = P('tp', 'fsdp')
    in_specs = (act_spec, act_spec, P('fsdp'), row_spec, kv_spec, kv_spec, col_spec, row_spec, row_spec, col_spec)
    out_specs = (act_spec, act_spec, P('fsdp'), row_spec, kv_spec, kv_spec, col_spec, row_spec, row_spec, col_spec)
    return jax.shard_map(device_step, mesh=mesh, in_specs=in_specs, out_specs=out_specs, check_vma=False)
```

time: 1060 us -> 270 us (0.25)
  waiting for transfers between devices: 537 us -> 0.02 us
  blocking collectives: 291 us -> 0 us
  Pallas kernels: 0 us -> 218 us
  matrix products: 173 us -> 0 us
  local copies, waits for them, and re-layouts: 5.4 us -> 27.6 us
  other arithmetic: 29.1 us -> 10.1 us
    reduce_scatter x5 -> x0, waiting for transfers between devices: 411 us -> none  [the longest x3 247 us: scatter_rows(): return lax.psum_scatter(grad_full, 'fsdp', scatter_dimension=0, tiled=True)]
    pallas_call x0 -> x6, Pallas kernels: none -> 218 us  [the longest x1 69.8 us: sum_grads(): pl.pallas_call(sum_kernel, name='sum_grads', out_shape=(jax.ShapeDtypeStr...]
    dot_general x26 -> x0, matrix products: 165 us -> none  [the longest x21 139 us: matmul_f32(): return jnp.einsum(form, left, right, preferred_element_type=jnp.float32)]
    unnamed x2 -> x0, blocking collectives: 136 us -> none
    all_gather x4 -> x0, blocking collectives: 93.1 us -> none  [the longest x3 68.4 us: gather_rows(): return lax.all_gather(w_part, 'fsdp', axis=0, tiled=True)]
    psum x1 -> x0, waiting for transfers between devices: 65.2 us -> none  [device_step(): branch_sum = lax.psum(branch_part, 'tp')]
    psum x1 -> x0, blocking collectives: 61.8 us -> none  [device_step(): lax.psum(jnp.concatenate([dk_part, dv_part], axis=-1).astype(jnp.float32)...]
    unnamed x13 -> x1, waiting for transfers between devices: 59.9 us -> 0.02 us
  transfers between devices with their start and end apart: 11 -> 1, of which waited for: 7 -> 0; matrix products, arithmetic and copies ran while one was open for 16% -> 5% of each run, Pallas kernels for 0% -> 35%
where the time goes in v2:
time: 270 us
  Pallas kernels  218 us (81%)
  local copies, waits for them, and re-layouts  27.6 us (10%)
  between operations  14.2 us (5%)
  other arithmetic  10.1 us (4%)
    pallas_call x1, Pallas kernels, sum_grads(): pl.pallas_call(sum_kernel, name='sum_grads', out_shape=(jax.ShapeDtypeStr...  69.8 us
    pallas_call x1, Pallas kernels, gather_weights(): pl.pallas_call(gather_kernel, name='gather_weights', out_shape=jax.ShapeD...  52.6 us
    pallas_call x1, Pallas kernels, layer_step(): pl.pallas_call(back_kernel, name='back', grid=(n_tp,), in_specs=[tok, tok...  26.8 us
    pallas_call x1, Pallas kernels, layer_step(): pl.pallas_call(wgrad_kernel, name='wgrad', grid=(n_tp,), in_specs=[whole(...  25 us
    pallas_call x1, Pallas kernels, layer_step(): pl.pallas_call(proj_kernel, name='proj', grid=(n_tp,), in_specs=[tok, tok...  23.6 us
    pallas_call x1, Pallas kernels, layer_step(): pl.pallas_call(att_kernel, name='attention', grid=(n_seq,), in_specs=[pai...  19.8 us
    unnamed x13, local copies, waits for them, and re-layouts  14 us
  transfers between devices with their start and end apart: 1, of which 0 were waited for; matrix products, arithmetic and copies ran while one was open for 5% of the time, Pallas kernels for 35%

profile of v2, /device:TPU:0, one launch (start us, length us, event | category | flops | bytes accessed | tf_op | source)
XLA Modules:
  0.0 269.6 jit_solution(1018043709949887804)
XLA Ops:
  7.2 0.7 slice.96
  7.9 0.8 slice.97
  8.7 0.7 fusion.10
  9.6 0.8 maximum_bitcast_fusion.1
  10.4 0.8 dynamic-slice_maximum_fusion
  11.2 0.9 concatenate.39
  12.1 52.6 %gather_weights.1 = bf16[2,4,4,4,2,3,8,1408]{7,6,5,4,3,2,1,0:T(8,128)(2,1)S(1)} custom-call(bf16[2,3,8,1408]{3,2,1,0:T(8,128)(2,1)S(1)} %pad_maximum_fusion.4.p_ref), custom_call_target="tpu_custom_call" | custom-call | tf_op jit(solution)/shard_map/gather_weights/pallas_call | solution.py:121
  64.7 5.9 %copy-done = bf16[2,4,4,4,2,3,8,1408]{7,6,5,4,3,2,1,0:T(8,128)(2,1)} copy-done((bf16[2,4,4,4,2,3,8,1408]{7,6,5,4,3,2,1,0:T(8,128)(2,1)}, bf16[2,4,4,4,2,3,8,1408]{7,6,5,4,3,2,1,0:T(8,128)(2,1)S(1)}, u32[]{:S(2)}) %copy-start) | copy-done | bytes 17301528
  72.6 3.2 %constant_dynamic-slice_fusion.6 = (bf16[3,256,768]{2,1,0:T(8,128)(2,1)}, bf16[3,256,768]{2,1,0:T(8,128)(2,1)}) fusion(bf16[12,256,768]{2,1,0:T(8,128)(2,1)} %param.11, s32[]{:T(128)S(6)} %select_n.24, bf16[12,256,768]{2,1,0:T(8,128)(2,1)} %param.10), kind=kLoop, calls=%fused_computation.40 | loop fusion | bytes 4718596 | tf_op jit(solution)/shard_map/dynamic_slice | solution.py:665
  75.8 0.9 pad_maximum_fusion.3.wkv_ref
  76.8 23.6 %proj.1 = (bf16[768,768]{1,0:T(8,128)(2,1)}, bf16[4,768,256]{2,1,0:T(8,128)(2,1)}, bf16[768,128]{1,0:T(8,128)(2,1)}, bf16[4,768,256]{2,1,0:T(8,128)(2,1)}, bf16[...) custom-call(bf16[768,768]{1,0:T(8,128)(2,1)} %bitcast.67, ...), custom_call_target="tpu_custom_call" | custom-call | tf_op jit(solution)/shard_map/proj/pallas_call | solution.py:326
  100.3 1.0 fusion.2
  101.4 19.8 %attention.1 = (bf16[4,768,256]{2,1,0:T(8,128)(2,1)}, bf16[4,768,256]{2,1,0:T(8,128)(2,1)}, bf16[768,128]{1,0:T(8,128)(2,1)}) custom-call(bf16[4,768,256]{2,1,0:T(8,128)(2,1)} %get-tuple-element.28.q_ref, bf16[768,128]{1,0:T(8,128)(2,1)} %get-tuple-element.29.kv_ref, bf16[4,768,256]{2,1,0:T(8,128)(2,1)} %get-tuple-element.30.do_ref, ...), custom_call_target="tpu_custom_call" | custom-call | tf_op jit(solution)/shard_map/attention/pallas_call | solution.py:348
  121.2 26.8 %back.1 = (bf16[768,768]{1,0:T(8,128)(2,1)}, bf16[768,768]{1,0:T(8,128)(2,1)}, f32[1,768]{1,0:T(1,128)}) custom-call(bf16[768,768]{1,0:T(8,128)(2,1)} %bitcast.68, bf16[768,768]{1,0:T(8,128)(2,1)} %bitcast.64, f32[1,768]{1,0:T(1,128)} %add.48.gain_ref, bf16[2,4,768,1408]{3,2,1,0:T(8,128)(2,1)} %bitcast.61, bf16[2,4,768,1408]{3,2,1,0:T(8,128)(2,1)} %bitcast.62, ...), custom_call_target="tpu_custom_call" | custom-call | tf_op jit(solution)/shard_map/back/pallas_call | solution.py:357
  148.1 0.8 reduce.1
  149.3 0.6 copy.41
  150.0 0.6 copy.42
  150.9 0.8 pad_maximum_fusion.2.gcol_ref
  151.8 1.2 pad_maximum_fusion.ht_ref
  153.0 1.1 pad_maximum_fusion.1.dyt_ref
  154.2 25.0 %wgrad.1 = (f32[2,4,384,1408]{3,2,1,0:T(8,128)}, bf16[2,4,384,1408]{3,2,1,0:T(8,128)(2,1)}) custom-call(bf16[2,384,768]{2,1,0:T(8,128)(2,1)} %pad_maximum_fusion.ht_ref, bf16[2,384,768]{2,1,0:T(8,128)(2,1)} %pad_maximum_fusion.1.dyt_ref, f32[2,384,128]{2,1,0:T(8,128)} %pad_maximum_fusion.2.gcol_ref, bf16[4,768,256]{2,1,0:T(8,128)(2,1)} %get-tuple-element.31.o_ref, ...), custom_call_target="tpu_custom_call" | custom-call | tf_op jit(solution)/shard_map/wgrad/pallas_call | solution.py:378
  179.1 69.8 %sum_grads.1 = (f32[2,3,8,1408]{3,2,1,0:T(8,128)}, f32[4,3,8,128]{3,2,1,0:T(8,128)}, bf16[12,256,768]{2,1,0:T(8,128)(2,1)}) custom-call(f32[2,4,4,4,3,8,1408]{6,5,4,3,2,1,0:T(8,128)} %bitcast.66, bf16[2,4,4,4,3,8,1408]{6,5,4,3,2,1,0:T(8,128)(2,1)} %bitcast.69, bf16[3,256,768]{2,1,0:T(8,128)(2,1)} %bitcast.78), custom_call_target="tpu_custom_call" | custom-call | tf_op jit(solution)/shard_map/sum_grads/pallas_call | solution.py:614
  249.0 1.0 slice_bitcast_fusion.6
  250.0 0.6 slice.113
  250.6 0.6 slice.114
  251.3 0.8 slice_bitcast_fusion.8
  252.2 0.7 slice_bitcast_fusion.10
  253.6 0.6 maximum_bitcast_fusion
  254.2 0.7 fusion.11
  254.9 0.7 slice_bitcast_fusion.9
  255.6 5.0 %copy.49 = bf16[12,256,768]{2,1,0:T(8,128)(2,1)} copy(bf16[12,256,768]{2,1,0:T(8,128)(2,1)} %all-gather.2.cloned.1.call-done) | data formatting | bytes 9437184
  260.6 2.2 copy.50
  (42 shorter events, 3.9 us)
Async XLA Ops:
  7.2 248.4 %all-gather.2.cloned.1.call-start = ((), (), s32[]{:S(2)}) async-start(), calls=%async_computation | async-start | bytes 5898240 | tf_op jit(solution)/shard_map/all_gather | solution.py:667
  64.7 5.9 %copy-start = (bf16[2,4,4,4,2,3,8,1408]{7,6,5,4,3,2,1,0:T(8,128)(2,1)}, bf16[2,4,4,4,2,3,8,1408]{7,6,5,4,3,2,1,0:T(8,128)(2,1)S(1)}, u32[]{:S(2)}) copy-start(bf16[2,4,4,4,2,3,8,1408]{7,6,5,4,3,2,1,0:T(8,128)(2,1)S(1)} %gather_weights.1) | copy-start | bytes 51904516
  148.0 1.3 copy-start.2
  148.0 1.9 copy-start.1
  254.2 6.3 %slice-start = ((s8[4718592]{0:T(1024)(128)(4,1)}), s8[524288]{0:T(1024)(128)(4,1)S(1)}, s32[]{:S(2)}) async-start(s8[4718592]{0:T(1024)(128)(4,1)} %bitcast.70), calls=%async_computation.1 | async-start | bytes 1048576
  255.6 5.0 %slice-start.1 = ((s8[4718592]{0:T(1024)(128)(4,1)}), s8[4194304]{0:T(1024)(128)(4,1)S(1)}, s32[]{:S(2)}) async-start(s8[4718592]{0:T(1024)(128)(4,1)} %bitcast.70), calls=%async_computation.2 | async-start | bytes 8388608
Sparse Core Ops, SparseCore 0:
  148.2 63.4 all-gather.1

commit v3 on v2

--- a/solution.py
+++ b/solution.py
@@ -125,7 +125,7 @@
         in_specs=[any_spec],
         out_specs=any_spec,
         scratch_shapes=[dma((N1,)), dma((N3, N3)), dma((N3, N3)), dma((N3, 6)), dma((N3, 6)), dma((N3, 6)), dma((N3, 6)), dma((N3, 14)), dma((N3, 14))],
-        compiler_params=pltpu.CompilerParams(collective_id=N2, has_side_effects=True, vmem_limit_bytes=32 * KIB * KIB),
+        compiler_params=pltpu.CompilerParams(collective_id=N2, has_side_effects=True, vmem_limit_bytes=60 * KIB * KIB),
     )(packed.reshape(N2, N3, SUB, wide))
 
 
@@ -138,21 +138,29 @@
     return lax.dot_general(left, right, dims, preferred_element_type=jnp.float32)
 
 
-def proj_kernel(x_ref, dy_ref, gain_ref, w0_ref, w1_ref, wkv_ref, h_out, q_out, kv_out, do_out, act_out, dg_out, du_out):
+def by_class(out, cols, vals, core):
+    for n in range(32):
+        out[lax.rem(n % N2 + core, N2), 24 * (n // N2):24 * (n // N2) + 24, cols] = vals[24 * n:24 * n + 24]
+
+
+def proj_kernel(who_ref, x_ref, dy_ref, gain_ref, w0_ref, w1_ref, wkv_ref, ht_out, dyt_out, q_out, kv_out, do_out, act_out, dg_out, du_out, h_out):
     f32 = jnp.float32
     bf16 = jnp.bfloat16
-    tokens = x_ref.shape[N0]
+    tokens, width = h_out.shape
+    dy_tok = dy_ref[ALL].reshape(tokens, width)
 
     @pl.when(pl.program_id(N0) == N0)
     def _():
-        def norm(n, carry):
-            at = pl.ds(n * LANES, LANES)
-            x_f32 = x_ref[at, :].astype(f32)
+        for n in range(tokens // LANES):
+            at = slice(n * LANES, n * LANES + LANES)
+            seq, row = divmod(n * LANES, x_ref.shape[N1])
+            x_f32 = x_ref[seq, row:row + LANES, :].astype(f32)
             x_cent = x_f32 - jnp.mean(x_f32, axis=-N1, keepdims=True)
             x_var = jnp.mean(x_cent * x_cent, axis=-N1, keepdims=True)
-            h_out[at, :] = (x_cent * lax.rsqrt(x_var + 1e-5) * gain_ref[ALL]).astype(bf16)
-            return carry
-        lax.fori_loop(N0, tokens // LANES, norm, N0)
+            h_norm = (x_cent * lax.rsqrt(x_var + 1e-5) * gain_ref[ALL]).astype(bf16)
+            h_out[at, :] = h_norm
+            by_class(ht_out, at, h_norm.astype(f32).T.astype(bf16), who_ref[N1])
+            by_class(dyt_out, at, dy_ref[seq, row:row + LANES, :].astype(f32).T.astype(bf16), who_ref[N1])
         kv_out[ALL] = dot(h_out[ALL], wkv_ref[ALL]).astype(bf16)
 
     for n in range(N3):
@@ -160,18 +168,18 @@
         gate = dot(h_out[ALL], w0_ref[N0, N0, :, cols]).astype(bf16).astype(f32)
         up = dot(h_out[ALL], w1_ref[N0, N0, :, cols]).astype(bf16).astype(f32)
         if n == N0:
-            d_low = dot(dy_ref[ALL], w0_ref[N0, N0, :, 1280:1408])
-            d_act = jnp.concatenate([d_low, dot(dy_ref[ALL], w1_ref[N0, N0, :, 768:896])], axis=N1)
+            d_low = dot(dy_tok, w0_ref[N0, N0, :, 1280:1408])
+            d_act = jnp.concatenate([d_low, dot(dy_tok, w1_ref[N0, N0, :, 768:896])], axis=N1)
         else:
-            d_act = dot(dy_ref[ALL], w1_ref[N0, N0, :, 640 + n * PAIR:896 + n * PAIR])
+            d_act = dot(dy_tok, w1_ref[N0, N0, :, 640 + n * PAIR:896 + n * PAIR])
         d_act = d_act.astype(bf16).astype(f32)
-        sig = jax.nn.sigmoid(gate)
+        sig = 0.5 * jnp.tanh(0.5 * gate) + 0.5
         silu = gate * sig
         act_out[N0, :, cols] = (silu * up).astype(bf16)
         du_out[N0, :, cols] = (d_act * silu).astype(bf16)
-        dg_out[N0, :, cols] = (d_act * up * (sig * (1.0 + gate * (1.0 - sig)))).astype(bf16)
+        dg_out[N0, :, cols] = (d_act * up * (sig + silu * (1.0 - sig))).astype(bf16)
     q_out[N0] = dot(h_out[ALL], w0_ref[N0, N0, :, 768:KIB]).astype(bf16)
-    do_out[N0] = dot(dy_ref[ALL], w0_ref[N0, N0, :, 896:1152]).astype(bf16)
+    do_out[N0] = dot(dy_tok, w0_ref[N0, N0, :, 896:1152]).astype(bf16)
 
 
 def att_kernel(q_ref, kv_ref, do_ref, cq_ref, sq_ref, ck_ref, sk_ref, o_out, dq_out, dkv_out, dk_lo, dk_hi, dv_lo, dv_hi):
@@ -201,7 +209,7 @@
     def head(q_tile, k_part, v_part, do_tile):
         scores = jnp.where(causal, dot(q_tile, k_part, NT), -1e30)
         exp_val = jnp.exp(scores - jnp.max(scores, axis=-N1, keepdims=True))
-        prob = exp_val / jnp.sum(exp_val, axis=-N1, keepdims=True)
+        prob = exp_val * (1.0 / jnp.sum(exp_val, axis=-N1, keepdims=True))
         d_prob = dot(do_tile, v_part, NT).astype(bf16).astype(f32)
         d_score = prob * (d_prob - jnp.sum(d_prob * prob, axis=-N1, keepdims=True))
         return prob.astype(bf16), d_score.astype(bf16)
@@ -234,13 +242,17 @@
     dkv_out[ALL] = jnp.where(low, dk_raw, dv).astype(bf16)
 
 
-def back_kernel(x_ref, dy_ref, gain_ref, w0_ref, w1_ref, wkv_ref, o_ref, act_ref, dq_ref, dg_ref, du_ref, dkv_ref, y_out, gx_out, gain_out, y_acc, dh_acc):
+def back_kernel(who_ref, x_ref, dy_ref, gain_ref, w0_ref, w1_ref, wkv_ref, o_ref, act_ref, dq_ref, dg_ref, du_ref, dkv_ref, y_out, gx_out, gcol_out, y_acc, dh_acc):
     f32 = jnp.float32
     bf16 = jnp.bfloat16
     step = pl.program_id(N0)
-    tokens = x_ref.shape[N0]
-    y_part = dot(o_ref[N0], w0_ref[N0, N0, :, 896:1152], NT) + dot(act_ref[N0, :, N0:LANES], w0_ref[N0, N0, :, 1280:1408], NT) + dot(act_ref[N0, :, LANES:768], w1_ref[N0, N0, :, 768:1408], NT)
-    dh_part = dot(dq_ref[N0], w0_ref[N0, N0, :, 768:KIB], NT) + dot(dg_ref[N0], w0_ref[N0, N0, :, N0:768], NT) + dot(du_ref[N0], w1_ref[N0, N0, :, N0:768], NT)
+    tokens, width = y_acc.shape
+    y_left = jnp.concatenate([o_ref[N0], act_ref[N0]], axis=N1)
+    y_right = jnp.concatenate([w0_ref[N0, N0, :, 896:1152], w0_ref[N0, N0, :, 1280:1408], w1_ref[N0, N0, :, 768:1408]], axis=N1)
+    h_left = jnp.concatenate([dg_ref[N0], dq_ref[N0], du_ref[N0]], axis=N1)
+    h_right = jnp.concatenate([w0_ref[N0, N0, :, N0:KIB], w1_ref[N0, N0, :, N0:768]], axis=N1)
+    y_part = dot(y_left, y_right, NT)
+    dh_part = dot(h_left, h_right, NT)
 
     @pl.when(step == N0)
     def _():
@@ -254,83 +266,131 @@
 
     @pl.when(step == pl.num_programs(N0) - N1)
     def _():
-        gain_out[ALL] = jnp.zeros_like(gain_out)
-
-        def finish(n, carry):
-            at = pl.ds(n * LANES, LANES)
-            x_f32 = x_ref[at, :].astype(f32)
+        gain = jnp.zeros((N1, width), f32)
+        for n in range(tokens // LANES):
+            at = slice(n * LANES, n * LANES + LANES)
+            seq, row = divmod(n * LANES, x_ref.shape[N1])
+            x_f32 = x_ref[seq, row:row + LANES, :].astype(f32)
             y_out[at, :] = (x_f32 + y_acc[at, :]).astype(bf16)
             x_cent = x_f32 - jnp.mean(x_f32, axis=-N1, keepdims=True)
             rstd = lax.rsqrt(jnp.mean(x_cent * x_cent, axis=-N1, keepdims=True) + 1e-5)
             x_hat = x_cent * rstd
             dh = dh_acc[at, :].astype(bf16).astype(f32)
-            gain_out[ALL] += jnp.sum(dh * x_hat, axis=N0, keepdims=True)
+            gain += jnp.sum(dh * x_hat, axis=N0, keepdims=True)
             d_hat = dh * gain_ref[ALL]
             dx = rstd * (d_hat - jnp.mean(d_hat, axis=-N1, keepdims=True) - x_hat * jnp.mean(d_hat * x_hat, axis=-N1, keepdims=True))
-            gx_out[at, :] = (dy_ref[at, :].astype(f32) + dx).astype(bf16)
-            return carry
-        lax.fori_loop(N0, tokens // LANES, finish, N0)
+            gx_out[at, :] = (dy_ref[seq, row:row + LANES, :].astype(f32) + dx).astype(bf16)
+        lane = lax.broadcasted_iota(jnp.int32, (width, LANES), N1)
+        by_class(gcol_out, slice(None), jnp.where(lane == 32, jnp.broadcast_to(gain, (LANES, width)).T, 0.0), who_ref[N1])
 
 
 def wgrad_kernel(ht_ref, dyt_ref, gcol_ref, o_ref, act_ref, dq_ref, dg_ref, du_ref, dkv_ref, own_out, oth_out):
-    f32 = jnp.float32
     tt = pl.program_id(N0)
-    lane = lax.broadcasted_iota(jnp.int32, (LANES, LANES), N1)
-
-    def chunk(n, carry):
-        at = pl.ds(n * LANES, LANES)
-        for cls, out in ((N0, own_out), (N1, oth_out)):
-            ht = ht_ref[cls, at, :]
-            dyt = dyt_ref[cls, at, :]
-            for k in range(N3):
-                cols = slice(k * PAIR, k * PAIR + PAIR)
-                out[N0, N0, at, cols] = dot(ht, dg_ref[N0, :, cols]).astype(out.dtype)
-                out[N1, N0, at, cols] = dot(ht, du_ref[N0, :, cols]).astype(out.dtype)
-            g_q = dot(ht, dq_ref[N0])
-            g_o = dot(dyt, o_ref[N0])
-            out[N0, N0, at, 768:896] = g_q[:, N0:LANES].astype(out.dtype)
-            out[N0, N0, at, 896:KIB] = (g_q[:, LANES:PAIR] + g_o[:, N0:LANES]).astype(out.dtype)
-            out[N0, N0, at, KIB:1152] = g_o[:, LANES:PAIR].astype(out.dtype)
-            g_kv = pltpu.roll(dot(ht, dkv_ref[ALL]), lax.rem(LANES - 32 * tt, LANES), N1)
-            out[N0, N0, at, 1152:1280] = (jnp.where(lane < 32, g_kv, 0.0) + gcol_ref[cls, at, :]).astype(out.dtype)
-            out[N0, N0, at, 1280:1408] = dot(dyt, act_ref[N0, :, N0:LANES]).astype(out.dtype)
-            for lo, hi in ((LANES, 384), (384, 640), (640, 768)):
-                out[N1, N0, at, lo + 640:hi + 640] = dot(dyt, act_ref[N0, :, lo:hi]).astype(out.dtype)
-        return carry
-    lax.fori_loop(N0, N3, chunk, N0)
-
-
-def layer_step(x_tok, dy_tok, gain_row, w_full, w_kv, core, seq_len, head_dim):
+    half = ht_ref.shape[N1]
+    lane = lax.broadcasted_iota(jnp.int32, (half, LANES), N1)
+    ht = ht_ref[ALL].reshape(N2 * half, ht_ref.shape[N2])
+    dyt = dyt_ref[ALL].reshape(N2 * half, dyt_ref.shape[N2])
+
+    def put(n, cols, vals):
+        own_out[n, N0, :, cols] = vals[:half]
+        oth_out[n, N0, :, cols] = vals[half:].astype(jnp.bfloat16)
+
+    for k in range(N3):
+        cols = slice(k * PAIR, k * PAIR + PAIR)
+        put(N0, cols, dot(ht, dg_ref[N0, :, cols]))
+        put(N1, cols, dot(ht, du_ref[N0, :, cols]))
+    g_q = dot(ht, dq_ref[N0])
+    g_o = dot(dyt, o_ref[N0])
+    put(N0, slice(768, 896), g_q[:, N0:LANES])
+    put(N0, slice(896, KIB), g_q[:, LANES:PAIR] + g_o[:, N0:LANES])
+    put(N0, slice(KIB, 1152), g_o[:, LANES:PAIR])
+    g_kv = dot(ht, dkv_ref[ALL])
+    for cls, out in ((N0, own_out), (N1, oth_out)):
+        part = pltpu.roll(g_kv[cls * half:cls * half + half], lax.rem(LANES - 32 * tt, LANES), N1)
+        out[N0, N0, :, 1152:1280] = (jnp.where(lane < 32, part, 0.0) + gcol_ref[cls]).astype(out.dtype)
+    put(N0, slice(1280, 1408), dot(dyt, act_ref[N0, :, N0:LANES]))
+    for lo, hi in ((LANES, 384), (384, 640), (640, 768)):
+        put(N1, slice(lo + 640, hi + 640), dot(dyt, act_ref[N0, :, lo:hi]))
+
+
+def layer_step(x_in, dy_in, gain_row, w_full, w_kv, tables, who, seq_len):
     f32 = jnp.float32
     bf16 = jnp.bfloat16
-    tokens, width = x_tok.shape
     n_tp = w_full.shape[N1]
     wide = w_full.shape[N3]
-    n_seq = tokens // seq_len
+    width = w_full.shape[N2]
+    n_seq = x_in.shape[N0] // n_tp
+    tokens = n_seq * seq_len
     half = width // N2
 
     def whole(shape):
-        return pl.BlockSpec(shape, lambda i: (N0,) * len(shape))
+        return pl.BlockSpec(shape, lambda i, *_: (N0,) * len(shape))
 
     def per(shape):
-        return pl.BlockSpec((N1,) + shape, lambda i: (i,) + (N0,) * len(shape))
-
-    w0_spec = pl.BlockSpec((N1, N1, width, wide), lambda i: (N0, i, N0, N0))
-    w1_spec = pl.BlockSpec((N1, N1, width, wide), lambda i: (N1, i, N0, N0))
+        return pl.BlockSpec((N1,) + shape, lambda i, *_: (i,) + (N0,) * len(shape))
+
+    w0_spec = pl.BlockSpec((N1, N1, width, wide), lambda i, *_: (N0, i, N0, N0))
+    w1_spec = pl.BlockSpec((N1, N1, width, wide), lambda i, *_: (N1, i, N0, N0))
+    mine = pl.BlockSpec((n_seq, seq_len, width), lambda i, who_ref: (who_ref[N0], N0, N0))
     tok = whole((tokens, width))
+    classes = whole((N2, half, tokens))
     params = pltpu.CompilerParams(dimension_semantics=('arbitrary',), vmem_limit_bytes=56 * KIB * KIB)
     wide_t = jax.ShapeDtypeStruct((n_tp, tokens, width), bf16)
     pair_t = jax.ShapeDtypeStruct((n_tp, tokens, PAIR), bf16)
     row_t = jax.ShapeDtypeStruct((tokens, width), bf16)
+    class_t = jax.ShapeDtypeStruct((N2, half, tokens), bf16)
     kv_t = jax.ShapeDtypeStruct((tokens, LANES), bf16)
-    h_norm, q_raw, kv_raw, d_o, act, d_gate, d_up = pl.pallas_call(
-        proj_kernel, name='proj', grid=(n_tp,),
-        in_specs=[tok, tok, whole((N1, width)), w0_spec, w1_spec, whole((width, LANES))],
-        out_specs=(tok, per((tokens, PAIR)), whole((tokens, LANES)), per((tokens, PAIR)), per((tokens, width)), per((tokens, width)), per((tokens, width))),
-        out_shape=(row_t, pair_t, kv_t, pair_t, wide_t, wide_t, wide_t),
-        compiler_params=params,
-    )(x_tok, dy_tok, gain_row, w_full, w_full, w_kv)
-
+    work = pl.CostEstimate(flops=13 * 10**9, bytes_accessed=40 * 10**6, transcendentals=N0)
+    h_t, dy_t, q_raw, kv_raw, d_o, act, d_gate, d_up = pl.pallas_call(
+        proj_kernel, name='proj',
+        grid_spec=pltpu.PrefetchScalarGridSpec(
+            num_scalar_prefetch=N1, grid=(n_tp,),
+            in_specs=[mine, mine, whole((N1, width)), w0_spec, w1_spec, whole((width, LANES))],
+            out_specs=(classes, classes, per((tokens, PAIR)), whole((tokens, LANES)), per((tokens, PAIR)), per((tokens, width)), per((tokens, width)), per((tokens, width))),
+            scratch_shapes=[pltpu.VMEM((tokens, width), bf16)]),
+        out_shape=(class_t, class_t, pair_t, kv_t, pair_t, wide_t, wide_t, wide_t),
+        compiler_params=params, cost_estimate=work,
+    )(who, x_in, dy_in, gain_row, w_full, w_full, w_kv)
+
+    pair_spec = pl.BlockSpec((n_tp, seq_len, PAIR), lambda i: (N0, i, N0))
+    kv_spec = pl.BlockSpec((seq_len, LANES), lambda i: (i, N0))
+    table = whole((seq_len, LANES))
+    att, d_q, d_kv = pl.pallas_call(
+        att_kernel, name='attention', grid=(n_seq,),
+        in_specs=[pair_spec, kv_spec, pair_spec, table, table, table, table],
+        out_specs=(pair_spec, pair_spec, kv_spec),
+        out_shape=(pair_t, pair_t, kv_t),
+        scratch_shapes=[pltpu.VMEM((seq_len, LANES), f32)] * RING,
+        compiler_params=params, cost_estimate=work,
+    )(q_raw, kv_raw, d_o, *tables)
+
+    gcol_t = jax.ShapeDtypeStruct((N2, half, LANES), f32)
+    y_tok, gx_tok, gain_col = pl.pallas_call(
+        back_kernel, name='back',
+        grid_spec=pltpu.PrefetchScalarGridSpec(
+            num_scalar_prefetch=N1, grid=(n_tp,),
+            in_specs=[mine, mine, whole((N1, width)), w0_spec, w1_spec, whole((width, LANES)), per((tokens, PAIR)), per((tokens, width)), per((tokens, PAIR)),
+                      per((tokens, width)), per((tokens, width)), whole((tokens, LANES))],
+            out_specs=(tok, tok, whole((N2, half, LANES))),
+            scratch_shapes=[pltpu.VMEM((tokens, width), f32)] * N2),
+        out_shape=(row_t, row_t, gcol_t),
+        compiler_params=params, cost_estimate=work,
+    )(who, x_in, dy_in, gain_row, w_full, w_full, w_kv, att, act, d_q, d_gate, d_up, d_kv)
+
+    class_spec = pl.BlockSpec((N2, N1, half, wide), lambda i: (N0, i, N0, N0))
+    own, oth = pl.pallas_call(
+        wgrad_kernel, name='wgrad', grid=(n_tp,),
+        in_specs=[classes, classes, whole((N2, half, LANES)), per((tokens, PAIR)), per((tokens, width)), per((tokens, PAIR)),
+                  per((tokens, width)), per((tokens, width)), whole((tokens, LANES))],
+        out_specs=(class_spec, class_spec),
+        out_shape=(jax.ShapeDtypeStruct((N2, n_tp, half, wide), f32), jax.ShapeDtypeStruct((N2, n_tp, half, wide), bf16)),
+        compiler_params=params, cost_estimate=work,
+    )(h_t, dy_t, gain_col, att, act, d_q, d_gate, d_up, d_kv)
+    return y_tok, gx_tok, own, oth
+
+
+def rope_tables(seq_len, head_dim):
+    f32 = jnp.float32
     half_dim = head_dim // N2
     inv_freq = jnp.power(10000.0, -2.0 * jnp.arange(half_dim, dtype=f32) / head_dim)
     angle = jnp.arange(seq_len, dtype=f32)[:, None] * inv_freq[None, :]
@@ -342,51 +402,10 @@
     sin_q = jnp.concatenate([sin_h, sin_h], axis=N1)
     cos_k = jnp.concatenate([cos_h, jnp.ones_like(cos_h)], axis=N1)
     sin_k = jnp.concatenate([sin_h, jnp.zeros_like(sin_h)], axis=N1)
-    pair_spec = pl.BlockSpec((n_tp, seq_len, PAIR), lambda i: (N0, i, N0))
-    kv_spec = pl.BlockSpec((seq_len, LANES), lambda i: (i, N0))
-    table = whole((seq_len, LANES))
-    att, d_q, d_kv = pl.pallas_call(
-        att_kernel, name='attention', grid=(n_seq,),
-        in_specs=[pair_spec, kv_spec, pair_spec, table, table, table, table],
-        out_specs=(pair_spec, pair_spec, kv_spec),
-        out_shape=(pair_t, pair_t, kv_t),
-        scratch_shapes=[pltpu.VMEM((seq_len, LANES), f32)] * RING,
-        compiler_params=params,
-    )(q_raw, kv_raw, d_o, cos_q, sin_q, cos_k, sin_k)
-
-    y_tok, gx_tok, gain_part = pl.pallas_call(
-        back_kernel, name='back', grid=(n_tp,),
-        in_specs=[tok, tok, whole((N1, width)), w0_spec, w1_spec, whole((width, LANES)), per((tokens, PAIR)), per((tokens, width)), per((tokens, PAIR)),
-                  per((tokens, width)), per((tokens, width)), whole((tokens, LANES))],
-        out_specs=(tok, tok, whole((N1, width))),
-        out_shape=(row_t, row_t, jax.ShapeDtypeStruct((N1, width), f32)),
-        scratch_shapes=[pltpu.VMEM((tokens, width), f32)] * N2,
-        compiler_params=params,
-    )(x_tok, dy_tok, gain_row, w_full, w_full, w_kv, att, act, d_q, d_gate, d_up, d_kv)
-
-    def by_class(vals):
-        vals = vals.reshape(16, N2, 24, vals.shape[N1])
-        mine = lax.dynamic_index_in_dim(vals, core, N1, keepdims=False)
-        theirs = lax.dynamic_index_in_dim(vals, N1 - core, N1, keepdims=False)
-        return jnp.stack([mine, theirs]).reshape(N2, half, vals.shape[N3])
-
-    h_t = by_class(h_norm.T)
-    dy_t = by_class(dy_tok.T)
-    gain_col = jnp.where(jnp.arange(LANES)[None, :] == 32, gain_part.reshape(width, N1), 0.0)
-    gain_col = by_class(gain_col)
-    class_spec = pl.BlockSpec((N2, N1, half, wide), lambda i: (N0, i, N0, N0))
-    own, oth = pl.pallas_call(
-        wgrad_kernel, name='wgrad', grid=(n_tp,),
-        in_specs=[whole((N2, half, tokens)), whole((N2, half, tokens)), whole((N2, half, LANES)), per((tokens, PAIR)), per((tokens, width)), per((tokens, PAIR)),
-                  per((tokens, width)), per((tokens, width)), whole((tokens, LANES))],
-        out_specs=(class_spec, class_spec),
-        out_shape=(jax.ShapeDtypeStruct((N2, n_tp, half, wide), f32), jax.ShapeDtypeStruct((N2, n_tp, half, wide), bf16)),
-        compiler_params=params,
-    )(h_t, dy_t, gain_col, att, act, d_q, d_gate, d_up, d_kv)
-    return y_tok, gx_tok, own, oth
-
-
-def sum_kernel(g_ref, gs_ref, gx_ref, w_out, kv_out, gx_out, acc, rp, sa, ra1, ra2, sb, rb1, rb2, sc, rc, kvx, gsem, d2s, d2r, ss, rs, cs, cr, ks, kr, xs, xr, lsem):
+    return cos_q, sin_q, cos_k, sin_k
+
+
+def sum_kernel(g_ref, gs_ref, gx_ref, y_ref, below_ref, above_ref, w_out, kv_out, gx_out, y_out, acc, rp, sa, ra1, ra2, sb, rb1, rb2, sc, rc, kvx, gsem, d2s, d2r, ss, rs, cs, cr, ks, kr, xs, xr, lsem):
     f32 = jnp.float32
     bf16 = jnp.bfloat16
     t = lax.axis_index('tp')
@@ -440,6 +459,16 @@
             pair[col][n].start()
     mine = gx_ref.shape[N0]
     my_rows = pl.ds(t * mine, mine)
+    lower = pl.ds(up(t, N3) * mine, mine)
+    upper = pl.ds(up(t, N1) * mine, mine)
+    y_up = rcopy(below_ref.at[:, pl.ds(N0, LANES)], y_out.at[lower, pl.ds(N0, LANES)], xs.at[RING], xr.at[RING], xp[N1])
+    y_dn = rcopy(above_ref.at[:, pl.ds(LANES, LANES)], y_out.at[upper, pl.ds(LANES, LANES)], xs.at[5], xr.at[5], xp[N3])
+    y_up.start()
+    y_dn.start()
+    y_keep = []
+    for n, (ref, place) in enumerate(((y_ref, my_rows), (below_ref, lower), (above_ref, upper))):
+        y_keep.append(pltpu.make_async_copy(ref, y_out.at[place], lsem.at[n + N1]))
+        y_keep[n].start()
     x_up = rcopy(gx_ref, gx_out.at[my_rows], xs.at[N0], xr.at[N0], xp[N1])
     x_dn = rcopy(gx_ref, gx_out.at[my_rows], xs.at[N1], xr.at[N1], xp[N3])
     x_up.start()
@@ -502,10 +531,8 @@
             send(sa.at[col, n, pl.ds(base, N2)], ra2.at[col, n - N1, pl.ds(base, N2)], ss.at[col, n + N3], rs.at[col, n + N3], dev_a[col][peer])
     x_up.wait_recv()
     x_dn.wait_recv()
-    from_dn = up(t, N3) * mine * N2
-    from_up = up(t, N1) * mine * N2
-    half_dn = gx_out.at[pl.ds(up(t, N3) * mine, mine), pl.ds(N0, LANES)]
-    half_up = gx_out.at[pl.ds(up(t, N1) * mine, mine), pl.ds(LANES, LANES)]
+    half_dn = gx_out.at[lower, pl.ds(N0, LANES)]
+    half_up = gx_out.at[upper, pl.ds(LANES, LANES)]
     x_up2 = rcopy(half_dn, half_dn, xs.at[N2], xr.at[N2], xp[N1])
     x_dn2 = rcopy(half_up, half_up, xs.at[N3], xr.at[N3], xp[N3])
     x_up2.start()
@@ -602,9 +629,13 @@
     x_dn.wait_send()
     x_up2.wait()
     x_dn2.wait()
-
-
-def sum_grads(g_pack, g_send, gx_my, n_batch):
+    y_up.wait()
+    y_dn.wait()
+    for copy in y_keep:
+        copy.wait()
+
+
+def sum_grads(g_pack, g_send, gx_my, y_blocks, n_batch):
     f32 = jnp.float32
     bf16 = jnp.bfloat16
     wide = g_pack.shape[-N1]
@@ -615,18 +646,19 @@
         sum_kernel,
         name='sum_grads',
         out_shape=(jax.ShapeDtypeStruct((N2, N3, SUB, wide), f32), jax.ShapeDtypeStruct((RING, N3, SUB, LANES), f32),
-                   jax.ShapeDtypeStruct((n_batch,) + gx_my.shape[N1:], bf16)),
-        in_specs=[any_spec, any_spec, any_spec],
-        out_specs=(vmem, vmem, any_spec),
+                   jax.ShapeDtypeStruct((n_batch,) + gx_my.shape[N1:], bf16), jax.ShapeDtypeStruct((n_batch,) + gx_my.shape[N1:], bf16)),
+        in_specs=[any_spec] * 6,
+        out_specs=(vmem, vmem, any_spec, any_spec),
         scratch_shapes=[
             pltpu.VMEM((N2, RING, RING, RING, N3, SUB, wide), f32), pltpu.VMEM((N2, RING, RING, RING, N3, SUB, wide), bf16),
             pltpu.VMEM((N2, N3, RING, RING, N3, SUB, wide), bf16), pltpu.VMEM((N2, N2, N2, RING, N3, SUB, wide), bf16), pltpu.VMEM((N2, N2, RING, RING, N3, SUB, wide), bf16),
             pltpu.VMEM((N2, N3, RING, N3, SUB, wide), bf16), pltpu.VMEM((N2, N2, N2, N3, SUB, wide), bf16), pltpu.VMEM((N2, N2, RING, N3, SUB, wide), bf16),
             pltpu.VMEM((N2, RING, N3, SUB, wide), bf16), pltpu.VMEM((N2, N3, N3, SUB, wide), bf16), pltpu.VMEM((RING, RING, N3, SUB, LANES), f32),
-            dma((N2, RING)), dma((N2, RING)), dma((N2, RING)), dma((N2, 12)), dma((N2, 12)), dma((N2, N3)), dma((N2, N3)), dma((N3,)), dma((N3,)), dma((RING,)), dma((RING,)), dma((N1,)),
+            dma((N2, RING)), dma((N2, RING)), dma((N2, RING)), dma((N2, 12)), dma((N2, 12)), dma((N2, N3)), dma((N2, N3)), dma((N3,)), dma((N3,)), dma((6,)), dma((6,)), dma((RING,)),
         ],
+        cost_estimate=pl.CostEstimate(flops=60 * 10**9, bytes_accessed=30 * 10**6, transcendentals=N0),
         compiler_params=pltpu.CompilerParams(collective_id=N1, has_side_effects=True, vmem_limit_bytes=60 * KIB * KIB),
-    )(g_pack, g_send, gx_my)
+    )(g_pack, g_send, gx_my, *y_blocks)
 
 
 def solution(mesh):
@@ -643,7 +675,6 @@
         nf = w_gate.shape[N1]
         part = N2 * head_dim // n_tp
         mine = n_batch // n_tp
-        tokens = mine * seq_len
         tp = lax.axis_index('tp')
         core = lax.rem(lax.axis_index('fsdp'), N2)
         gain_hi = lax.reduce_precision(ln_gain, SUB, 7)
@@ -655,18 +686,20 @@
         down = w_down.T
         packed = jnp.stack([jnp.concatenate([w_gate, w_q, w_o.T, small, down[:, :LANES]], axis=N1), jnp.concatenate([w_up, down[:, LANES:]], axis=N1)])
         wide = packed.shape[N2]
+        tables = rope_tables(seq_len, head_dim)
         full = gather_weights(packed).reshape(N2, n_tp, width, wide)
         small_full = full[N0, :, :, KV_AT:KV_AT + LANES]
         w_kv = jnp.concatenate([small_full[n, :, :part] for n in range(n_tp)], axis=N1)
         gain3 = small_full[N0, :, part:part + N3].astype(f32)
         gain_row = (gain3[:, N0] + gain3[:, N1] + gain3[:, N2]).reshape(N1, width)
 
-        x_tok = lax.dynamic_slice_in_dim(x_in, tp * mine, mine, N0).reshape(tokens, width)
-        dy_tok = lax.dynamic_slice_in_dim(dy_out, tp * mine, mine, N0).reshape(tokens, width)
-        y_tok, gx_tok, g_own, g_oth = layer_step(x_tok, dy_tok, gain_row, full, w_kv, core, seq_len, head_dim)
-        y_out = lax.all_gather(y_tok.reshape(mine, seq_len, width), 'tp', axis=N0, tiled=True)
+        who = jnp.stack([tp, core]).astype(jnp.int32)
+        y_tok, gx_tok, g_own, g_oth = layer_step(x_in, dy_out, gain_row, full, w_kv, tables, who, seq_len)
+        y_my = y_tok.reshape(mine, seq_len, width)
+        below = lax.ppermute(y_my, 'tp', [(n, (n + N1) % n_tp) for n in range(n_tp)])
+        above = lax.ppermute(y_my, 'tp', [(n, (n - N1) % n_tp) for n in range(n_tp)])
         split = (N2, n_tp, RING, RING, N3, SUB, wide)
-        w_sum, kv_sum, grad_x = sum_grads(g_own.reshape(split), g_oth.reshape(split), gx_tok.reshape(mine, seq_len, width), n_batch)
+        w_sum, kv_sum, grad_x, y_out = sum_grads(g_own.reshape(split), g_oth.reshape(split), gx_tok.reshape(mine, seq_len, width), (y_my, below, above), n_batch)
         w0 = w_sum[N0].reshape(rows, wide)
         w1 = w_sum[N1].reshape(rows, wide)
         kv_all = jnp.swapaxes(kv_sum.reshape(n_tp, rows, LANES)[:, :, :part], N0, N1).reshape(rows, N2 * head_dim)

time: 270 us -> 329 us (1.22)
  Pallas kernels: 218 us -> 295 us
  between operations: 14.2 us -> 0.75 us
  local copies, waits for them, and re-layouts: 27.6 us -> 19.3 us
    pallas_call x1, Pallas kernels: 69.8 us -> 148 us  [sum_grads(): pl.pallas_call(sum_kernel, name='sum_grads', out_shape=(jax.ShapeDtypeStr...]
    unnamed x13 -> x11, local copies, waits for them, and re-layouts: 14 us -> 9.34 us
    dynamic_slice x4 -> x0, local copies, waits for them, and re-layouts: 3.41 us -> none  [the longest x1 3.21 us: device_step(): lax.dynamic_slice_in_dim(dy_out, tp * mine, mine, N0).reshape(tokens, width)]
  transfers between devices with their start and end apart: 1 -> 2, of which waited for: 0 -> 1; matrix products, arithmetic and copies ran while one was open for 5% -> 0% of each run, Pallas kernels for 35% -> 7%
where the time goes in v3:
time: 329 us; the launch traced here: 328 us
  Pallas kernels  295 us (90%)
  local copies, waits for them, and re-layouts  19.3 us (6%)
  other arithmetic  7.18 us (2%)
    pallas_call x1, Pallas kernels, sum_grads(): pl.pallas_call(sum_kernel, name='sum_grads', out_shape=(jax.ShapeDtypeStr...  148 us
    pallas_call x1, Pallas kernels, gather_weights(): pl.pallas_call(gather_kernel, name='gather_weights', out_shape=jax.ShapeD...  52.5 us
    pallas_call x1, Pallas kernels, layer_step(): pl.pallas_call(back_kernel, name='back', grid_spec=pltpu.PrefetchScalarGr...  26.4 us
    pallas_call x1, Pallas kernels, layer_step(): pl.pallas_call(proj_kernel, name='proj', grid_spec=pltpu.PrefetchScalarGr...  24.5 us
    pallas_call x1, Pallas kernels, layer_step(): pl.pallas_call(wgrad_kernel, name='wgrad', grid=(n_tp,), in_specs=[classe...  23.6 us
    pallas_call x1, Pallas kernels, layer_step(): pl.pallas_call(att_kernel, name='attention', grid=(n_seq,), in_specs=[pai...  19.8 us
    unnamed x11, local copies, waits for them, and re-layouts  9.34 us
  transfers between devices with their start and end apart: 2, of which 1 were waited for; matrix products, arithmetic and copies ran while one was open for 0% of the time, Pallas kernels for 7%

profile of v3, /device:TPU:0, one launch (start us, length us, event | category | flops | bytes accessed | tf_op | source)
XLA Modules:
  0.0 328.3 jit_solution(13343768947227351803)
XLA Ops:
  0.6 0.7 slice.96
  1.3 0.8 slice.97
  2.1 0.7 fusion.10
  3.0 0.8 maximum_bitcast_fusion.1
  3.8 0.8 dynamic-slice_maximum_fusion
  4.6 0.9 concatenate.36
  5.5 0.7 pad_maximum_fusion.1.p_ref
  6.2 52.5 %gather_weights.1 = bf16[2,4,4,4,2,3,8,1408]{7,6,5,4,3,2,1,0:T(8,128)(2,1)} custom-call(bf16[2,3,8,1408]{3,2,1,0:T(8,128)(2,1)} %pad_maximum_fusion.1.p_ref), custom_call_target="tpu_custom_call" | custom-call | tf_op jit(solution)/shard_map/gather_weights/pallas_call | solution.py:121
  58.7 1.2 slice_bitcast_fusion
  61.8 0.6 pad_add_fusion.who_ref
  62.4 0.9 pad_maximum_fusion.wkv_ref
  63.3 24.5 %proj.1 = (bf16[2,384,768]{2,1,0:T(8,128)(2,1)}, bf16[2,384,768]{2,1,0:T(8,128)(2,1)}, bf16[4,768,256]{2,1,0:T(8,128)(2,1)}, bf16[768,128]{1,0:T(8,128)(2,1)}, b...) custom-call(s32[2]{0:T(128)} %pad_add_fusion.who_ref, ...), custom_call_target="tpu_custom_call" | custom-call | flops 12999999488 | bytes 40000000 | tf_op jit(solution)/shard_map/proj/pallas_call | solution.py:344
  87.8 1.0 fusion.2
  88.9 19.8 %attention.1 = (bf16[4,768,256]{2,1,0:T(8,128)(2,1)}, bf16[4,768,256]{2,1,0:T(8,128)(2,1)}, bf16[768,128]{1,0:T(8,128)(2,1)}) custom-call(bf16[4,768,256]{2,1,0:T(8,128)(2,1)} %get-tuple-element.32.q_ref, bf16[768,128]{1,0:T(8,128)(2,1)} %get-tuple-element.33.kv_ref, bf16[4,768,256]{2,1,0:T(8,128)(2,1)} %get-tuple-element.34.do_ref, ...), custom_call_target="tpu_custom_call" | custom-call | flops 12999999488 | bytes 40000000 | tf_op jit(solution)/shard_map/attention/pallas_call | solution.py:358
  108.7 26.4 %back.1 = (bf16[768,768]{1,0:T(8,128)(2,1)}, bf16[768,768]{1,0:T(8,128)(2,1)}, f32[2,384,128]{2,1,0:T(8,128)}) custom-call(s32[2]{0:T(128)} %pad_add_fusion.who_ref, bf16[12,256,768]{2,1,0:T(8,128)(2,1)} %x_ref.3, bf16[12,256,768]{2,1,0:T(8,128)(2,1)} %dy_ref.3, f32[1,768]{1,0:T(1,128)} %add.30.gain_ref, bf16[2,4,768,1408]{3,2,1,0:T(8,128)(2,1)} %bitcast.50, ...), custom_call_target="tpu_custom_call" | custom-call | flops 12999999488 | bytes 40000000 | tf_op jit(solution)/shard_map/back/pallas_call | solution.py:368
  135.1 0.7 collective-permute-start
  135.8 2.5 collective-permute-start.1
  138.3 23.6 %wgrad.1 = (f32[2,4,384,1408]{3,2,1,0:T(8,128)}, bf16[2,4,384,1408]{3,2,1,0:T(8,128)(2,1)}) custom-call(bf16[2,384,768]{2,1,0:T(8,128)(2,1)} %get-tuple-element.30.ht_ref, bf16[2,384,768]{2,1,0:T(8,128)(2,1)} %get-tuple-element.31.dyt_ref, f32[2,384,128]{2,1,0:T(8,128)} %get-tuple-element.41.gcol_ref, bf16[4,768,256]{2,1,0:T(8,128)(2,1)} %get-tuple-element.35.o_ref, ...), custom_call_target="tpu_custom_call" | custom-call | flops 12999999488 | bytes 40000000 | tf_op jit(solution)/shard_map/wgrad/pallas_call | solution.py:381
  161.9 2.7 collective-permute-done.below_ref
  164.6 1.0 copy-done
  166.0 148.3 %sum_grads.1 = (f32[2,3,8,1408]{3,2,1,0:T(8,128)}, f32[4,3,8,128]{3,2,1,0:T(8,128)}, bf16[12,256,768]{2,1,0:T(8,128)(2,1)}, bf16[12,256,768]{2,1,0:T(8,128)(2,1)}) custom-call(f32[2,4,4,4,3,8,1408]{6,5,4,3,2,1,0:T(8,128)} %bitcast.64, bf16[2,4,4,4,3,8,1408]{6,5,4,3,2,1,0:T(8,128)(2,1)} %bitcast.65, bf16[3,256,768]{2,1,0:T(8,128)(2,1)} %bitcast.63, ...), custom_call_target="tpu_custom_call" | custom-call | flops 60000002048 | bytes 30000000 | tf_op jit(solution)/shard_map/sum_grads/pallas_call | solution.py:645
  314.3 1.0 slice_bitcast_fusion.6
  315.3 0.6 slice.113
  316.0 0.6 slice.114
  316.6 0.7 slice_bitcast_fusion.9
  317.3 0.7 slice_bitcast_fusion.10
  318.0 0.8 slice_bitcast_fusion.8
  318.9 0.7 fusion.11
  319.7 0.6 copy.30
  320.3 0.6 maximum_bitcast_fusion
  320.9 5.2 %copy.33 = bf16[12,256,768]{2,1,0:T(8,128)(2,1)} copy(bf16[12,256,768]{2,1,0:T(8,128)(2,1)} %get-tuple-element.82) | data formatting | bytes 9437184
  326.1 2.2 copy.34
  (28 shorter events, 2.7 us)
Async XLA Ops:
  135.1 29.5 %collective-permute-start = (bf16[3,256,768]{2,1,0:T(8,128)(2,1)}, bf16[3,256,768]{2,1,0:T(8,128)(2,1)S(1)}, u32[]{:S(2)}, u32[]{:S(2)}) collective-permute-start(bf16[3,256,768]{2,1,0:T(8,128)(2,1)} %bitcast.60), channel_id=1, source_target_pairs={{0,32},{32,64},{64,96},{96,0},{1,33},{33,65},{65,97},{97,1},{2,34}... | collective-permute-start | bytes 3538952 | tf_op jit(solution)/shard_map/ppermute | solution.py:699
  135.8 28.8 %collective-permute-start.1 = (bf16[3,256,768]{2,1,0:T(8,128)(2,1)}, bf16[3,256,768]{2,1,0:T(8,128)(2,1)S(1)}, u32[]{:S(2)}, u32[]{:S(2)}) collective-permute-start(bf16[3,256,768]{2,1,0:T(8,128)(2,1)} %bitcast.61), channel_id=1, source_target_pairs={{0,96},{32,0},{64,32},{96,64},{1,97},{33,1},{65,33},{97,65},{2,98}... | collective-permute-start | bytes 3538952 | tf_op jit(solution)/shard_map/ppermute | solution.py:700
  164.6 1.0 copy-start
  164.6 1.4 copy-start.1
  320.3 5.8 %slice-start = ((s8[4718592]{0:T(1024)(128)(4,1)}), s8[4194304]{0:T(1024)(128)(4,1)S(1)}, s32[]{:S(2)}) async-start(s8[4718592]{0:T(1024)(128)(4,1)} %bitcast.52), calls=%async_computation | async-start | bytes 8388608
  320.9 5.2 %slice-start.1 = ((s8[4718592]{0:T(1024)(128)(4,1)}), s8[524288]{0:T(1024)(128)(4,1)S(1)}, s32[]{:S(2)}) async-start(s8[4718592]{0:T(1024)(128)(4,1)} %bitcast.52), calls=%async_computation.1 | async-start | bytes 1048576

commit v4 on v3

--- a/solution.py
+++ b/solution.py
@@ -17,7 +17,7 @@
 MESH_ID = pl.DeviceIdType.MESH
 
 
-def gather_kernel(p_ref, g_ref, lsem, s1, r1, s2, r2, s3, r3, ds, dr):
+def gather_kernel(p_ref, g_ref, hold, lsem, s1, r1, s2, r2, s3, r3, ds, dr):
     t = lax.axis_index('tp')
     f = lax.axis_index('fsdp')
     c = lax.rem(f, N2)
@@ -37,7 +37,7 @@
     greeted = [partner] + [peer(axis, d) for axis in 'xyz' for d in (N1, N2, N3)]
     for who in greeted:
         pl.semaphore_signal(barrier, inc=N1, device_id=who, device_id_type=MESH_ID)
-    own = pltpu.make_async_copy(p_ref, g_ref.at[:, at['x'], at['z'], at['y'], c], lsem.at[N0])
+    own = pltpu.make_async_copy(p_ref, hold, lsem.at[N0])
     own.start()
     pl.semaphore_wait(barrier, len(greeted))
 
@@ -82,9 +82,12 @@
                 landed(view(k, h, there, c), ss.at[k, n], rr.at[k, n])
             share(k, h, there, base + m)
 
+    own.wait()
+    own = pltpu.make_async_copy(hold, g_ref.at[:, at['x'], at['z'], at['y'], c], lsem.at[N0])
+    own.start()
     for k, order in enumerate(orders):
         for d in (N1, N3, N2):
-            push(p_ref.at[:, k], view(k, both, at, c), s1.at[k, d - N1], r1.at[k, d - N1], peer(order[N0], d))
+            push(hold.at[:, k], view(k, both, at, c), s1.at[k, d - N1], r1.at[k, d - N1], peer(order[N0], d))
     own.wait()
     second = []
     third = []
@@ -124,7 +127,7 @@
         out_shape=jax.ShapeDtypeStruct((N2, RING, RING, RING, N2, N3, SUB, wide), packed.dtype),
         in_specs=[any_spec],
         out_specs=any_spec,
-        scratch_shapes=[dma((N1,)), dma((N3, N3)), dma((N3, N3)), dma((N3, 6)), dma((N3, 6)), dma((N3, 6)), dma((N3, 6)), dma((N3, 14)), dma((N3, 14))],
+        scratch_shapes=[pltpu.VMEM((N2, N3, SUB, wide), packed.dtype), dma((N1,)), dma((N3, N3)), dma((N3, N3)), dma((N3, 6)), dma((N3, 6)), dma((N3, 6)), dma((N3, 6)), dma((N3, 14)), dma((N3, 14))],
         compiler_params=pltpu.CompilerParams(collective_id=N2, has_side_effects=True, vmem_limit_bytes=60 * KIB * KIB),
     )(packed.reshape(N2, N3, SUB, wide))
 
@@ -405,7 +408,7 @@
     return cos_q, sin_q, cos_k, sin_k
 
 
-def sum_kernel(g_ref, gs_ref, gx_ref, y_ref, below_ref, above_ref, w_out, kv_out, gx_out, y_out, acc, rp, sa, ra1, ra2, sb, rb1, rb2, sc, rc, kvx, gsem, d2s, d2r, ss, rs, cs, cr, ks, kr, xs, xr, lsem):
+def sum_kernel(g_ref, gs_ref, gx_ref, y_ref, below_ref, above_ref, w_out, kv_out, gx_out, y_out, acc, rp, sa, ra1, ra2, sb, rb1, rb2, sc, rc, kvx, gsem, d2s, d2r, ss, rs, cs, cr, ks, kr, xs, xr, lsem, keep):
     f32 = jnp.float32
     bf16 = jnp.bfloat16
     t = lax.axis_index('tp')
@@ -465,16 +468,15 @@
     y_dn = rcopy(above_ref.at[:, pl.ds(LANES, LANES)], y_out.at[upper, pl.ds(LANES, LANES)], xs.at[5], xr.at[5], xp[N3])
     y_up.start()
     y_dn.start()
-    y_keep = []
-    for n, (ref, place) in enumerate(((y_ref, my_rows), (below_ref, lower), (above_ref, upper))):
-        y_keep.append(pltpu.make_async_copy(ref, y_out.at[place], lsem.at[n + N1]))
-        y_keep[n].start()
     x_up = rcopy(gx_ref, gx_out.at[my_rows], xs.at[N0], xr.at[N0], xp[N1])
     x_dn = rcopy(gx_ref, gx_out.at[my_rows], xs.at[N1], xr.at[N1], xp[N3])
     x_up.start()
     x_dn.start()
-    x_me = pltpu.make_async_copy(gx_ref, gx_out.at[my_rows], lsem.at[N0])
-    x_me.start()
+    local = ((gx_ref, gx_out, my_rows), (y_ref, y_out, my_rows), (below_ref, y_out, lower), (above_ref, y_out, upper))
+    taken = [pltpu.make_async_copy(ref, keep.at[n], lsem.at[n]) for n, (ref, _, _) in enumerate(local)]
+    placed = [pltpu.make_async_copy(keep.at[n], out.at[place], lsem.at[n]) for n, (_, out, place) in enumerate(local)]
+    for copy in taken:
+        copy.start()
 
     def each(count, body):
         def step(n, carry):
@@ -529,6 +531,9 @@
                 sa[col, n, a2, tt, r] = val.astype(bf16)
             each(24, joined)
             send(sa.at[col, n, pl.ds(base, N2)], ra2.at[col, n - N1, pl.ds(base, N2)], ss.at[col, n + N3], rs.at[col, n + N3], dev_a[col][peer])
+    for n in range(RING):
+        taken[n].wait()
+        placed[n].start()
     x_up.wait_recv()
     x_dn.wait_recv()
     half_dn = gx_out.at[lower, pl.ds(N0, LANES)]
@@ -624,14 +629,13 @@
     for col in range(N2):
         for n in range(RING):
             pair[col][n].wait_send()
-    x_me.wait()
     x_up.wait_send()
     x_dn.wait_send()
     x_up2.wait()
     x_dn2.wait()
     y_up.wait()
     y_dn.wait()
-    for copy in y_keep:
+    for copy in placed:
         copy.wait()
 
 
@@ -654,7 +658,7 @@
             pltpu.VMEM((N2, N3, RING, RING, N3, SUB, wide), bf16), pltpu.VMEM((N2, N2, N2, RING, N3, SUB, wide), bf16), pltpu.VMEM((N2, N2, RING, RING, N3, SUB, wide), bf16),
             pltpu.VMEM((N2, N3, RING, N3, SUB, wide), bf16), pltpu.VMEM((N2, N2, N2, N3, SUB, wide), bf16), pltpu.VMEM((N2, N2, RING, N3, SUB, wide), bf16),
             pltpu.VMEM((N2, RING, N3, SUB, wide), bf16), pltpu.VMEM((N2, N3, N3, SUB, wide), bf16), pltpu.VMEM((RING, RING, N3, SUB, LANES), f32),
-            dma((N2, RING)), dma((N2, RING)), dma((N2, RING)), dma((N2, 12)), dma((N2, 12)), dma((N2, N3)), dma((N2, N3)), dma((N3,)), dma((N3,)), dma((6,)), dma((6,)), dma((RING,)),
+            dma((N2, RING)), dma((N2, RING)), dma((N2, RING)), dma((N2, 12)), dma((N2, 12)), dma((N2, N3)), dma((N2, N3)), dma((N3,)), dma((N3,)), dma((6,)), dma((6,)), dma((RING,)), pltpu.VMEM((RING,) + gx_my.shape, bf16),
         ],
         cost_estimate=pl.CostEstimate(flops=60 * 10**9, bytes_accessed=30 * 10**6, transcendentals=N0),
         compiler_params=pltpu.CompilerParams(collective_id=N1, has_side_effects=True, vmem_limit_bytes=60 * KIB * KIB),

time: 329 us -> 248 us (0.75)
  Pallas kernels: 295 us -> 214 us
    pallas_call x1, Pallas kernels: 148 us -> 67 us  [sum_grads(): pl.pallas_call(sum_kernel, name='sum_grads', out_shape=(jax.ShapeDtypeStr...]
  transfers between devices with their start and end apart: 2 -> 2, of which waited for: 1 -> 1; matrix products, arithmetic and copies ran while one was open for 0% -> 0% of each run, Pallas kernels for 7% -> 10%
where the time goes in v4:
time: 248 us; the launch traced here: 247 us
  Pallas kernels  214 us (86%)
  local copies, waits for them, and re-layouts  19.3 us (8%)
  other arithmetic  7.18 us (3%)
  starting transfers between devices  3.24 us (1%)
  waiting for transfers between devices  2.68 us (1%)
    pallas_call x1, Pallas kernels, sum_grads(): pl.pallas_call(sum_kernel, name='sum_grads', out_shape=(jax.ShapeDtypeStr...  67 us
    pallas_call x1, Pallas kernels, gather_weights(): pl.pallas_call(gather_kernel, name='gather_weights', out_shape=jax.ShapeD...  52.5 us
    pallas_call x1, Pallas kernels, layer_step(): pl.pallas_call(back_kernel, name='back', grid_spec=pltpu.PrefetchScalarGr...  26.4 us
    pallas_call x1, Pallas kernels, layer_step(): pl.pallas_call(proj_kernel, name='proj', grid_spec=pltpu.PrefetchScalarGr...  24.5 us
    pallas_call x1, Pallas kernels, layer_step(): pl.pallas_call(wgrad_kernel, name='wgrad', grid=(n_tp,), in_specs=[classe...  23.6 us
    pallas_call x1, Pallas kernels, layer_step(): pl.pallas_call(att_kernel, name='attention', grid=(n_seq,), in_specs=[pai...  19.8 us
    unnamed x11, local copies, waits for them, and re-layouts  9.34 us
  transfers between devices with their start and end apart: 2, of which 1 were waited for; matrix products, arithmetic and copies ran while one was open for 0% of the time, Pallas kernels for 10%

profile of v4, /device:TPU:0, one launch (start us, length us, event | category | flops | bytes accessed | tf_op | source)
XLA Modules:
  0.0 247.0 jit_solution(15657555205875147458)
XLA Ops:
  0.6 0.7 slice.96
  1.3 0.8 slice.97
  2.1 0.7 fusion.10
  3.0 0.8 maximum_bitcast_fusion.1
  3.8 0.8 dynamic-slice_maximum_fusion
  4.6 0.9 concatenate.36
  5.5 0.7 pad_maximum_fusion.1.p_ref
  6.2 52.5 %gather_weights.1 = bf16[2,4,4,4,2,3,8,1408]{7,6,5,4,3,2,1,0:T(8,128)(2,1)} custom-call(bf16[2,3,8,1408]{3,2,1,0:T(8,128)(2,1)} %pad_maximum_fusion.1.p_ref), custom_call_target="tpu_custom_call" | custom-call | tf_op jit(solution)/shard_map/gather_weights/pallas_call | solution.py:124
  58.7 1.2 slice_bitcast_fusion
  61.8 0.6 pad_add_fusion.who_ref
  62.4 0.9 pad_maximum_fusion.wkv_ref
  63.3 24.5 %proj.1 = (bf16[2,384,768]{2,1,0:T(8,128)(2,1)}, bf16[2,384,768]{2,1,0:T(8,128)(2,1)}, bf16[4,768,256]{2,1,0:T(8,128)(2,1)}, bf16[768,128]{1,0:T(8,128)(2,1)}, b...) custom-call(s32[2]{0:T(128)} %pad_add_fusion.who_ref, ...), custom_call_target="tpu_custom_call" | custom-call | flops 12999999488 | bytes 40000000 | tf_op jit(solution)/shard_map/proj/pallas_call | solution.py:347
  87.8 1.0 fusion.2
  88.9 19.8 %attention.1 = (bf16[4,768,256]{2,1,0:T(8,128)(2,1)}, bf16[4,768,256]{2,1,0:T(8,128)(2,1)}, bf16[768,128]{1,0:T(8,128)(2,1)}) custom-call(bf16[4,768,256]{2,1,0:T(8,128)(2,1)} %get-tuple-element.32.q_ref, bf16[768,128]{1,0:T(8,128)(2,1)} %get-tuple-element.33.kv_ref, bf16[4,768,256]{2,1,0:T(8,128)(2,1)} %get-tuple-element.34.do_ref, ...), custom_call_target="tpu_custom_call" | custom-call | flops 12999999488 | bytes 40000000 | tf_op jit(solution)/shard_map/attention/pallas_call | solution.py:361
  108.7 26.4 %back.1 = (bf16[768,768]{1,0:T(8,128)(2,1)}, bf16[768,768]{1,0:T(8,128)(2,1)}, f32[2,384,128]{2,1,0:T(8,128)}) custom-call(s32[2]{0:T(128)} %pad_add_fusion.who_ref, bf16[12,256,768]{2,1,0:T(8,128)(2,1)} %x_ref.3, bf16[12,256,768]{2,1,0:T(8,128)(2,1)} %dy_ref.3, f32[1,768]{1,0:T(1,128)} %add.30.gain_ref, bf16[2,4,768,1408]{3,2,1,0:T(8,128)(2,1)} %bitcast.50, ...), custom_call_target="tpu_custom_call" | custom-call | flops 12999999488 | bytes 40000000 | tf_op jit(solution)/shard_map/back/pallas_call | solution.py:371
  135.1 0.7 collective-permute-start
  135.8 2.5 %collective-permute-start.1 = (bf16[3,256,768]{2,1,0:T(8,128)(2,1)}, bf16[3,256,768]{2,1,0:T(8,128)(2,1)S(1)}, u32[]{:S(2)}, u32[]{:S(2)}) collective-permute-start(bf16[3,256,768]{2,1,0:T(8,128)(2,1)} %bitcast.61), channel_id=1, source_target_pairs={{0,96},{32,0},{64,32},{96,64},{1,97},{33,1},{65,33},{97,65},{2,98}... | collective-permute-start | bytes 3538952 | tf_op jit(solution)/shard_map/ppermute | solution.py:704
  138.3 23.6 %wgrad.1 = (f32[2,4,384,1408]{3,2,1,0:T(8,128)}, bf16[2,4,384,1408]{3,2,1,0:T(8,128)(2,1)}) custom-call(bf16[2,384,768]{2,1,0:T(8,128)(2,1)} %get-tuple-element.30.ht_ref, bf16[2,384,768]{2,1,0:T(8,128)(2,1)} %get-tuple-element.31.dyt_ref, f32[2,384,128]{2,1,0:T(8,128)} %get-tuple-element.41.gcol_ref, bf16[4,768,256]{2,1,0:T(8,128)(2,1)} %get-tuple-element.35.o_ref, ...), custom_call_target="tpu_custom_call" | custom-call | flops 12999999488 | bytes 40000000 | tf_op jit(solution)/shard_map/wgrad/pallas_call | solution.py:384
  161.9 2.7 %collective-permute-done.below_ref = bf16[3,256,768]{2,1,0:T(8,128)(2,1)S(1)} collective-permute-done((bf16[3,256,768]{2,1,0:T(8,128)(2,1)}, bf16[3,256,768]{2,1,0:T(8,128)(2,1)S(1)}, u32[]{:S(2)}, u32[]{:S(2)}) %collective-permute-start) | collective-permute-done | bytes 1179680 | tf_op jit(solution)/shard_map/ppermute | solution.py:703
  164.6 1.0 copy-done
  166.0 67.0 %sum_grads.1 = (f32[2,3,8,1408]{3,2,1,0:T(8,128)}, f32[4,3,8,128]{3,2,1,0:T(8,128)}, bf16[12,256,768]{2,1,0:T(8,128)(2,1)}, bf16[12,256,768]{2,1,0:T(8,128)(2,1)}) custom-call(f32[2,4,4,4,3,8,1408]{6,5,4,3,2,1,0:T(8,128)} %bitcast.64, bf16[2,4,4,4,3,8,1408]{6,5,4,3,2,1,0:T(8,128)(2,1)} %bitcast.65, bf16[3,256,768]{2,1,0:T(8,128)(2,1)} %bitcast.63, ...), custom_call_target="tpu_custom_call" | custom-call | flops 60000002048 | bytes 30000000 | tf_op jit(solution)/shard_map/sum_grads/pallas_call | solution.py:649
  233.1 1.0 slice_bitcast_fusion.6
  234.1 0.6 slice.113
  234.7 0.6 slice.114
  235.4 0.7 slice_bitcast_fusion.9
  236.0 0.7 slice_bitcast_fusion.10
  236.8 0.8 slice_bitcast_fusion.8
  237.7 0.7 fusion.11
  238.4 0.6 copy.30
  239.0 0.6 maximum_bitcast_fusion
  239.6 5.2 %copy.33 = bf16[12,256,768]{2,1,0:T(8,128)(2,1)} copy(bf16[12,256,768]{2,1,0:T(8,128)(2,1)} %get-tuple-element.82) | data formatting | bytes 9437184
  244.8 2.2 copy.34
  (28 shorter events, 2.7 us)
Async XLA Ops:
  135.1 29.5 %collective-permute-start = (bf16[3,256,768]{2,1,0:T(8,128)(2,1)}, bf16[3,256,768]{2,1,0:T(8,128)(2,1)S(1)}, u32[]{:S(2)}, u32[]{:S(2)}) collective-permute-start(bf16[3,256,768]{2,1,0:T(8,128)(2,1)} %bitcast.60), channel_id=1, source_target_pairs={{0,32},{32,64},{64,96},{96,0},{1,33},{33,65},{65,97},{97,1},{2,34}... | collective-permute-start | bytes 3538952 | tf_op jit(solution)/shard_map/ppermute | solution.py:703
  135.8 28.8 %collective-permute-start.1 = (bf16[3,256,768]{2,1,0:T(8,128)(2,1)}, bf16[3,256,768]{2,1,0:T(8,128)(2,1)S(1)}, u32[]{:S(2)}, u32[]{:S(2)}) collective-permute-start(bf16[3,256,768]{2,1,0:T(8,128)(2,1)} %bitcast.61), channel_id=1, source_target_pairs={{0,96},{32,0},{64,32},{96,64},{1,97},{33,1},{65,33},{97,65},{2,98}... | collective-permute-start | bytes 3538952 | tf_op jit(solution)/shard_map/ppermute | solution.py:704
  164.6 1.0 copy-start
  164.6 1.4 copy-start.1
  239.0 5.8 %slice-start = ((s8[4718592]{0:T(1024)(128)(4,1)}), s8[4194304]{0:T(1024)(128)(4,1)S(1)}, s32[]{:S(2)}) async-start(s8[4718592]{0:T(1024)(128)(4,1)} %bitcast.52), calls=%async_computation | async-start | bytes 8388608
  239.6 5.2 %slice-start.1 = ((s8[4718592]{0:T(1024)(128)(4,1)}), s8[524288]{0:T(1024)(128)(4,1)S(1)}, s32[]{:S(2)}) async-start(s8[4718592]{0:T(1024)(128)(4,1)} %bitcast.52), calls=%async_computation.1 | async-start | bytes 1048576

commit v5 on v4

--- a/solution.py
+++ b/solution.py
@@ -1,3 +1,4 @@
+import numpy as np
 import jax
 import jax.numpy as jnp
 from jax import lax
@@ -17,7 +18,7 @@
 MESH_ID = pl.DeviceIdType.MESH
 
 
-def gather_kernel(p_ref, g_ref, hold, lsem, s1, r1, s2, r2, s3, r3, ds, dr):
+def gather_kernel(wg_ref, wq_ref, wo_ref, wu_ref, wd_ref, wk_ref, wv_ref, gain_ref, g_ref, hold, lsem, s1, r1, s2, r2, s3, r3, ds, dr):
     t = lax.axis_index('tp')
     f = lax.axis_index('fsdp')
     c = lax.rem(f, N2)
@@ -37,9 +38,29 @@
     greeted = [partner] + [peer(axis, d) for axis in 'xyz' for d in (N1, N2, N3)]
     for who in greeted:
         pl.semaphore_signal(barrier, inc=N1, device_id=who, device_id_type=MESH_ID)
-    own = pltpu.make_async_copy(p_ref, hold, lsem.at[N0])
+    f32 = jnp.float32
+    bf16 = jnp.bfloat16
+    rows = wg_ref.shape[N0]
+    lane = lax.broadcasted_iota(jnp.int32, (rows, LANES), N1)
+    kv = jnp.concatenate([wk_ref[ALL].astype(f32), wv_ref[ALL].astype(f32)], axis=N1)
+    kv = pltpu.roll(kv, lax.rem(LANES - 32 * t, LANES), N1)
+    diag = lax.broadcasted_iota(jnp.int32, (rows, rows), N0) == lax.broadcasted_iota(jnp.int32, (rows, rows), N1)
+    gain = jnp.sum(jnp.where(diag, jnp.broadcast_to(gain_ref[ALL], (rows, rows)), 0.0), axis=N1, keepdims=True)
+    gain_hi = gain.astype(bf16).astype(f32)
+    gain_mid = (gain - gain_hi).astype(bf16).astype(f32)
+    gain_lo = gain - gain_hi - gain_mid
+    small = jnp.where(lane < 32, kv, jnp.where(lane == 32, gain_hi, jnp.where(lane == 33, gain_mid, jnp.where(lane == 34, gain_lo, 0.0))))
+    middle = jnp.concatenate([wq_ref[ALL].astype(f32), wo_ref[ALL].astype(f32), small], axis=N1)
+    for n in range(N3):
+        at_rows = slice(SUB * n, SUB * n + SUB)
+        hold[N0, n, :, N0:768] = wg_ref[at_rows, :]
+        hold[N0, n, :, 768:1280] = middle[at_rows].astype(bf16)
+        hold[N0, n, :, 1280:1408] = wd_ref[at_rows, N0:LANES]
+        hold[N1, n, :, N0:768] = wu_ref[at_rows, :]
+        hold[N1, n, :, 768:1408] = wd_ref[at_rows, LANES:768]
+    pl.semaphore_wait(barrier, len(greeted))
+    own = pltpu.make_async_copy(hold, g_ref.at[:, at['x'], at['z'], at['y'], c], lsem.at[N0])
     own.start()
-    pl.semaphore_wait(barrier, len(greeted))
 
     sent = []
 
@@ -51,85 +72,84 @@
     def landed(ref, s_sem, r_sem):
         pltpu.make_async_remote_copy(src_ref=ref, dst_ref=ref, send_sem=s_sem, recv_sem=r_sem, device_id=partner, device_id_type=MESH_ID).wait_recv()
 
-    def view(k, h, fixed, core):
+    parts = (pl.ds(N0, 768), pl.ds(768, 640))
+
+    def view(k, h, fixed, core, cols=None):
         spot = [fixed.get(axis, slice(None)) for axis in 'xzy']
-        return g_ref.at[h, spot[N0], spot[N1], spot[N2], core, k]
+        block = g_ref.at[h, spot[N0], spot[N1], spot[N2], core, k]
+        return block if cols is None else g_ref.at[h, spot[N0], spot[N1], spot[N2], core, k, slice(None), cols]
 
     orders = ('xyz', 'yzx', 'zxy')
-    both = slice(None)
     across = []
 
-    def share(k, h, fixed, n):
-        push(view(k, h, fixed, c), view(k, h, fixed, c), ds.at[k, n], dr.at[k, n], partner)
-        across.append((k, h, fixed, n))
-
-    def ring_start(k, axis, fixed, ss, rr):
+    def share(k, h, fixed, cols, n):
+        push(view(k, h, fixed, c, cols), view(k, h, fixed, c, cols), ds.at[k, h, n], dr.at[k, h, n], partner)
+        across.append((k, h, fixed, cols, n))
+
+    def ring_start(k, h, axis, fixed, ss, rr):
         here = {**fixed, axis: at[axis]}
         for n in range(N2):
-            push(view(k, n, here, c), view(k, n, here, c), ss.at[k, n], rr.at[k, n], peer(axis, N1))
-            push(view(k, N1 - n, here, c), view(k, N1 - n, here, c), ss.at[k, N3 - n], rr.at[k, N3 - n], peer(axis, N3))
-
-    def ring_forward(k, axis, fixed, ss, rr):
-        for h, d, n in ((N0, N3, N0), (N1, N1, N3)):
-            there = {**fixed, axis: up(at[axis], d)}
-            landed(view(k, h, there, c), ss.at[k, n], rr.at[k, n])
-            push(view(k, h, there, c), view(k, h, there, c), ss.at[k, RING + h], rr.at[k, RING + h], peer(axis, RING - d))
-
-    def ring_share(k, axis, fixed, ss, rr, base):
-        for m, (h, d, n) in enumerate(((N0, N3, N0), (N1, N1, N3), (N1, N3, N1), (N0, N1, N2), (N0, N2, RING), (N1, N2, 5))):
+            ref = view(k, h, here, c, parts[n])
+            push(ref, ref, ss.at[k, h, n], rr.at[k, h, n], peer(axis, N1))
+            ref = view(k, h, here, c, parts[N1 - n])
+            push(ref, ref, ss.at[k, h, N3 - n], rr.at[k, h, N3 - n], peer(axis, N3))
+
+    def ring_forward(k, h, axis, fixed, ss, rr):
+        for p, d, n in ((N0, N3, N0), (N1, N1, N3)):
+            ref = view(k, h, {**fixed, axis: up(at[axis], d)}, c, parts[p])
+            landed(ref, ss.at[k, h, n], rr.at[k, h, n])
+            push(ref, ref, ss.at[k, h, RING + p], rr.at[k, h, RING + p], peer(axis, RING - d))
+
+    def ring_share(k, h, axis, fixed, ss, rr, base):
+        for m, (p, d, n) in enumerate(((N0, N3, N0), (N1, N1, N3), (N1, N3, N1), (N0, N1, N2), (N0, N2, RING), (N1, N2, 5))):
             there = {**fixed, axis: up(at[axis], d)}
             if n not in (N0, N3):
-                landed(view(k, h, there, c), ss.at[k, n], rr.at[k, n])
-            share(k, h, there, base + m)
-
+                landed(view(k, h, there, c, parts[p]), ss.at[k, h, n], rr.at[k, h, n])
+            share(k, h, there, parts[p], base + m)
+
+    streams = [(k, h) for h in range(N2) for k in range(N3)]
+    for k, h in streams:
+        for d in (N1, N3, N2):
+            push(hold.at[h, k], view(k, h, at, c), s1.at[k, h, d - N1], r1.at[k, h, d - N1], peer(orders[k][N0], d))
     own.wait()
-    own = pltpu.make_async_copy(hold, g_ref.at[:, at['x'], at['z'], at['y'], c], lsem.at[N0])
-    own.start()
-    for k, order in enumerate(orders):
+    second = {}
+    third = {}
+    for k, h in streams:
+        order = orders[k]
         for d in (N1, N3, N2):
-            push(hold.at[:, k], view(k, both, at, c), s1.at[k, d - N1], r1.at[k, d - N1], peer(order[N0], d))
-    own.wait()
-    second = []
-    third = []
-    for k, order in enumerate(orders):
-        for d in (N1, N3, N2):
-            landed(view(k, both, {**at, order[N0]: up(at[order[N0]], RING - d)}, c), s1.at[k, d - N1], r1.at[k, d - N1])
-        fixed = {order[N2]: at[order[N2]]}
-        second.append((k, order[N1], fixed, s2, r2))
-        third.append((k, order[N2], {}, s3, r3))
-        ring_start(*second[k])
-    for k, order in enumerate(orders):
-        here = {order[N1]: at[order[N1]], order[N2]: at[order[N2]]}
-        share(k, N0, here, N0)
-        share(k, N1, here, N1)
-    for k in range(N3):
-        ring_forward(*second[k])
-    for k in range(N3):
-        ring_share(*second[k], N2)
-        ring_start(*third[k])
-    for k in range(N3):
-        ring_forward(*third[k])
-    for k in range(N3):
-        ring_share(*third[k], SUB)
-    for k, h, fixed, n in across:
-        landed(view(k, h, fixed, N1 - c), ds.at[k, n], dr.at[k, n])
+            landed(view(k, h, {**at, order[N0]: up(at[order[N0]], RING - d)}, c), s1.at[k, h, d - N1], r1.at[k, h, d - N1])
+        second[k, h] = (k, h, order[N1], {order[N2]: at[order[N2]]}, s2, r2)
+        third[k, h] = (k, h, order[N2], {}, s3, r3)
+        ring_start(*second[k, h])
+        share(k, h, {order[N1]: at[order[N1]], order[N2]: at[order[N2]]}, None, N0)
+    for stream in streams:
+        ring_forward(*second[stream])
+    for stream in streams:
+        ring_share(*second[stream], N1)
+        ring_start(*third[stream])
+    for stream in streams:
+        ring_forward(*third[stream])
+    for stream in streams:
+        ring_share(*third[stream], 7)
+    for k, h, fixed, cols, n in across:
+        landed(view(k, h, fixed, N1 - c, cols), ds.at[k, h, n], dr.at[k, h, n])
     for copy in sent:
         copy.wait_send()
 
 
-def gather_weights(packed):
+def gather_weights(w_gate, w_q, w_o, w_up, w_down, w_k, w_v, gain):
     dma = pltpu.SemaphoreType.DMA
-    any_spec = pl.BlockSpec(memory_space=pl.ANY)
-    wide = packed.shape[N2]
+    rows = w_gate.shape[N0]
+    vmem = pl.BlockSpec(memory_space=pltpu.VMEM)
     return pl.pallas_call(
         gather_kernel,
         name='gather_weights',
-        out_shape=jax.ShapeDtypeStruct((N2, RING, RING, RING, N2, N3, SUB, wide), packed.dtype),
-        in_specs=[any_spec],
-        out_specs=any_spec,
-        scratch_shapes=[pltpu.VMEM((N2, N3, SUB, wide), packed.dtype), dma((N1,)), dma((N3, N3)), dma((N3, N3)), dma((N3, 6)), dma((N3, 6)), dma((N3, 6)), dma((N3, 6)), dma((N3, 14)), dma((N3, 14))],
+        out_shape=jax.ShapeDtypeStruct((N2, RING, RING, RING, N2, N3, SUB, 1408), w_gate.dtype),
+        in_specs=[vmem] * SUB,
+        out_specs=pl.BlockSpec(memory_space=pl.ANY),
+        scratch_shapes=[pltpu.VMEM((N2, N3, SUB, 1408), w_gate.dtype), dma((N1,))] + [dma((N3, N2, N3))] * N2 + [dma((N3, N2, 6))] * RING + [dma((N3, N2, 13))] * N2,
         compiler_params=pltpu.CompilerParams(collective_id=N2, has_side_effects=True, vmem_limit_bytes=60 * KIB * KIB),
-    )(packed.reshape(N2, N3, SUB, wide))
+    )(w_gate, w_q, w_o.T, w_up, w_down.T, w_k, w_v, gain.reshape(N1, rows))
 
 
 NT = (((N1,), (N1,)), ((), ()))
@@ -146,7 +166,7 @@
         out[lax.rem(n % N2 + core, N2), 24 * (n // N2):24 * (n // N2) + 24, cols] = vals[24 * n:24 * n + 24]
 
 
-def proj_kernel(who_ref, x_ref, dy_ref, gain_ref, w0_ref, w1_ref, wkv_ref, ht_out, dyt_out, q_out, kv_out, do_out, act_out, dg_out, du_out, h_out):
+def proj_kernel(who_ref, x_ref, dy_ref, w0_ref, w1_ref, small_ref, gain_ref, wkv_ref, ht_out, dyt_out, q_out, kv_out, do_out, act_out, dg_out, du_out, h_out):
     f32 = jnp.float32
     bf16 = jnp.bfloat16
     tokens, width = h_out.shape
@@ -154,6 +174,14 @@
 
     @pl.when(pl.program_id(N0) == N0)
     def _():
+        lane = lax.broadcasted_iota(jnp.int32, (width, LANES), N1)
+        first = small_ref[N0, N0].astype(f32)
+        w_kv = jnp.where(lane < 32, first, 0.0)
+        for n in range(N1, RING):
+            w_kv += pltpu.roll(jnp.where(lane < 32, small_ref[N0, n].astype(f32), 0.0), 32 * n, N1)
+        wkv_ref[ALL] = w_kv.astype(bf16)
+        parts = first.T
+        gain_ref[ALL] = (parts[32:33] + parts[33:34]) + parts[34:35]
         for n in range(tokens // LANES):
             at = slice(n * LANES, n * LANES + LANES)
             seq, row = divmod(n * LANES, x_ref.shape[N1])
@@ -185,14 +213,14 @@
     do_out[N0] = dot(dy_tok, w0_ref[N0, N0, :, 896:1152]).astype(bf16)
 
 
-def att_kernel(q_ref, kv_ref, do_ref, cq_ref, sq_ref, ck_ref, sk_ref, o_out, dq_out, dkv_out, dk_lo, dk_hi, dv_lo, dv_hi):
+def att_kernel(q_ref, kv_ref, do_ref, cq_ref, sq_ref, ck_ref, sk_ref, cqt_ref, sqt_ref, swap_ref, o_out, dq_out, dkv_out, dk_lo, dk_hi, dv_lo, dv_hi):
     f32 = jnp.float32
     bf16 = jnp.bfloat16
     seq_len = kv_ref.shape[N0]
     lane = lax.broadcasted_iota(jnp.int32, (seq_len, LANES), N1)
     low = lane < 64
     first = lax.rem(lane, 64) < 32
-    causal = lax.broadcasted_iota(jnp.int32, (seq_len, seq_len), N0) >= lax.broadcasted_iota(jnp.int32, (seq_len, seq_len), N1)
+    causal = lax.broadcasted_iota(jnp.int32, (seq_len, seq_len), N0) <= lax.broadcasted_iota(jnp.int32, (seq_len, seq_len), N1)
 
     def other(vals):
         return jnp.where(first, pltpu.roll(vals, 96, N1), pltpu.roll(vals, 32, N1))
@@ -202,43 +230,45 @@
     zero = jnp.zeros_like(kv_rot)
     k_lo = jnp.where(low, kv_rot, zero)
     v_hi = jnp.where(low, zero, kv_rot)
-    k_hi = pltpu.roll(k_lo, 64, N1).astype(bf16)
-    v_lo = pltpu.roll(v_hi, 64, N1).astype(bf16)
-    k_lo = k_lo.astype(bf16)
-    v_hi = v_hi.astype(bf16)
+    k_hi = pltpu.roll(k_lo, 64, N1)
+    v_lo = pltpu.roll(v_hi, 64, N1)
+    k_cols = jnp.concatenate([k_lo.T, k_hi.T], axis=N1).astype(bf16)
+    v_cols = jnp.concatenate([v_lo.T, v_hi.T], axis=N1).astype(bf16)
+    k_lo, k_hi, v_lo, v_hi = (vals.astype(bf16) for vals in (k_lo, k_hi, v_lo, v_hi))
     for ref in (dk_lo, dk_hi, dv_lo, dv_hi):
         ref[ALL] = jnp.zeros_like(ref)
 
     def head(q_tile, k_part, v_part, do_tile):
-        scores = jnp.where(causal, dot(q_tile, k_part, NT), -1e30)
-        exp_val = jnp.exp(scores - jnp.max(scores, axis=-N1, keepdims=True))
-        prob = exp_val * (1.0 / jnp.sum(exp_val, axis=-N1, keepdims=True))
-        d_prob = dot(do_tile, v_part, NT).astype(bf16).astype(f32)
-        d_score = prob * (d_prob - jnp.sum(d_prob * prob, axis=-N1, keepdims=True))
+        scores = jnp.where(causal, dot(k_part, q_tile, NT), -1e30)
+        exp_val = jnp.exp(scores - jnp.max(scores, axis=N0, keepdims=True))
+        prob = exp_val * (1.0 / jnp.sum(exp_val, axis=N0, keepdims=True))
+        d_prob = dot(v_part, do_tile, NT).astype(bf16).astype(f32)
+        d_score = prob * (d_prob - jnp.sum(d_prob * prob, axis=N0, keepdims=True))
         return prob.astype(bf16), d_score.astype(bf16)
 
     def block(tt, carry):
         tiles = []
         for n in range(N2):
             cols = slice(n * LANES, n * LANES + LANES)
-            vals = q_ref[tt, :, cols].astype(f32)
-            tiles.append(((vals * cq_ref[ALL] + other(vals) * sq_ref[ALL]) * 0.125).astype(bf16))
+            vals = q_ref[tt, :, cols]
+            tiles.append(((vals.astype(f32) * cq_ref[ALL] + dot(vals, swap_ref[ALL]) * sq_ref[ALL]) * 0.125).astype(bf16))
         do0 = do_ref[tt, :, N0:LANES]
         do1 = do_ref[tt, :, LANES:PAIR]
         p0, s0 = head(tiles[N0], k_lo, v_hi, do0)
         p1, s1 = head(tiles[N0], k_hi, v_lo, do1)
         p2, s2 = head(tiles[N1], k_lo, v_hi, do1)
-        o_out[tt, :, N0:LANES] = dot(p0, v_hi).astype(bf16)
-        o_out[tt, :, LANES:PAIR] = (dot(p1, v_lo) + dot(p2, v_hi)).astype(bf16)
-        dv_hi[ALL] += dot(p0, do0, TN) + dot(p2, do1, TN)
-        dv_lo[ALL] += dot(p1, do1, TN)
-        dk_lo[ALL] += dot(s0, tiles[N0], TN) + dot(s2, tiles[N1], TN)
-        dk_hi[ALL] += dot(s1, tiles[N0], TN)
-        for n, grad in ((N0, dot(s0, k_lo) + dot(s1, k_hi)), (N1, dot(s2, k_lo))):
+        o_out[tt, :, N0:LANES] = dot(v_cols[:, PAIR:512], p0).T.astype(bf16)
+        o_out[tt, :, LANES:PAIR] = dot(v_cols, jnp.concatenate([p1, p2], axis=N0)).T.astype(bf16)
+        dv_hi[ALL] += dot(jnp.concatenate([p0, p2], axis=N1), jnp.concatenate([do0, do1], axis=N0))
+        dv_lo[ALL] += dot(p1, do1)
+        dk_lo[ALL] += dot(jnp.concatenate([s0, s2], axis=N1), jnp.concatenate(tiles, axis=N0))
+        dk_hi[ALL] += dot(s1, tiles[N0])
+        for n, grad in ((N0, dot(k_cols, jnp.concatenate([s0, s1], axis=N0))), (N1, dot(k_cols[:, N0:PAIR], s2))):
             grad = grad.astype(bf16).astype(f32) * 0.125
-            dq_out[tt, :, n * LANES:n * LANES + LANES] = (grad * cq_ref[ALL] - other(grad) * sq_ref[ALL]).astype(bf16)
+            swapped = jnp.concatenate([grad[32:64], grad[N0:32], grad[96:LANES], grad[64:96]], axis=N0)
+            dq_out[tt, :, n * LANES:n * LANES + LANES] = (grad * cqt_ref[ALL] - swapped * sqt_ref[ALL]).T.astype(bf16)
         return carry
-    lax.fori_loop(N0, q_ref.shape[N0], block, N0)
+    lax.fori_loop(N0, q_ref.shape[N0], block, N0, unroll=True)
     dk = (dk_lo[ALL] + pltpu.roll(dk_hi[ALL], 64, N1)).astype(bf16).astype(f32)
     dk_raw = dk * ck_ref[ALL] - other(dk) * sk_ref[ALL]
     dv = dv_hi[ALL] + pltpu.roll(dv_lo[ALL], 64, N1)
@@ -316,7 +346,7 @@
         put(N1, slice(lo + 640, hi + 640), dot(dyt, act_ref[N0, :, lo:hi]))
 
 
-def layer_step(x_in, dy_in, gain_row, w_full, w_kv, tables, who, seq_len):
+def layer_step(x_in, dy_in, w_full, tables, who, seq_len):
     f32 = jnp.float32
     bf16 = jnp.bfloat16
     n_tp = w_full.shape[N1]
@@ -344,23 +374,24 @@
     class_t = jax.ShapeDtypeStruct((N2, half, tokens), bf16)
     kv_t = jax.ShapeDtypeStruct((tokens, LANES), bf16)
     work = pl.CostEstimate(flops=13 * 10**9, bytes_accessed=40 * 10**6, transcendentals=N0)
-    h_t, dy_t, q_raw, kv_raw, d_o, act, d_gate, d_up = pl.pallas_call(
+    small = pl.BlockSpec((N1, n_tp, width, LANES), lambda i, *_: (N0, N0, N0, KV_AT // LANES))
+    gain_row, w_kv, h_t, dy_t, q_raw, kv_raw, d_o, act, d_gate, d_up = pl.pallas_call(
         proj_kernel, name='proj',
         grid_spec=pltpu.PrefetchScalarGridSpec(
             num_scalar_prefetch=N1, grid=(n_tp,),
-            in_specs=[mine, mine, whole((N1, width)), w0_spec, w1_spec, whole((width, LANES))],
-            out_specs=(classes, classes, per((tokens, PAIR)), whole((tokens, LANES)), per((tokens, PAIR)), per((tokens, width)), per((tokens, width)), per((tokens, width))),
+            in_specs=[mine, mine, w0_spec, w1_spec, small],
+            out_specs=(whole((N1, width)), whole((width, LANES)), classes, classes, per((tokens, PAIR)), whole((tokens, LANES)), per((tokens, PAIR)), per((tokens, width)), per((tokens, width)), per((tokens, width))),
             scratch_shapes=[pltpu.VMEM((tokens, width), bf16)]),
-        out_shape=(class_t, class_t, pair_t, kv_t, pair_t, wide_t, wide_t, wide_t),
+        out_shape=(jax.ShapeDtypeStruct((N1, width), f32), jax.ShapeDtypeStruct((width, LANES), bf16), class_t, class_t, pair_t, kv_t, pair_t, wide_t, wide_t, wide_t),
         compiler_params=params, cost_estimate=work,
-    )(who, x_in, dy_in, gain_row, w_full, w_full, w_kv)
+    )(who, x_in, dy_in, w_full, w_full, w_full)
 
     pair_spec = pl.BlockSpec((n_tp, seq_len, PAIR), lambda i: (N0, i, N0))
     kv_spec = pl.BlockSpec((seq_len, LANES), lambda i: (i, N0))
     table = whole((seq_len, LANES))
     att, d_q, d_kv = pl.pallas_call(
         att_kernel, name='attention', grid=(n_seq,),
-        in_specs=[pair_spec, kv_spec, pair_spec, table, table, table, table],
+        in_specs=[pair_spec, kv_spec, pair_spec, table, table, table, table, whole((LANES, seq_len)), whole((LANES, seq_len)), whole((LANES, LANES))],
         out_specs=(pair_spec, pair_spec, kv_spec),
         out_shape=(pair_t, pair_t, kv_t),
         scratch_shapes=[pltpu.VMEM((seq_len, LANES), f32)] * RING,
@@ -393,19 +424,19 @@
 
 
 def rope_tables(seq_len, head_dim):
-    f32 = jnp.float32
     half_dim = head_dim // N2
-    inv_freq = jnp.power(10000.0, -2.0 * jnp.arange(half_dim, dtype=f32) / head_dim)
-    angle = jnp.arange(seq_len, dtype=f32)[:, None] * inv_freq[None, :]
-    cos_t = jnp.cos(angle)
-    sin_t = jnp.sin(angle)
-    cos_h = jnp.concatenate([cos_t, cos_t], axis=N1)
-    sin_h = jnp.concatenate([-sin_t, sin_t], axis=N1)
-    cos_q = jnp.concatenate([cos_h, cos_h], axis=N1)
-    sin_q = jnp.concatenate([sin_h, sin_h], axis=N1)
-    cos_k = jnp.concatenate([cos_h, jnp.ones_like(cos_h)], axis=N1)
-    sin_k = jnp.concatenate([sin_h, jnp.zeros_like(sin_h)], axis=N1)
-    return cos_q, sin_q, cos_k, sin_k
+    inv_freq = np.power(np.float32(10000.0), (-2.0 * np.arange(half_dim) / head_dim).astype(np.float32))
+    angle = (np.arange(seq_len, dtype=np.float32)[:, None] * inv_freq[None, :]).astype(np.float32)
+    cos_t = np.cos(angle)
+    sin_t = np.sin(angle)
+    cos_h = np.concatenate([cos_t, cos_t], axis=N1)
+    sin_h = np.concatenate([-sin_t, sin_t], axis=N1)
+    cos_q = np.concatenate([cos_h, cos_h], axis=N1)
+    sin_q = np.concatenate([sin_h, sin_h], axis=N1)
+    cos_k = np.concatenate([cos_h, np.ones_like(cos_h)], axis=N1)
+    sin_k = np.concatenate([sin_h, np.zeros_like(sin_h)], axis=N1)
+    swap = np.eye(LANES)[np.arange(LANES) ^ 32]
+    return tuple(jnp.asarray(table, jnp.float32) for table in (cos_q, sin_q, cos_k, sin_k, cos_q.T, sin_q.T)) + (jnp.asarray(swap, jnp.bfloat16),)
 
 
 def sum_kernel(g_ref, gs_ref, gx_ref, y_ref, below_ref, above_ref, w_out, kv_out, gx_out, y_out, acc, rp, sa, ra1, ra2, sb, rb1, rb2, sc, rc, kvx, gsem, d2s, d2r, ss, rs, cs, cr, ks, kr, xs, xr, lsem, keep):
@@ -667,11 +698,8 @@
 
 def solution(mesh):
     n_tp = mesh.shape['tp']
-    n_fsdp = mesh.shape['fsdp']
 
     def device_step(x_in, dy_out, ln_gain, w_q, w_k, w_v, w_o, w_gate, w_up, w_down):
-        bf16 = jnp.bfloat16
-        f32 = jnp.float32
         n_batch, seq_len, width = x_in.shape
         head_dim = w_k.shape[N1]
         rows = w_q.shape[N0]
@@ -681,24 +709,11 @@
         mine = n_batch // n_tp
         tp = lax.axis_index('tp')
         core = lax.rem(lax.axis_index('fsdp'), N2)
-        gain_hi = lax.reduce_precision(ln_gain, SUB, 7)
-        gain_mid = lax.reduce_precision(ln_gain - gain_hi, SUB, 7)
-        gain_lo = ln_gain - gain_hi - gain_mid
-        gain_cols = jnp.stack([gain_hi, gain_mid, gain_lo], axis=N1).astype(bf16)
-        kv_mine = lax.dynamic_slice_in_dim(jnp.concatenate([w_k, w_v], axis=N1), tp * part, part, N1)
-        small = jnp.concatenate([kv_mine, gain_cols, jnp.zeros((rows, LANES - part - N3), bf16)], axis=N1)
-        down = w_down.T
-        packed = jnp.stack([jnp.concatenate([w_gate, w_q, w_o.T, small, down[:, :LANES]], axis=N1), jnp.concatenate([w_up, down[:, LANES:]], axis=N1)])
-        wide = packed.shape[N2]
+        full = gather_weights(w_gate, w_q, w_o, w_up, w_down, w_k, w_v, ln_gain).reshape(N2, n_tp, width, -N1)
+        wide = full.shape[N3]
         tables = rope_tables(seq_len, head_dim)
-        full = gather_weights(packed).reshape(N2, n_tp, width, wide)
-        small_full = full[N0, :, :, KV_AT:KV_AT + LANES]
-        w_kv = jnp.concatenate([small_full[n, :, :part] for n in range(n_tp)], axis=N1)
-        gain3 = small_full[N0, :, part:part + N3].astype(f32)
-        gain_row = (gain3[:, N0] + gain3[:, N1] + gain3[:, N2]).reshape(N1, width)
-
         who = jnp.stack([tp, core]).astype(jnp.int32)
-        y_tok, gx_tok, g_own, g_oth = layer_step(x_in, dy_out, gain_row, full, w_kv, tables, who, seq_len)
+        y_tok, gx_tok, g_own, g_oth = layer_step(x_in, dy_out, full, tables, who, seq_len)
         y_my = y_tok.reshape(mine, seq_len, width)
         below = lax.ppermute(y_my, 'tp', [(n, (n + N1) % n_tp) for n in range(n_tp)])
         above = lax.ppermute(y_my, 'tp', [(n, (n - N1) % n_tp) for n in range(n_tp)])

time: 248 us -> 234 us (0.944)
  other arithmetic: 7.18 us -> 1.22 us
  local copies, waits for them, and re-layouts: 19.3 us -> 14.7 us
  Pallas kernels: 214 us -> 210 us
    pallas_call x1, Pallas kernels: 19.8 us -> 14.5 us  [layer_step(): pl.pallas_call(att_kernel, name='attention', grid=(n_seq,), in_specs=[pai...]
    concatenate x3 -> x0, other arithmetic: 2.79 us -> none  [the longest x1 1.04 us: rope_tables(): cos_k = jnp.concatenate([cos_h, jnp.ones_like(cos_h)], axis=N1)]
where the time goes in v5:
time: 234 us; the launch traced here: 233 us
  Pallas kernels  210 us (90%)
  local copies, waits for them, and re-layouts  14.7 us (6%)
  starting transfers between devices  3.24 us (1%)
  waiting for transfers between devices  2.78 us (1%)
    pallas_call x1, Pallas kernels, sum_grads(): pl.pallas_call(sum_kernel, name='sum_grads', out_shape=(jax.ShapeDtypeStr...  67.9 us
    pallas_call x1, Pallas kernels, gather_weights(): pl.pallas_call(gather_kernel, name='gather_weights', out_shape=jax.ShapeD...  52.8 us
    pallas_call x1, Pallas kernels, layer_step(): pl.pallas_call(back_kernel, name='back', grid_spec=pltpu.PrefetchScalarGr...  26.4 us
    pallas_call x1, Pallas kernels, layer_step(): pl.pallas_call(proj_kernel, name='proj', grid_spec=pltpu.PrefetchScalarGr...  25.1 us
    pallas_call x1, Pallas kernels, layer_step(): pl.pallas_call(wgrad_kernel, name='wgrad', grid=(n_tp,), in_specs=[classe...  23.7 us
    pallas_call x1, Pallas kernels, layer_step(): pl.pallas_call(att_kernel, name='attention', grid=(n_seq,), in_specs=[pai...  14.5 us
    unnamed x11, local copies, waits for them, and re-layouts  9.34 us
  transfers between devices with their start and end apart: 2, of which 1 were waited for; matrix products, arithmetic and copies ran while one was open for 0% of the time, Pallas kernels for 10%

profile of v5, /device:TPU:0, one launch (start us, length us, event | category | flops | bytes accessed | tf_op | source)
XLA Modules:
  0.0 233.0 jit_solution(4371855433782481462)
XLA Ops:
  0.6 0.6 pad_add_fusion.who_ref
  1.2 52.8 %gather_weights.1 = bf16[2,4,4,4,2,3,8,1408]{7,6,5,4,3,2,1,0:T(8,128)(2,1)} custom-call(bf16[24,768]{1,0:T(8,128)(2,1)} %wg_ref.1, bf16[24,192]{1,0:T(8,128)(2,1)} %wq_ref.1, bf16[24,192]{1,0:T(8,128)(2,1)} %bitcast.33, bf16[24,768]{1,0:T(8,128)(2,1)} %wu_ref.1, bf16[24,768]{1,0:T(8,128)(2,1)} %bitcast.32, bf16[24,64]{1,0:T(8,128)(2,1)} %wk_ref.1, ...), custom_call_target="tpu_custom_call" | custom-call | tf_op jit(solution)/shard_map/gather_weights/pallas_call | solution.py:144
  54.1 25.1 %proj.1 = (f32[1,768]{1,0:T(1,128)}, bf16[768,128]{1,0:T(8,128)(2,1)}, bf16[2,384,768]{2,1,0:T(8,128)(2,1)}, bf16[2,384,768]{2,1,0:T(8,128)(2,1)}, bf16[4,768,25...) custom-call(s32[2]{0:T(128)} %pad_add_fusion.who_ref, ...), custom_call_target="tpu_custom_call" | custom-call | flops 12999999488 | bytes 40000000 | tf_op jit(solution)/shard_map/proj/pallas_call | solution.py:378
  79.2 14.5 %attention.1 = (bf16[4,768,256]{2,1,0:T(8,128)(2,1)}, bf16[4,768,256]{2,1,0:T(8,128)(2,1)}, bf16[768,128]{1,0:T(8,128)(2,1)}) custom-call(bf16[4,768,256]{2,1,0:T(8,128)(2,1)} %get-tuple-element.36.q_ref, bf16[768,128]{1,0:T(8,128)(2,1)} %get-tuple-element.37.kv_ref, bf16[4,768,256]{2,1,0:T(8,128)(2,1)} %get-tuple-element.38.do_ref, ...), custom_call_target="tpu_custom_call" | custom-call | flops 12999999488 | bytes 40000000 | tf_op jit(solution)/shard_map/attention/pallas_call | solution.py:392
  93.7 26.4 %back.1 = (bf16[768,768]{1,0:T(8,128)(2,1)}, bf16[768,768]{1,0:T(8,128)(2,1)}, f32[2,384,128]{2,1,0:T(8,128)}) custom-call(s32[2]{0:T(128)} %pad_add_fusion.who_ref, bf16[12,256,768]{2,1,0:T(8,128)(2,1)} %x_ref.3, bf16[12,256,768]{2,1,0:T(8,128)(2,1)} %dy_ref.3, f32[1,768]{1,0:T(1,128)} %get-tuple-element.34.gain_ref, bf16[2,4,768,1408]{3,2,1,0:T(8,128)(2,1)} %bitcast.27, ...), custom_call_target="tpu_custom_call" | custom-call | flops 12999999488 | bytes 40000000 | tf_op jit(solution)/shard_map/back/pallas_call | solution.py:402
  120.1 1.0 collective-permute-start
  121.1 2.2 collective-permute-start.1
  123.3 23.7 %wgrad.1 = (f32[2,4,384,1408]{3,2,1,0:T(8,128)}, bf16[2,4,384,1408]{3,2,1,0:T(8,128)(2,1)}) custom-call(bf16[2,384,768]{2,1,0:T(8,128)(2,1)} %get-tuple-element.32.ht_ref, bf16[2,384,768]{2,1,0:T(8,128)(2,1)} %get-tuple-element.33.dyt_ref, f32[2,384,128]{2,1,0:T(8,128)} %get-tuple-element.45.gcol_ref, bf16[4,768,256]{2,1,0:T(8,128)(2,1)} %get-tuple-element.39.o_ref, ...), custom_call_target="tpu_custom_call" | custom-call | flops 12999999488 | bytes 40000000 | tf_op jit(solution)/shard_map/wgrad/pallas_call | solution.py:415
  147.0 2.8 %collective-permute-done.below_ref = bf16[3,256,768]{2,1,0:T(8,128)(2,1)S(1)} collective-permute-done((bf16[3,256,768]{2,1,0:T(8,128)(2,1)}, bf16[3,256,768]{2,1,0:T(8,128)(2,1)S(1)}, u32[]{:S(2)}, u32[]{:S(2)}) %collective-permute-start) | collective-permute-done | bytes 1179680 | tf_op jit(solution)/shard_map/ppermute | solution.py:718
  149.8 0.0 copy-start
  149.8 0.0 collective-permute-done.1.above_ref
  149.8 0.0 copy-start.1
  149.8 1.0 copy-done
  150.8 0.4 copy-done.1
  151.2 67.9 %sum_grads.1 = (f32[2,3,8,1408]{3,2,1,0:T(8,128)}, f32[4,3,8,128]{3,2,1,0:T(8,128)}, bf16[12,256,768]{2,1,0:T(8,128)(2,1)}, bf16[12,256,768]{2,1,0:T(8,128)(2,1)}) custom-call(f32[2,4,4,4,3,8,1408]{6,5,4,3,2,1,0:T(8,128)} %bitcast.40, bf16[2,4,4,4,3,8,1408]{6,5,4,3,2,1,0:T(8,128)(2,1)} %bitcast.41, bf16[3,256,768]{2,1,0:T(8,128)(2,1)} %bitcast.39, ...), custom_call_target="tpu_custom_call" | custom-call | flops 60000002048 | bytes 30000000 | tf_op jit(solution)/shard_map/sum_grads/pallas_call | solution.py:680
  219.1 1.0 slice_bitcast_fusion
  220.1 0.6 slice.58
  220.7 0.6 slice.59
  221.4 0.7 slice_bitcast_fusion.3
  222.0 0.7 slice_bitcast_fusion.4
  222.7 0.8 slice_bitcast_fusion.2
  223.6 0.1 reshape.51
  223.7 0.7 fusion
  224.3 0.1 slice.52
  224.4 0.6 copy.29
  225.0 0.0 slice-start
  225.0 0.6 maximum_bitcast_fusion
  225.6 0.0 slice-start.1
  225.6 5.2 %copy.32 = bf16[12,256,768]{2,1,0:T(8,128)(2,1)} copy(bf16[12,256,768]{2,1,0:T(8,128)(2,1)} %get-tuple-element.70) | data formatting | bytes 9437184
  230.8 0.0 slice-done
  230.8 0.0 slice-done.1
  230.8 2.2 copy.33
  (4 shorter events, 0.0 us)
Async XLA Ops:
  120.1 29.7 %collective-permute-start = (bf16[3,256,768]{2,1,0:T(8,128)(2,1)}, bf16[3,256,768]{2,1,0:T(8,128)(2,1)S(1)}, u32[]{:S(2)}, u32[]{:S(2)}) collective-permute-start(bf16[3,256,768]{2,1,0:T(8,128)(2,1)} %bitcast.36), channel_id=1, source_target_pairs={{0,32},{32,64},{64,96},{96,0},{1,33},{33,65},{65,97},{97,1},{2,34}... | collective-permute-start | bytes 3538952 | tf_op jit(solution)/shard_map/ppermute | solution.py:718
  121.1 28.7 %collective-permute-start.1 = (bf16[3,256,768]{2,1,0:T(8,128)(2,1)}, bf16[3,256,768]{2,1,0:T(8,128)(2,1)S(1)}, u32[]{:S(2)}, u32[]{:S(2)}) collective-permute-start(bf16[3,256,768]{2,1,0:T(8,128)(2,1)} %bitcast.37), channel_id=1, source_target_pairs={{0,96},{32,0},{64,32},{96,64},{1,97},{33,1},{65,33},{97,65},{2,98}... | collective-permute-start | bytes 3538952 | tf_op jit(solution)/shard_map/ppermute | solution.py:719
  149.8 1.0 copy-start
  149.8 1.4 copy-start.1
  225.0 5.8 %slice-start = ((s8[4718592]{0:T(1024)(128)(4,1)}), s8[4194304]{0:T(1024)(128)(4,1)S(1)}, s32[]{:S(2)}) async-start(s8[4718592]{0:T(1024)(128)(4,1)} %bitcast.29), calls=%async_computation | async-start | bytes 8388608
  225.6 5.2 %slice-start.1 = ((s8[4718592]{0:T(1024)(128)(4,1)}), s8[524288]{0:T(1024)(128)(4,1)S(1)}, s32[]{:S(2)}) async-start(s8[4718592]{0:T(1024)(128)(4,1)} %bitcast.29), calls=%async_computation.1 | async-start | bytes 1048576

commit v6 on v5

--- a/solution.py
+++ b/solution.py
@@ -503,9 +503,12 @@
     x_dn = rcopy(gx_ref, gx_out.at[my_rows], xs.at[N1], xr.at[N1], xp[N3])
     x_up.start()
     x_dn.start()
-    local = ((gx_ref, gx_out, my_rows), (y_ref, y_out, my_rows), (below_ref, y_out, lower), (above_ref, y_out, upper))
+    local = ((gx_ref, gx_out, my_rows), (y_ref, y_out, my_rows))
     taken = [pltpu.make_async_copy(ref, keep.at[n], lsem.at[n]) for n, (ref, _, _) in enumerate(local)]
     placed = [pltpu.make_async_copy(keep.at[n], out.at[place], lsem.at[n]) for n, (_, out, place) in enumerate(local)]
+    for n, (ref, place) in enumerate(((below_ref, lower), (above_ref, upper))):
+        placed.append(pltpu.make_async_copy(ref, y_out.at[place], lsem.at[n + N2]))
+        placed[n + N2].start()
     for copy in taken:
         copy.start()
 
@@ -562,7 +565,7 @@
                 sa[col, n, a2, tt, r] = val.astype(bf16)
             each(24, joined)
             send(sa.at[col, n, pl.ds(base, N2)], ra2.at[col, n - N1, pl.ds(base, N2)], ss.at[col, n + N3], rs.at[col, n + N3], dev_a[col][peer])
-    for n in range(RING):
+    for n in range(N2):
         taken[n].wait()
         placed[n].start()
     x_up.wait_recv()
@@ -682,18 +685,71 @@
         name='sum_grads',
         out_shape=(jax.ShapeDtypeStruct((N2, N3, SUB, wide), f32), jax.ShapeDtypeStruct((RING, N3, SUB, LANES), f32),
                    jax.ShapeDtypeStruct((n_batch,) + gx_my.shape[N1:], bf16), jax.ShapeDtypeStruct((n_batch,) + gx_my.shape[N1:], bf16)),
-        in_specs=[any_spec] * 6,
+        in_specs=[any_spec] * RING + [vmem] * N2,
         out_specs=(vmem, vmem, any_spec, any_spec),
         scratch_shapes=[
             pltpu.VMEM((N2, RING, RING, RING, N3, SUB, wide), f32), pltpu.VMEM((N2, RING, RING, RING, N3, SUB, wide), bf16),
             pltpu.VMEM((N2, N3, RING, RING, N3, SUB, wide), bf16), pltpu.VMEM((N2, N2, N2, RING, N3, SUB, wide), bf16), pltpu.VMEM((N2, N2, RING, RING, N3, SUB, wide), bf16),
             pltpu.VMEM((N2, N3, RING, N3, SUB, wide), bf16), pltpu.VMEM((N2, N2, N2, N3, SUB, wide), bf16), pltpu.VMEM((N2, N2, RING, N3, SUB, wide), bf16),
             pltpu.VMEM((N2, RING, N3, SUB, wide), bf16), pltpu.VMEM((N2, N3, N3, SUB, wide), bf16), pltpu.VMEM((RING, RING, N3, SUB, LANES), f32),
-            dma((N2, RING)), dma((N2, RING)), dma((N2, RING)), dma((N2, 12)), dma((N2, 12)), dma((N2, N3)), dma((N2, N3)), dma((N3,)), dma((N3,)), dma((6,)), dma((6,)), dma((RING,)), pltpu.VMEM((RING,) + gx_my.shape, bf16),
+            dma((N2, RING)), dma((N2, RING)), dma((N2, RING)), dma((N2, 12)), dma((N2, 12)), dma((N2, N3)), dma((N2, N3)), dma((N3,)), dma((N3,)), dma((6,)), dma((6,)), dma((RING,)), pltpu.VMEM((N2,) + gx_my.shape, bf16),
         ],
         cost_estimate=pl.CostEstimate(flops=60 * 10**9, bytes_accessed=30 * 10**6, transcendentals=N0),
         compiler_params=pltpu.CompilerParams(collective_id=N1, has_side_effects=True, vmem_limit_bytes=60 * KIB * KIB),
     )(g_pack, g_send, gx_my, *y_blocks)
+
+
+def finish_kernel(w_ref, kv_ref, y_ref, gx_ref, y_out, gx_out, gain_out, q_out, k_out, v_out, o_out, gate_out, up_out, down_out, buf, isem, osem):
+    n_batch = y_ref.shape[N0]
+    moves = [(ref, out, n) for ref, out in ((y_ref, y_out), (gx_ref, gx_out)) for n in range(n_batch)]
+    loads = [pltpu.make_async_copy(ref.at[n], buf.at[m], isem.at[m]) for m, (ref, _, n) in enumerate(moves)]
+    stores = [pltpu.make_async_copy(buf.at[m], out.at[n], osem.at[m]) for m, (_, out, n) in enumerate(moves)]
+    for copy in loads:
+        copy.start()
+    lane = lax.broadcasted_iota(jnp.int32, (SUB, LANES), N1)
+    gains = []
+    for r in range(N3):
+        at = slice(SUB * r, SUB * r + SUB)
+        gate_out[at, :] = w_ref[N0, r, :, N0:768]
+        up_out[at, :] = w_ref[N1, r, :, N0:768]
+        q_out[at, :] = w_ref[N0, r, :, 768:960]
+        o_out[at, :] = w_ref[N0, r, :, 960:1152]
+        down_out[at, N0:LANES] = w_ref[N0, r, :, 1280:1408]
+        down_out[at, LANES:768] = w_ref[N1, r, :, 768:1408]
+        kv = jnp.where(lane < 32, kv_ref[N0, r], 0.0)
+        for n in range(N1, RING):
+            kv += pltpu.roll(jnp.where(lane < 32, kv_ref[n, r], 0.0), 32 * n, N1)
+        k_out[at, :] = kv[:, N0:64]
+        v_out[at, :] = pltpu.roll(kv, 64, N1)[:, N0:64]
+        gains.append(jnp.sum(jnp.where(lane == 32, kv_ref[N0, r], 0.0), axis=N1, keepdims=True))
+    gain = jnp.concatenate(gains, axis=N0)
+    rows = gain.shape[N0]
+    diag = lax.broadcasted_iota(jnp.int32, (rows, rows), N0) == lax.broadcasted_iota(jnp.int32, (rows, rows), N1)
+    gain_out[ALL] = jnp.sum(jnp.where(diag, jnp.broadcast_to(gain, (rows, rows)), 0.0), axis=N0, keepdims=True)
+    for load, store in zip(loads, stores):
+        load.wait()
+        store.start()
+    for store in stores:
+        store.wait()
+
+
+def finish(w_sum, kv_sum, y_land, gx_land, rows, width, nq, head_dim):
+    f32 = jnp.float32
+    dma = pltpu.SemaphoreType.DMA
+    vmem = pl.BlockSpec(memory_space=pltpu.VMEM)
+    any_spec = pl.BlockSpec(memory_space=pl.ANY)
+    act_t = jax.ShapeDtypeStruct(y_land.shape, y_land.dtype)
+    n_moves = N2 * y_land.shape[N0]
+    grads = [(N1, rows), (rows, nq), (rows, head_dim), (rows, head_dim), (rows, nq), (rows, width), (rows, width), (rows, width)]
+    return pl.pallas_call(
+        finish_kernel,
+        name='finish',
+        out_shape=[act_t, act_t] + [jax.ShapeDtypeStruct(shape, f32) for shape in grads],
+        in_specs=[vmem, vmem, any_spec, any_spec],
+        out_specs=[any_spec, any_spec] + [vmem] * SUB,
+        scratch_shapes=[pltpu.VMEM((n_moves,) + y_land.shape[N1:], y_land.dtype), dma((n_moves,)), dma((n_moves,))],
+        compiler_params=pltpu.CompilerParams(vmem_limit_bytes=56 * KIB * KIB),
+    )(w_sum, kv_sum, y_land, gx_land)
 
 
 def solution(mesh):
@@ -704,8 +760,6 @@
         head_dim = w_k.shape[N1]
         rows = w_q.shape[N0]
         nq = w_q.shape[N1]
-        nf = w_gate.shape[N1]
-        part = N2 * head_dim // n_tp
         mine = n_batch // n_tp
         tp = lax.axis_index('tp')
         core = lax.rem(lax.axis_index('fsdp'), N2)
@@ -718,19 +772,9 @@
         below = lax.ppermute(y_my, 'tp', [(n, (n + N1) % n_tp) for n in range(n_tp)])
         above = lax.ppermute(y_my, 'tp', [(n, (n - N1) % n_tp) for n in range(n_tp)])
         split = (N2, n_tp, RING, RING, N3, SUB, wide)
-        w_sum, kv_sum, grad_x, y_out = sum_grads(g_own.reshape(split), g_oth.reshape(split), gx_tok.reshape(mine, seq_len, width), (y_my, below, above), n_batch)
-        w0 = w_sum[N0].reshape(rows, wide)
-        w1 = w_sum[N1].reshape(rows, wide)
-        kv_all = jnp.swapaxes(kv_sum.reshape(n_tp, rows, LANES)[:, :, :part], N0, N1).reshape(rows, N2 * head_dim)
-        grad_wgate = w0[:, :nf]
-        grad_wq = w0[:, nf:nf + nq]
-        grad_wo = w0[:, nf + nq:nf + N2 * nq].T
-        grad_wdown = jnp.concatenate([w0[:, wide - LANES:], w1[:, nf:]], axis=N1).T
-        grad_wup = w1[:, :nf]
-        grad_wk = kv_all[:, :head_dim]
-        grad_wv = kv_all[:, head_dim:]
-        grad_gain = kv_sum[N0].reshape(rows, LANES)[:, part]
-        return (y_out, grad_x, grad_gain, grad_wq, grad_wk, grad_wv, grad_wo, grad_wgate, grad_wup, grad_wdown)
+        w_sum, kv_sum, gx_land, y_land = sum_grads(g_own.reshape(split), g_oth.reshape(split), gx_tok.reshape(mine, seq_len, width), (y_my, below, above), n_batch)
+        y_out, grad_x, gain, grad_wq, grad_wk, grad_wv, wo_t, grad_wgate, grad_wup, down_t = finish(w_sum, kv_sum, y_land, gx_land, rows, width, nq, head_dim)
+        return (y_out, grad_x, gain.reshape(rows), grad_wq, grad_wk, grad_wv, wo_t.T, grad_wgate, grad_wup, down_t.T)
 
     act_spec = P('fsdp', None, None)
     row_spec = P('fsdp', 'tp')

time: 234 us -> 231 us (0.987)
  local copies, waits for them, and re-layouts: 14.7 us -> 1.4 us
  Pallas kernels: 210 us -> 221 us
    pallas_call x0 -> x1, Pallas kernels: none -> 9.33 us  [finish(): pl.pallas_call(finish_kernel, name='finish', out_shape=[act_t, act_t] + [...]
    unnamed x11 -> x4, local copies, waits for them, and re-layouts: 9.34 us -> 1.4 us
where the time goes in v6:
time: 231 us; the launch traced here: 230 us
  Pallas kernels  221 us (96%)
  starting transfers between devices  3.24 us (1%)
  waiting for transfers between devices  2.88 us (1%)
    pallas_call x1, Pallas kernels, sum_grads(): pl.pallas_call(sum_kernel, name='sum_grads', out_shape=(jax.ShapeDtypeStr...  69.5 us
    pallas_call x1, Pallas kernels, gather_weights(): pl.pallas_call(gather_kernel, name='gather_weights', out_shape=jax.ShapeD...  52.8 us
    pallas_call x1, Pallas kernels, layer_step(): pl.pallas_call(back_kernel, name='back', grid_spec=pltpu.PrefetchScalarGr...  26.4 us
    pallas_call x1, Pallas kernels, layer_step(): pl.pallas_call(proj_kernel, name='proj', grid_spec=pltpu.PrefetchScalarGr...  25.1 us
    pallas_call x1, Pallas kernels, layer_step(): pl.pallas_call(wgrad_kernel, name='wgrad', grid=(n_tp,), in_specs=[classe...  23.6 us
    pallas_call x1, Pallas kernels, layer_step(): pl.pallas_call(att_kernel, name='attention', grid=(n_seq,), in_specs=[pai...  14.5 us
    pallas_call x1, Pallas kernels, finish(): pl.pallas_call(finish_kernel, name='finish', out_shape=[act_t, act_t] + [...  9.33 us
  transfers between devices with their start and end apart: 2, of which 1 were waited for; matrix products, arithmetic and copies ran while one was open for 0% of the time, Pallas kernels for 10%

profile of v6, /device:TPU:0, one launch (start us, length us, event | category | flops | bytes accessed | tf_op | source)
XLA Modules:
  0.0 230.3 jit_solution(9905197527152961781)
XLA Ops:
  0.6 0.6 pad_add_fusion.who_ref
  1.2 52.8 %gather_weights.1 = bf16[2,4,4,4,2,3,8,1408]{7,6,5,4,3,2,1,0:T(8,128)(2,1)} custom-call(bf16[24,768]{1,0:T(8,128)(2,1)} %wg_ref.1, bf16[24,192]{1,0:T(8,128)(2,1)} %wq_ref.1, bf16[24,192]{1,0:T(8,128)(2,1)} %bitcast.19, bf16[24,768]{1,0:T(8,128)(2,1)} %wu_ref.1, bf16[24,768]{1,0:T(8,128)(2,1)} %bitcast.18, bf16[24,64]{1,0:T(8,128)(2,1)} %wk_ref.1, ...), custom_call_target="tpu_custom_call" | custom-call | tf_op jit(solution)/shard_map/gather_weights/pallas_call | solution.py:144
  54.1 25.1 %proj.1 = (f32[1,768]{1,0:T(1,128)}, bf16[768,128]{1,0:T(8,128)(2,1)}, bf16[2,384,768]{2,1,0:T(8,128)(2,1)}, bf16[2,384,768]{2,1,0:T(8,128)(2,1)}, bf16[4,768,25...) custom-call(s32[2]{0:T(128)} %pad_add_fusion.who_ref, ...), custom_call_target="tpu_custom_call" | custom-call | flops 12999999488 | bytes 40000000 | tf_op jit(solution)/shard_map/proj/pallas_call | solution.py:378
  79.2 14.5 %attention.1 = (bf16[4,768,256]{2,1,0:T(8,128)(2,1)}, bf16[4,768,256]{2,1,0:T(8,128)(2,1)}, bf16[768,128]{1,0:T(8,128)(2,1)}) custom-call(bf16[4,768,256]{2,1,0:T(8,128)(2,1)} %get-tuple-element.46.q_ref, bf16[768,128]{1,0:T(8,128)(2,1)} %get-tuple-element.47.kv_ref, bf16[4,768,256]{2,1,0:T(8,128)(2,1)} %get-tuple-element.48.do_ref, ...), custom_call_target="tpu_custom_call" | custom-call | flops 12999999488 | bytes 40000000 | tf_op jit(solution)/shard_map/attention/pallas_call | solution.py:392
  93.7 26.4 %back.1 = (bf16[768,768]{1,0:T(8,128)(2,1)}, bf16[768,768]{1,0:T(8,128)(2,1)}, f32[2,384,128]{2,1,0:T(8,128)}) custom-call(s32[2]{0:T(128)} %pad_add_fusion.who_ref, bf16[12,256,768]{2,1,0:T(8,128)(2,1)} %x_ref.3, bf16[12,256,768]{2,1,0:T(8,128)(2,1)} %dy_ref.3, f32[1,768]{1,0:T(1,128)} %get-tuple-element.44.gain_ref, bf16[2,4,768,1408]{3,2,1,0:T(8,128)(2,1)} %bitcast.16, ...), custom_call_target="tpu_custom_call" | custom-call | flops 12999999488 | bytes 40000000 | tf_op jit(solution)/shard_map/back/pallas_call | solution.py:402
  120.1 1.0 collective-permute-start
  121.1 2.2 collective-permute-start.1
  123.4 23.6 %wgrad.1 = (f32[2,4,384,1408]{3,2,1,0:T(8,128)}, bf16[2,4,384,1408]{3,2,1,0:T(8,128)(2,1)}) custom-call(bf16[2,384,768]{2,1,0:T(8,128)(2,1)} %get-tuple-element.42.ht_ref, bf16[2,384,768]{2,1,0:T(8,128)(2,1)} %get-tuple-element.43.dyt_ref, f32[2,384,128]{2,1,0:T(8,128)} %get-tuple-element.55.gcol_ref, bf16[4,768,256]{2,1,0:T(8,128)(2,1)} %get-tuple-element.49.o_ref, ...), custom_call_target="tpu_custom_call" | custom-call | flops 12999999488 | bytes 40000000 | tf_op jit(solution)/shard_map/wgrad/pallas_call | solution.py:415
  146.9 2.9 %collective-permute-done.below_ref = bf16[3,256,768]{2,1,0:T(8,128)(2,1)S(1)} collective-permute-done((bf16[3,256,768]{2,1,0:T(8,128)(2,1)}, bf16[3,256,768]{2,1,0:T(8,128)(2,1)S(1)}, u32[]{:S(2)}, u32[]{:S(2)}) %collective-permute-start) | collective-permute-done | bytes 1179680 | tf_op jit(solution)/shard_map/ppermute | solution.py:772
  149.8 0.0 copy-start
  149.8 0.0 collective-permute-done.1.above_ref
  149.8 0.0 copy-start.1
  149.8 1.0 copy-done
  150.8 0.4 copy-done.1
  151.2 69.5 %sum_grads.1 = (f32[2,3,8,1408]{3,2,1,0:T(8,128)}, f32[4,3,8,128]{3,2,1,0:T(8,128)}, bf16[12,256,768]{2,1,0:T(8,128)(2,1)}, bf16[12,256,768]{2,1,0:T(8,128)(2,1)}) custom-call(f32[2,4,4,4,3,8,1408]{6,5,4,3,2,1,0:T(8,128)} %bitcast.28, bf16[2,4,4,4,3,8,1408]{6,5,4,3,2,1,0:T(8,128)(2,1)} %bitcast.29, bf16[3,256,768]{2,1,0:T(8,128)(2,1)} %bitcast.24, ...), custom_call_target="tpu_custom_call" | custom-call | flops 60000002048 | bytes 30000000 | tf_op jit(solution)/shard_map/sum_grads/pallas_call | solution.py:683
  220.7 9.3 %finish.1 = (bf16[12,256,768]{2,1,0:T(8,128)(2,1)}, bf16[12,256,768]{2,1,0:T(8,128)(2,1)}, f32[1,24]{1,0:T(1,128)}, f32[24,192]{1,0:T(8,128)}, f32[24,64]{1,0:T(...) custom-call(f32[2,3,8,1408]{3,2,1,0:T(8,128)} %get-tuple-element.60., ...), custom_call_target="tpu_custom_call" | custom-call | tf_op jit(solution)/shard_map/finish/pallas_call | solution.py:744
Async XLA Ops:
  120.1 29.7 %collective-permute-start = (bf16[3,256,768]{2,1,0:T(8,128)(2,1)}, bf16[3,256,768]{2,1,0:T(8,128)(2,1)S(1)}, u32[]{:S(2)}, u32[]{:S(2)}) collective-permute-start(bf16[3,256,768]{2,1,0:T(8,128)(2,1)} %bitcast.21), channel_id=1, source_target_pairs={{0,32},{32,64},{64,96},{96,0},{1,33},{33,65},{65,97},{97,1},{2,34}... | collective-permute-start | bytes 3538952 | tf_op jit(solution)/shard_map/ppermute | solution.py:772
  121.1 28.7 %collective-permute-start.1 = (bf16[3,256,768]{2,1,0:T(8,128)(2,1)}, bf16[3,256,768]{2,1,0:T(8,128)(2,1)S(1)}, u32[]{:S(2)}, u32[]{:S(2)}) collective-permute-start(bf16[3,256,768]{2,1,0:T(8,128)(2,1)} %bitcast.22), channel_id=1, source_target_pairs={{0,96},{32,0},{64,32},{96,64},{1,97},{33,1},{65,33},{97,65},{2,98}... | collective-permute-start | bytes 3538952 | tf_op jit(solution)/shard_map/ppermute | solution.py:773
  149.8 1.0 copy-start
  149.8 1.4 copy-start.1

commit v7 on v6

--- a/solution.py
+++ b/solution.py
@@ -86,7 +86,7 @@
         push(view(k, h, fixed, c, cols), view(k, h, fixed, c, cols), ds.at[k, h, n], dr.at[k, h, n], partner)
         across.append((k, h, fixed, cols, n))
 
-    def ring_start(k, h, axis, fixed, ss, rr):
+    def ring_start(k, h, axis, fixed, ss, rr, base):
         here = {**fixed, axis: at[axis]}
         for n in range(N2):
             ref = view(k, h, here, c, parts[n])
@@ -94,18 +94,18 @@
             ref = view(k, h, here, c, parts[N1 - n])
             push(ref, ref, ss.at[k, h, N3 - n], rr.at[k, h, N3 - n], peer(axis, N3))
 
-    def ring_forward(k, h, axis, fixed, ss, rr):
+    def ring_forward(k, h, axis, fixed, ss, rr, base):
         for p, d, n in ((N0, N3, N0), (N1, N1, N3)):
             ref = view(k, h, {**fixed, axis: up(at[axis], d)}, c, parts[p])
             landed(ref, ss.at[k, h, n], rr.at[k, h, n])
             push(ref, ref, ss.at[k, h, RING + p], rr.at[k, h, RING + p], peer(axis, RING - d))
+            share(k, h, {**fixed, axis: up(at[axis], d)}, parts[p], base + p)
 
     def ring_share(k, h, axis, fixed, ss, rr, base):
-        for m, (p, d, n) in enumerate(((N0, N3, N0), (N1, N1, N3), (N1, N3, N1), (N0, N1, N2), (N0, N2, RING), (N1, N2, 5))):
+        for m, (p, d, n) in enumerate(((N1, N3, N1), (N0, N1, N2), (N0, N2, RING), (N1, N2, 5))):
             there = {**fixed, axis: up(at[axis], d)}
-            if n not in (N0, N3):
-                landed(view(k, h, there, c, parts[p]), ss.at[k, h, n], rr.at[k, h, n])
-            share(k, h, there, parts[p], base + m)
+            landed(view(k, h, there, c, parts[p]), ss.at[k, h, n], rr.at[k, h, n])
+            share(k, h, there, parts[p], base + N2 + m)
 
     streams = [(k, h) for h in range(N2) for k in range(N3)]
     for k, h in streams:
@@ -118,19 +118,19 @@
         order = orders[k]
         for d in (N1, N3, N2):
             landed(view(k, h, {**at, order[N0]: up(at[order[N0]], RING - d)}, c), s1.at[k, h, d - N1], r1.at[k, h, d - N1])
-        second[k, h] = (k, h, order[N1], {order[N2]: at[order[N2]]}, s2, r2)
-        third[k, h] = (k, h, order[N2], {}, s3, r3)
+        second[k, h] = (k, h, order[N1], {order[N2]: at[order[N2]]}, s2, r2, N1)
+        third[k, h] = (k, h, order[N2], {}, s3, r3, 7)
         ring_start(*second[k, h])
         share(k, h, {order[N1]: at[order[N1]], order[N2]: at[order[N2]]}, None, N0)
     for stream in streams:
         ring_forward(*second[stream])
     for stream in streams:
-        ring_share(*second[stream], N1)
+        ring_share(*second[stream])
         ring_start(*third[stream])
     for stream in streams:
         ring_forward(*third[stream])
     for stream in streams:
-        ring_share(*third[stream], 7)
+        ring_share(*third[stream])
     for k, h, fixed, cols, n in across:
         landed(view(k, h, fixed, N1 - c, cols), ds.at[k, h, n], dr.at[k, h, n])
     for copy in sent:
@@ -516,7 +516,7 @@
         def step(n, carry):
             body(n)
             return carry
-        lax.fori_loop(N0, count, step, N0)
+        lax.fori_loop(N0, count, step, N0, unroll=N3)
 
     def arrived(col, n):
         load[col][n].wait()

time: 231 us -> 228 us (0.987)
  Pallas kernels: 221 us -> 218 us
    pallas_call x1, Pallas kernels: 52.8 us -> 50.2 us  [gather_weights(): pl.pallas_call(gather_kernel, name='gather_weights', out_shape=jax.ShapeD...]
where the time goes in v7:
time: 228 us; the launch traced here: 227 us
  Pallas kernels  218 us (96%)
  starting transfers between devices  3.24 us (1%)
  waiting for transfers between devices  2.89 us (1%)
    pallas_call x1, Pallas kernels, sum_grads(): pl.pallas_call(sum_kernel, name='sum_grads', out_shape=(jax.ShapeDtypeStr...  68.7 us
    pallas_call x1, Pallas kernels, gather_weights(): pl.pallas_call(gather_kernel, name='gather_weights', out_shape=jax.ShapeD...  50.2 us
    pallas_call x1, Pallas kernels, layer_step(): pl.pallas_call(back_kernel, name='back', grid_spec=pltpu.PrefetchScalarGr...  26.4 us
    pallas_call x1, Pallas kernels, layer_step(): pl.pallas_call(proj_kernel, name='proj', grid_spec=pltpu.PrefetchScalarGr...  25.1 us
    pallas_call x1, Pallas kernels, layer_step(): pl.pallas_call(wgrad_kernel, name='wgrad', grid=(n_tp,), in_specs=[classe...  23.6 us
    pallas_call x1, Pallas kernels, layer_step(): pl.pallas_call(att_kernel, name='attention', grid=(n_seq,), in_specs=[pai...  14.5 us
    pallas_call x1, Pallas kernels, finish(): pl.pallas_call(finish_kernel, name='finish', out_shape=[act_t, act_t] + [...  9.33 us
  transfers between devices with their start and end apart: 2, of which 1 were waited for; matrix products, arithmetic and copies ran while one was open for 0% of the time, Pallas kernels for 10%

profile of v7, /device:TPU:0, one launch (start us, length us, event | category | flops | bytes accessed | tf_op | source)
XLA Modules:
  0.0 226.8 jit_solution(2393735869875526168)
XLA Ops:
  0.6 0.6 pad_add_fusion.who_ref
  1.2 50.2 %gather_weights.1 = bf16[2,4,4,4,2,3,8,1408]{7,6,5,4,3,2,1,0:T(8,128)(2,1)} custom-call(bf16[24,768]{1,0:T(8,128)(2,1)} %wg_ref.1, bf16[24,192]{1,0:T(8,128)(2,1)} %wq_ref.1, bf16[24,192]{1,0:T(8,128)(2,1)} %bitcast.19, bf16[24,768]{1,0:T(8,128)(2,1)} %wu_ref.1, bf16[24,768]{1,0:T(8,128)(2,1)} %bitcast.18, bf16[24,64]{1,0:T(8,128)(2,1)} %wk_ref.1, ...), custom_call_target="tpu_custom_call" | custom-call | tf_op jit(solution)/shard_map/gather_weights/pallas_call | solution.py:144
  51.5 25.1 %proj.1 = (f32[1,768]{1,0:T(1,128)}, bf16[768,128]{1,0:T(8,128)(2,1)}, bf16[2,384,768]{2,1,0:T(8,128)(2,1)}, bf16[2,384,768]{2,1,0:T(8,128)(2,1)}, bf16[4,768,25...) custom-call(s32[2]{0:T(128)} %pad_add_fusion.who_ref, ...), custom_call_target="tpu_custom_call" | custom-call | flops 12999999488 | bytes 40000000 | tf_op jit(solution)/shard_map/proj/pallas_call | solution.py:378
  76.6 14.5 %attention.1 = (bf16[4,768,256]{2,1,0:T(8,128)(2,1)}, bf16[4,768,256]{2,1,0:T(8,128)(2,1)}, bf16[768,128]{1,0:T(8,128)(2,1)}) custom-call(bf16[4,768,256]{2,1,0:T(8,128)(2,1)} %get-tuple-element.46.q_ref, bf16[768,128]{1,0:T(8,128)(2,1)} %get-tuple-element.47.kv_ref, bf16[4,768,256]{2,1,0:T(8,128)(2,1)} %get-tuple-element.48.do_ref, ...), custom_call_target="tpu_custom_call" | custom-call | flops 12999999488 | bytes 40000000 | tf_op jit(solution)/shard_map/attention/pallas_call | solution.py:392
  91.1 26.4 %back.1 = (bf16[768,768]{1,0:T(8,128)(2,1)}, bf16[768,768]{1,0:T(8,128)(2,1)}, f32[2,384,128]{2,1,0:T(8,128)}) custom-call(s32[2]{0:T(128)} %pad_add_fusion.who_ref, bf16[12,256,768]{2,1,0:T(8,128)(2,1)} %x_ref.3, bf16[12,256,768]{2,1,0:T(8,128)(2,1)} %dy_ref.3, f32[1,768]{1,0:T(1,128)} %get-tuple-element.44.gain_ref, bf16[2,4,768,1408]{3,2,1,0:T(8,128)(2,1)} %bitcast.16, ...), custom_call_target="tpu_custom_call" | custom-call | flops 12999999488 | bytes 40000000 | tf_op jit(solution)/shard_map/back/pallas_call | solution.py:402
  117.5 1.0 collective-permute-start
  118.5 2.2 collective-permute-start.1
  120.8 23.6 %wgrad.1 = (f32[2,4,384,1408]{3,2,1,0:T(8,128)}, bf16[2,4,384,1408]{3,2,1,0:T(8,128)(2,1)}) custom-call(bf16[2,384,768]{2,1,0:T(8,128)(2,1)} %get-tuple-element.42.ht_ref, bf16[2,384,768]{2,1,0:T(8,128)(2,1)} %get-tuple-element.43.dyt_ref, f32[2,384,128]{2,1,0:T(8,128)} %get-tuple-element.55.gcol_ref, bf16[4,768,256]{2,1,0:T(8,128)(2,1)} %get-tuple-element.49.o_ref, ...), custom_call_target="tpu_custom_call" | custom-call | flops 12999999488 | bytes 40000000 | tf_op jit(solution)/shard_map/wgrad/pallas_call | solution.py:415
  144.3 2.9 %collective-permute-done.below_ref = bf16[3,256,768]{2,1,0:T(8,128)(2,1)S(1)} collective-permute-done((bf16[3,256,768]{2,1,0:T(8,128)(2,1)}, bf16[3,256,768]{2,1,0:T(8,128)(2,1)S(1)}, u32[]{:S(2)}, u32[]{:S(2)}) %collective-permute-start) | collective-permute-done | bytes 1179680 | tf_op jit(solution)/shard_map/ppermute | solution.py:772
  147.2 0.0 copy-start
  147.2 0.0 collective-permute-done.1.above_ref
  147.2 0.0 copy-start.1
  147.2 1.0 copy-done
  148.2 0.4 copy-done.1
  148.6 68.7 %sum_grads.1 = (f32[2,3,8,1408]{3,2,1,0:T(8,128)}, f32[4,3,8,128]{3,2,1,0:T(8,128)}, bf16[12,256,768]{2,1,0:T(8,128)(2,1)}, bf16[12,256,768]{2,1,0:T(8,128)(2,1)}) custom-call(f32[2,4,4,4,3,8,1408]{6,5,4,3,2,1,0:T(8,128)} %bitcast.28, bf16[2,4,4,4,3,8,1408]{6,5,4,3,2,1,0:T(8,128)(2,1)} %bitcast.29, bf16[3,256,768]{2,1,0:T(8,128)(2,1)} %bitcast.24, ...), custom_call_target="tpu_custom_call" | custom-call | flops 60000002048 | bytes 30000000 | tf_op jit(solution)/shard_map/sum_grads/pallas_call | solution.py:683
  217.3 9.3 %finish.1 = (bf16[12,256,768]{2,1,0:T(8,128)(2,1)}, bf16[12,256,768]{2,1,0:T(8,128)(2,1)}, f32[1,24]{1,0:T(1,128)}, f32[24,192]{1,0:T(8,128)}, f32[24,64]{1,0:T(...) custom-call(f32[2,3,8,1408]{3,2,1,0:T(8,128)} %get-tuple-element.60., ...), custom_call_target="tpu_custom_call" | custom-call | tf_op jit(solution)/shard_map/finish/pallas_call | solution.py:744
Async XLA Ops:
  117.5 29.7 %collective-permute-start = (bf16[3,256,768]{2,1,0:T(8,128)(2,1)}, bf16[3,256,768]{2,1,0:T(8,128)(2,1)S(1)}, u32[]{:S(2)}, u32[]{:S(2)}) collective-permute-start(bf16[3,256,768]{2,1,0:T(8,128)(2,1)} %bitcast.21), channel_id=1, source_target_pairs={{0,32},{32,64},{64,96},{96,0},{1,33},{33,65},{65,97},{97,1},{2,34}... | collective-permute-start | bytes 3538952 | tf_op jit(solution)/shard_map/ppermute | solution.py:772
  118.5 28.7 %collective-permute-start.1 = (bf16[3,256,768]{2,1,0:T(8,128)(2,1)}, bf16[3,256,768]{2,1,0:T(8,128)(2,1)S(1)}, u32[]{:S(2)}, u32[]{:S(2)}) collective-permute-start(bf16[3,256,768]{2,1,0:T(8,128)(2,1)} %bitcast.22), channel_id=1, source_target_pairs={{0,96},{32,0},{64,32},{96,64},{1,97},{33,1},{65,33},{97,65},{2,98}... | collective-permute-start | bytes 3538952 | tf_op jit(solution)/shard_map/ppermute | solution.py:773
  147.2 1.0 copy-start
  147.2 1.4 copy-start.1

commit v8 on v7

--- a/solution.py
+++ b/solution.py
@@ -533,14 +533,14 @@
     for col in range(N2):
         arrived(col, N0)
 
-        def first(q, col=col):
-            tt = lax.div(q, 12)
-            a2 = lax.rem(lax.div(q, N3), RING)
-            r = lax.rem(q, N3)
-            sa[col, N0, a2, tt, r] = (acc[col, N0, tt, a2, r] + rp[col, N0, tt, a2, r].astype(f32)).astype(bf16)
-        each(48, first)
-        send(sa.at[col, N0, pl.ds(N0, N2)], ra1.at[col, N0], ss.at[col, N0], rs.at[col, N0], dev_a[col][N1])
-        send(sa.at[col, N0, pl.ds(N2, N2)], ra1.at[col, N1], ss.at[col, N1], rs.at[col, N1], dev_a[col][N3])
+        for h, peer in ((N0, N1), (N1, N3)):
+            def first(q, col=col, h=h):
+                a2 = N2 * h + lax.div(q, 12)
+                tt = lax.rem(lax.div(q, N3), RING)
+                r = lax.rem(q, N3)
+                sa[col, N0, a2, tt, r] = (acc[col, N0, tt, a2, r] + rp[col, N0, tt, a2, r].astype(f32)).astype(bf16)
+            each(24, first)
+            send(sa.at[col, N0, pl.ds(N2 * h, N2)], ra1.at[col, h], ss.at[col, h], rs.at[col, h], dev_a[col][peer])
     for col in range(N2):
         for n, base, peer in ((N1, N2, N1), (N2, N0, N3)):
             arrived(col, n)

time: 228 us -> 227 us (level)
  no operation moved by 1% of the time
where the time goes in v8:
time: 227 us; the launch traced here: 226 us
  Pallas kernels  217 us (96%)
  starting transfers between devices  3.24 us (1%)
  waiting for transfers between devices  2.89 us (1%)
    pallas_call x1, Pallas kernels, sum_grads(): pl.pallas_call(sum_kernel, name='sum_grads', out_shape=(jax.ShapeDtypeStr...  68.3 us
    pallas_call x1, Pallas kernels, gather_weights(): pl.pallas_call(gather_kernel, name='gather_weights', out_shape=jax.ShapeD...  50.2 us
    pallas_call x1, Pallas kernels, layer_step(): pl.pallas_call(back_kernel, name='back', grid_spec=pltpu.PrefetchScalarGr...  26.4 us
    pallas_call x1, Pallas kernels, layer_step(): pl.pallas_call(proj_kernel, name='proj', grid_spec=pltpu.PrefetchScalarGr...  25.1 us
    pallas_call x1, Pallas kernels, layer_step(): pl.pallas_call(wgrad_kernel, name='wgrad', grid=(n_tp,), in_specs=[classe...  23.6 us
    pallas_call x1, Pallas kernels, layer_step(): pl.pallas_call(att_kernel, name='attention', grid=(n_seq,), in_specs=[pai...  14.5 us
    pallas_call x1, Pallas kernels, finish(): pl.pallas_call(finish_kernel, name='finish', out_shape=[act_t, act_t] + [...  9.33 us
  transfers between devices with their start and end apart: 2, of which 1 were waited for; matrix products, arithmetic and copies ran while one was open for 0% of the time, Pallas kernels for 10%

profile of v8, /device:TPU:0, one launch (start us, length us, event | category | flops | bytes accessed | tf_op | source)
XLA Modules:
  0.0 226.5 jit_solution(6935372496142541516)
XLA Ops:
  0.6 0.6 pad_add_fusion.who_ref
  1.2 50.2 %gather_weights.1 = bf16[2,4,4,4,2,3,8,1408]{7,6,5,4,3,2,1,0:T(8,128)(2,1)} custom-call(bf16[24,768]{1,0:T(8,128)(2,1)} %wg_ref.1, bf16[24,192]{1,0:T(8,128)(2,1)} %wq_ref.1, bf16[24,192]{1,0:T(8,128)(2,1)} %bitcast.19, bf16[24,768]{1,0:T(8,128)(2,1)} %wu_ref.1, bf16[24,768]{1,0:T(8,128)(2,1)} %bitcast.18, bf16[24,64]{1,0:T(8,128)(2,1)} %wk_ref.1, ...), custom_call_target="tpu_custom_call" | custom-call | tf_op jit(solution)/shard_map/gather_weights/pallas_call | solution.py:144
  51.5 25.1 %proj.1 = (f32[1,768]{1,0:T(1,128)}, bf16[768,128]{1,0:T(8,128)(2,1)}, bf16[2,384,768]{2,1,0:T(8,128)(2,1)}, bf16[2,384,768]{2,1,0:T(8,128)(2,1)}, bf16[4,768,25...) custom-call(s32[2]{0:T(128)} %pad_add_fusion.who_ref, ...), custom_call_target="tpu_custom_call" | custom-call | flops 12999999488 | bytes 40000000 | tf_op jit(solution)/shard_map/proj/pallas_call | solution.py:378
  76.6 14.5 %attention.1 = (bf16[4,768,256]{2,1,0:T(8,128)(2,1)}, bf16[4,768,256]{2,1,0:T(8,128)(2,1)}, bf16[768,128]{1,0:T(8,128)(2,1)}) custom-call(bf16[4,768,256]{2,1,0:T(8,128)(2,1)} %get-tuple-element.46.q_ref, bf16[768,128]{1,0:T(8,128)(2,1)} %get-tuple-element.47.kv_ref, bf16[4,768,256]{2,1,0:T(8,128)(2,1)} %get-tuple-element.48.do_ref, ...), custom_call_target="tpu_custom_call" | custom-call | flops 12999999488 | bytes 40000000 | tf_op jit(solution)/shard_map/attention/pallas_call | solution.py:392
  91.1 26.4 %back.1 = (bf16[768,768]{1,0:T(8,128)(2,1)}, bf16[768,768]{1,0:T(8,128)(2,1)}, f32[2,384,128]{2,1,0:T(8,128)}) custom-call(s32[2]{0:T(128)} %pad_add_fusion.who_ref, bf16[12,256,768]{2,1,0:T(8,128)(2,1)} %x_ref.3, bf16[12,256,768]{2,1,0:T(8,128)(2,1)} %dy_ref.3, f32[1,768]{1,0:T(1,128)} %get-tuple-element.44.gain_ref, bf16[2,4,768,1408]{3,2,1,0:T(8,128)(2,1)} %bitcast.16, ...), custom_call_target="tpu_custom_call" | custom-call | flops 12999999488 | bytes 40000000 | tf_op jit(solution)/shard_map/back/pallas_call | solution.py:402
  117.5 1.0 collective-permute-start
  118.5 2.2 collective-permute-start.1
  120.8 23.6 %wgrad.1 = (f32[2,4,384,1408]{3,2,1,0:T(8,128)}, bf16[2,4,384,1408]{3,2,1,0:T(8,128)(2,1)}) custom-call(bf16[2,384,768]{2,1,0:T(8,128)(2,1)} %get-tuple-element.42.ht_ref, bf16[2,384,768]{2,1,0:T(8,128)(2,1)} %get-tuple-element.43.dyt_ref, f32[2,384,128]{2,1,0:T(8,128)} %get-tuple-element.55.gcol_ref, bf16[4,768,256]{2,1,0:T(8,128)(2,1)} %get-tuple-element.49.o_ref, ...), custom_call_target="tpu_custom_call" | custom-call | flops 12999999488 | bytes 40000000 | tf_op jit(solution)/shard_map/wgrad/pallas_call | solution.py:415
  144.3 2.9 %collective-permute-done.below_ref = bf16[3,256,768]{2,1,0:T(8,128)(2,1)S(1)} collective-permute-done((bf16[3,256,768]{2,1,0:T(8,128)(2,1)}, bf16[3,256,768]{2,1,0:T(8,128)(2,1)S(1)}, u32[]{:S(2)}, u32[]{:S(2)}) %collective-permute-start) | collective-permute-done | bytes 1179680 | tf_op jit(solution)/shard_map/ppermute | solution.py:772
  147.2 0.0 copy-start
  147.2 0.0 collective-permute-done.1.above_ref
  147.2 0.0 copy-start.1
  147.2 1.0 copy-done
  148.2 0.4 copy-done.1
  148.6 68.3 %sum_grads.1 = (f32[2,3,8,1408]{3,2,1,0:T(8,128)}, f32[4,3,8,128]{3,2,1,0:T(8,128)}, bf16[12,256,768]{2,1,0:T(8,128)(2,1)}, bf16[12,256,768]{2,1,0:T(8,128)(2,1)}) custom-call(f32[2,4,4,4,3,8,1408]{6,5,4,3,2,1,0:T(8,128)} %bitcast.28, bf16[2,4,4,4,3,8,1408]{6,5,4,3,2,1,0:T(8,128)(2,1)} %bitcast.29, bf16[3,256,768]{2,1,0:T(8,128)(2,1)} %bitcast.24, ...), custom_call_target="tpu_custom_call" | custom-call | flops 60000002048 | bytes 30000000 | tf_op jit(solution)/shard_map/sum_grads/pallas_call | solution.py:683
  216.9 9.3 %finish.1 = (bf16[12,256,768]{2,1,0:T(8,128)(2,1)}, bf16[12,256,768]{2,1,0:T(8,128)(2,1)}, f32[1,24]{1,0:T(1,128)}, f32[24,192]{1,0:T(8,128)}, f32[24,64]{1,0:T(...) custom-call(f32[2,3,8,1408]{3,2,1,0:T(8,128)} %get-tuple-element.60., ...), custom_call_target="tpu_custom_call" | custom-call | tf_op jit(solution)/shard_map/finish/pallas_call | solution.py:744
Async XLA Ops:
  117.5 29.7 %collective-permute-start = (bf16[3,256,768]{2,1,0:T(8,128)(2,1)}, bf16[3,256,768]{2,1,0:T(8,128)(2,1)S(1)}, u32[]{:S(2)}, u32[]{:S(2)}) collective-permute-start(bf16[3,256,768]{2,1,0:T(8,128)(2,1)} %bitcast.21), channel_id=1, source_target_pairs={{0,32},{32,64},{64,96},{96,0},{1,33},{33,65},{65,97},{97,1},{2,34}... | collective-permute-start | bytes 3538952 | tf_op jit(solution)/shard_map/ppermute | solution.py:772
  118.5 28.7 %collective-permute-start.1 = (bf16[3,256,768]{2,1,0:T(8,128)(2,1)}, bf16[3,256,768]{2,1,0:T(8,128)(2,1)S(1)}, u32[]{:S(2)}, u32[]{:S(2)}) collective-permute-start(bf16[3,256,768]{2,1,0:T(8,128)(2,1)} %bitcast.22), channel_id=1, source_target_pairs={{0,96},{32,0},{64,32},{96,64},{1,97},{33,1},{65,33},{97,65},{2,98}... | collective-permute-start | bytes 3538952 | tf_op jit(solution)/shard_map/ppermute | solution.py:773
  147.2 1.0 copy-start
  147.2 1.4 copy-start.1
